TPU v7x, 64 devices: a 2x2x8 block of a 4x4x8 slice. The times are simulated.
64 devices in a mesh: data: 4 (over x, y), tensor: 16 (over z, core).
Axes of the slice: x: 2, y: 2, z: 8, core: 2. Of those that a mesh axis runs over, the one named last changes fastest.
The devices are a block of a 4x4x8 slice.
Arguments:
- token_ids: int32 [32768], P(('data', 'tensor')), parts along dimension 0
- emb_table: bfloat16 [49152, 960], P('tensor')
- norm_gain: bfloat16 [960], replicated
- w_up: bfloat16 [960, 2560], P(None, 'tensor')
- w_down: bfloat16 [2560, 960], P('tensor')
- grad_out: bfloat16 [32768, 960], P(('data', 'tensor')), parts along dimension 0
Outputs:
- output 1: bfloat16 [32768, 960], P(('data', 'tensor')), parts along dimension 0
- output 2: float32 [196608, 960], P(('data', 'tensor')), parts along dimension 0
- output 3: float32 [3840, 2560], P('data', 'tensor'), parts along dimension 0
- output 4: float32 [10240, 960], P(('data', 'tensor')), parts along dimension 0
There are 4 independent parts. A program takes and returns all parts, laid end to end along the dimension named above; an argument that names none is the same for every part.
All inputs are finite; a program needn't handle non-finite values.
Results may differ from a plain program's by a relative error of at most 0.00554385.
Values are sent between devices in bfloat16 or wider.
A program may use at most 768 MiB of HBM per device.

v0:
```python
import jax
import jax.numpy as jnp
from jax import lax
from jax.sharding import PartitionSpec as P

EPS = 1e-6


def rms_norm(x_rows, gain_f):
    inv_rms = lax.rsqrt(jnp.mean(x_rows * x_rows, axis=-1, keepdims=True) + EPS)
    return x_rows * inv_rms * gain_f


def gelu_tanh(values):
    return jax.nn.gelu(values, approximate=True)


def contract_last(left_op, right_op):
    return lax.dot_general(left_op, right_op, (((1,), (1,)), ((), ())), preferred_element_type=jnp.float32)


def contract_first(left_op, right_op):
    return lax.dot_general(left_op, right_op, (((0,), (0,)), ((), ())), preferred_element_type=jnp.float32)


def solution(mesh):
    tok_spec = P(('data', 'tensor'))
    row_spec = P(('data', 'tensor'), None)

    def local_step(token_ids, emb_shard, norm_gain, w_up, w_down, grad_out):
        vocab_local = emb_shard.shape[0]
        offset = lax.axis_index('tensor') * vocab_local
        ids_all = lax.all_gather(token_ids, 'tensor', tiled=True)
        rel_ids = ids_all - offset
        is_owned = (rel_ids >= 0) & (rel_ids < vocab_local)
        looked_up = jnp.take(emb_shard, jnp.clip(rel_ids, 0, vocab_local - 1), axis=0)
        emb_part = jnp.where(is_owned[:, None], looked_up, jnp.zeros((), looked_up.dtype))
        x_local = lax.psum_scatter(emb_part, 'tensor', scatter_dimension=0, tiled=True)
        x_f = x_local.astype(jnp.float32)
        gain_f = norm_gain.astype(jnp.float32)
        normed_f, norm_back = jax.vjp(lambda x_in: rms_norm(x_in, gain_f), x_f)
        normed = normed_f.astype(jnp.bfloat16)
        normed_all = lax.all_gather(normed, 'tensor', tiled=True)
        pre_act = jnp.dot(normed_all, w_up, preferred_element_type=jnp.float32).astype(jnp.bfloat16)
        act_f, gelu_back = jax.vjp(gelu_tanh, pre_act.astype(jnp.float32))
        hidden = act_f.astype(jnp.bfloat16)
        y_part = jnp.dot(hidden, w_down, preferred_element_type=jnp.float32)
        y_local = lax.psum_scatter(y_part, 'tensor', scatter_dimension=0, tiled=True)
        out_local = (x_f + y_local).astype(jnp.bfloat16)
        grad_all = lax.all_gather(grad_out, 'tensor', tiled=True)
        d_hidden = contract_last(grad_all, w_down)
        d_pre = gelu_back(d_hidden)[0].astype(jnp.bfloat16)
        d_w_down = contract_first(hidden, grad_all)
        d_w_up = contract_first(normed_all, d_pre)
        d_norm_part = contract_last(d_pre, w_up)
        d_norm = lax.psum_scatter(d_norm_part, 'tensor', scatter_dimension=0, tiled=True)
        dx_local = (grad_out.astype(jnp.float32) + norm_back(d_norm)[0]).astype(jnp.bfloat16)
        dx_all = lax.all_gather(dx_local, 'tensor', tiled=True)
        seg_ids = jnp.where(is_owned, rel_ids, vocab_local)
        d_emb = jax.ops.segment_sum(dx_all.astype(jnp.float32), seg_ids, num_segments=vocab_local + 1)[:vocab_local]
        return out_local, d_emb, d_w_up, d_w_down

    return jax.shard_map(
        local_step,
        mesh=mesh,
        in_specs=(tok_spec, P('tensor', None), P(None), P(None, 'tensor'), P('tensor', None), row_spec),
        out_specs=(row_spec, row_spec, P('data', 'tensor'), row_spec),
        check_vma=False,
    )
```

profile of v0, /device:TPU:21, one launch (start us, length us, event | category | flops | bytes accessed | tf_op | source)
XLA Modules:
  0.0 970.9 jit_solution(13304003082248637935)
XLA Ops:
  7.2 0.0 copy-start
  7.2 0.1 reduce-scatter.4.cloned.1.call-start
  7.3 22.8 %all-gather = s32[16,1,512]{2,1,0:T(1,128)S(1)} all-gather(s32[1,1,512]{2,1,0:T(1,128)} %bitcast.17), channel_id=1, replica_groups=mesh['data'=4,'tensor'=16] {'tensor'}, dimensions={0}, use_global_device_ids=true | all-gather | bytes 34816 | tf_op jit(solution)/shard_map/all_gather | solution.py:33
  30.1 0.6 broadcast_select_fusion
  30.7 8.5 copy.16
  39.2 44.2 %gather_fusion = bf16[8192,960]{1,0:T(8,128)(2,1)} fusion(bf16[3072,960]{1,0:T(8,128)(2,1)} %copy.16, s32[8192]{0:T(1024)S(1)} %get-tuple-element.15), kind=kCustom, calls=%fused_computation | custom fusion | bytes 31490048 | tf_op jit(solution)/shard_map/jit(_take)/gather | solution.py:36
  83.4 21.3 %copy.17 = bf16[8192,960]{0,1:T(8,128)(2,1)} copy(bf16[8192,960]{1,0:T(8,128)(2,1)} %gather_fusion) | data formatting | bytes 31457280 | tf_op jit(solution)/shard_map/jit(_take)/gather | solution.py:36
  104.8 13.4 %select_select_fusion = bf16[8192,960]{0,1:T(8,128)(2,1)} fusion(bf16[8192,960]{0,1:T(8,128)(2,1)} %copy.17, pred[8192]{0:T(1024)(128)(4,1)S(1)} %get-tuple-element.17, pred[8192]{0:T(1024)(128)(4,1)S(1)} %get-tuple-element.16), kind=kLoop, calls=%fused_computation.2 | loop fusion | flops 15728640 | bytes 31473664 | tf_op jit(solution)/shard_map/jit(_where)/select_n | solution.py:37
  118.2 0.1 reduce-scatter.4.cloned.1.call-update
  118.3 0.1 all-gather.7.cloned.1.call-start
  118.4 0.7 all-gather.7.cloned.1.call-update
  119.1 0.1 all-gather.5.cloned.1.call-start
  119.2 0.0 copy-done.8
  119.2 88.0 %reduce-scatter.4.cloned.1.call-done = bf16[512,960]{0,1:T(8,128)(2,1)} async-done(((bf16[8192,960]{0,1:T(8,128)(2,1)}), bf16[512,960]{0,1:T(8,128)(2,1)}) %reduce-scatter.4.cloned.1.call-update) | async-done | bytes 983056 | tf_op jit(solution)/shard_map/reduce_scatter | solution.py:38
  207.2 1.5 fusion.14
  208.7 2.4 fusion.16
  211.1 0.1 all-gather.5.cloned.1.call-update
  211.2 0.1 reduce-scatter.8.cloned.1.call-start
  211.2 84.6 %all-gather.7.cloned.1.call-done = bf16[8192,960]{0,1:T(8,128)(2,1)} async-done(((bf16[512,960]{0,1:T(8,128)(2,1)}), bf16[8192,960]{0,1:T(8,128)(2,1)}) %all-gather.7.cloned.1.call-update) | async-done | bytes 15728656 | tf_op jit(solution)/shard_map/all_gather | solution.py:50
  295.8 0.0 copy-done.7
  295.8 10.7 %fusion.27 = f32[8192,160]{0,1:T(8,128)} fusion(bf16[160,960]{1,0:T(8,128)(2,1)S(1)} %copy-done.7, bf16[8192,960]{0,1:T(8,128)(2,1)} %all-gather.7.cloned.1.call-done), kind=kOutput, calls=%fused_computation.47 | convolution fusion | flops 2516582400 | bytes 21278720 | tf_op jit(solution)/shard_map/dot_general | solution.py:19
  306.6 77.1 %all-gather.5.cloned.1.call-done = bf16[8192,960]{0,1:T(8,128)(2,1)} async-done(((bf16[512,960]{0,1:T(8,128)(2,1)}), bf16[8192,960]{0,1:T(8,128)(2,1)}) %all-gather.5.cloned.1.call-update) | async-done | bytes 15728656 | tf_op jit(solution)/shard_map/all_gather | solution.py:43
  383.7 0.0 copy-done
  383.7 10.4 %fusion.5 = (bf16[8192,160]{0,1:T(8,128)(2,1)S(1)}, bf16[8192,160]{0,1:T(8,128)(2,1)S(1)}) fusion(f32[8192,160]{0,1:T(8,128)} %fusion.27, bf16[960,160]{0,1:T(8,128)(2,1)S(1)} %copy-done, bf16[8192,960]{0,1:T(8,128)(2,1)} %all-gather.5.cloned.1.call-done), kind=kOutput, calls=%fused_computation.14 | convolution fusion | flops 2545418240 | bytes 26521600 | tf_op jit(solution)/shard_map/dot_general | solution.py:44
  394.1 0.0 copy-start.5
  394.1 0.0 copy-start.3
  394.1 1.5 copy-done.5
  395.6 12.5 %fusion.25 = f32[8192,960]{0,1:T(8,128)} fusion(bf16[8192,160]{0,1:T(8,128)(2,1)S(1)} %get-tuple-element.18, bf16[960,160]{0,1:T(8,128)(2,1)S(1)} %copy-done), kind=kOutput, calls=%fused_computation.45 | convolution fusion | flops 2516582400 | bytes 34385920 | tf_op jit(solution)/shard_map/dot_general | solution.py:19
  408.1 0.1 reduce-scatter.8.cloned.1.call-update
  408.1 0.2 reduce-scatter.6.cloned.1.call-start
  408.4 0.0 copy-done.3
  408.4 12.5 %fusion.23 = f32[8192,960]{0,1:T(8,128)} fusion(bf16[160,960]{1,0:T(8,128)(2,1)S(1)} %copy-done.7, bf16[8192,160]{0,1:T(8,128)(2,1)S(1)} %get-tuple-element.19), kind=kOutput, calls=%fused_computation.44 | convolution fusion | flops 2529689600 | bytes 34385920 | tf_op jit(solution)/shard_map/dot_general | solution.py:47
  420.9 0.1 reduce-scatter.6.cloned.1.call-update
  421.0 0.1 all-gather.9.cloned.1.call-start
  421.1 156.3 %reduce-scatter.8.cloned.1.call-done = f32[512,960]{0,1:T(8,128)} async-done(((f32[8192,960]{0,1:T(8,128)}), f32[512,960]{0,1:T(8,128)}) %reduce-scatter.8.cloned.1.call-update) | async-done | bytes 1966096 | tf_op jit(solution)/shard_map/reduce_scatter | solution.py:56
  577.4 1.9 fusion.18
  579.3 170.4 %reduce-scatter.6.cloned.1.call-done = f32[512,960]{0,1:T(8,128)} async-done(((f32[8192,960]{0,1:T(8,128)}), f32[512,960]{0,1:T(8,128)}) %reduce-scatter.6.cloned.1.call-update) | async-done | bytes 1966096 | tf_op jit(solution)/shard_map/reduce_scatter | solution.py:48
  749.7 0.0 copy-done.6
  749.7 4.1 fusion.13
  753.8 0.1 all-gather.9.cloned.1.call-update
  753.9 0.0 copy-start.4
  753.9 12.2 %fusion.26 = f32[960,160]{0,1:T(8,128)} fusion(bf16[8192,960]{0,1:T(8,128)(2,1)} %all-gather.5.cloned.1.call-done, bf16[8192,160]{0,1:T(8,128)(2,1)} %copy-done.5), kind=kOutput, calls=%fused_computation.46 | convolution fusion | flops 2516582400 | bytes 18964480 | tf_op jit(solution)/shard_map/dot_general | solution.py:23
  766.1 11.3 %fusion.21 = f32[160,960]{1,0:T(8,128)} fusion(bf16[8192,960]{0,1:T(8,128)(2,1)} %all-gather.7.cloned.1.call-done, bf16[8192,160]{0,1:T(8,128)(2,1)S(1)} %copy-done.4), kind=kOutput, calls=%fused_computation.43 | convolution fusion | flops 2529689600 | bytes 18964480 | tf_op jit(solution)/shard_map/dot_general | solution.py:23
  777.4 63.3 %all-gather.9.cloned.1.call-done = bf16[8192,960]{0,1:T(8,128)(2,1)} async-done(((bf16[512,960]{0,1:T(8,128)(2,1)}), bf16[8192,960]{0,1:T(8,128)(2,1)}) %all-gather.9.cloned.1.call-update) | async-done | bytes 15728656 | tf_op jit(solution)/shard_map/all_gather | solution.py:58
  840.7 23.0 %copy.18 = f32[8192,960]{1,0:T(8,128)} copy(bf16[8192,960]{0,1:T(8,128)(2,1)} %all-gather.9.cloned.1.call-done) | data formatting | bytes 47185920 | tf_op jit(solution)/shard_map/convert_element_type | solution.py:60
  863.7 76.2 %scatter_custom_fusion = f32[3073,960]{1,0:T(8,128)} fusion(s32[8192]{0:T(1024)} %get-tuple-element.14, f32[8192,960]{1,0:T(8,128)} %copy.18, f32[]{:T(128)} %constant.22.clone.1), kind=kCustom, calls=%fused_computation.10 | custom fusion | flops 7864320 | bytes 11800832 | tf_op jit(solution)/shard_map/scatter-add | solution.py:60
  939.9 11.8 %slice.6 = f32[3072,960]{1,0:T(8,128)} slice(f32[3073,960]{1,0:T(8,128)} %scatter_custom_fusion), slice={[0:3072], [0:960]} | slice | bytes 23592960 | tf_op jit(solution)/shard_map/slice | solution.py:60
  951.7 12.3 %copy.19 = f32[3072,960]{0,1:T(8,128)} copy(f32[3072,960]{1,0:T(8,128)} %slice.6) | data formatting | bytes 23592960
  (13 shorter events, 0.1 us)
Async XLA Ops:
  7.2 376.5 %copy-start = (bf16[960,160]{0,1:T(8,128)(2,1)S(1)}, bf16[960,160]{0,1:T(8,128)(2,1)}, u32[]{:S(2)}) copy-start(bf16[960,160]{0,1:T(8,128)(2,1)} %param.9) | copy-start | bytes 921604
  7.2 200.0 %reduce-scatter.4.cloned.1.call-start = ((), (), s32[]{:S(2)}) async-start(), calls=%async_computation.3 | async-start | bytes 16711680 | tf_op jit(solution)/shard_map/reduce_scatter | solution.py:38
  118.2 1.0 copy-start.8
  118.2 177.6 %copy-start.7 = (bf16[160,960]{1,0:T(8,128)(2,1)S(1)}, bf16[160,960]{1,0:T(8,128)(2,1)}, u32[]{:S(2)}) copy-start(bf16[160,960]{1,0:T(8,128)(2,1)} %param.10) | copy-start | bytes 921604
  118.3 177.5 %all-gather.7.cloned.1.call-start = ((), (), s32[]{:S(2)}) async-start(), calls=%async_computation.6 | async-start | bytes 16711680 | tf_op jit(solution)/shard_map/all_gather | solution.py:50
  119.1 264.6 %all-gather.5.cloned.1.call-start = ((), (), s32[]{:S(2)}) async-start(), calls=%async_computation.4 | async-start | bytes 16711680 | tf_op jit(solution)/shard_map/all_gather | solution.py:43
  211.2 366.2 %reduce-scatter.8.cloned.1.call-start = ((), (), s32[]{:S(2)}) async-start(), calls=%async_computation.7 | async-start | bytes 33423360 | tf_op jit(solution)/shard_map/reduce_scatter | solution.py:56
  394.1 1.5 copy-start.5
  394.1 14.3 %copy-start.3 = (bf16[8192,160]{0,1:T(8,128)(2,1)}, bf16[8192,160]{0,1:T(8,128)(2,1)S(1)}, u32[]{:S(2)}) copy-start(bf16[8192,160]{0,1:T(8,128)(2,1)S(1)} %get-tuple-element.19) | copy-start | bytes 7864324
  408.1 341.6 %reduce-scatter.6.cloned.1.call-start = ((), (), s32[]{:S(2)}) async-start(), calls=%async_computation.5 | async-start | bytes 33423360 | tf_op jit(solution)/shard_map/reduce_scatter | solution.py:48
  420.9 156.4 %copy-start.2 = (bf16[512,960]{0,1:T(8,128)(2,1)S(1)}, bf16[512,960]{0,1:T(8,128)(2,1)}, u32[]{:S(2)}) copy-start(bf16[512,960]{0,1:T(8,128)(2,1)} %reduce-scatter.4.cloned.1.call-done) | copy-start | bytes 2949124
  420.9 328.8 %copy-start.6 = (bf16[512,960]{0,1:T(8,128)(2,1)S(1)}, bf16[512,960]{0,1:T(8,128)(2,1)}, u32[]{:S(2)}) copy-start(bf16[512,960]{0,1:T(8,128)(2,1)} %param.11) | copy-start | bytes 2949124
  421.0 419.7 %all-gather.9.cloned.1.call-start = ((), (), s32[]{:S(2)}) async-start(), calls=%async_computation.8 | async-start | bytes 16711680 | tf_op jit(solution)/shard_map/all_gather | solution.py:58
  753.9 12.2 %copy-start.4 = (bf16[8192,160]{0,1:T(8,128)(2,1)S(1)}, bf16[8192,160]{0,1:T(8,128)(2,1)}, u32[]{:S(2)}) copy-start(bf16[8192,160]{0,1:T(8,128)(2,1)} %copy-done.3) | copy-start | bytes 7864324
  951.7 12.3 %copy-start.1 = (bf16[960,160]{0,1:T(8,128)(2,1)S(1)}, bf16[960,160]{0,1:T(8,128)(2,1)}, u32[]{:S(2)}) copy-start(bf16[960,160]{0,1:T(8,128)(2,1)} %param.9) | copy-start | bytes 921604
Sparse Core Ops, SparseCore 0:
  118.4 88.7 reduce-scatter.3
  208.8 86.9 all-gather.6
  298.1 85.5 all-gather.4
  408.3 169.0 reduce-scatter.7
  579.6 170.0 reduce-scatter.5
  754.0 86.6 all-gather.8
where the time goes:
time: 973 us; the launch traced here: 971 us
  waiting for transfers between devices  641 us (66%)
  local copies, waits for them, and re-layouts  123 us (13%)
  other arithmetic  100 us (10%)
  matrix products  69.6 us (7%)
  blocking collectives  22.8 us (2%)
  between operations  14.2 us (1%)
    reduce_scatter x1, waiting for transfers between devices, local_step(): lax.psum_scatter(y_part, 'tensor', scatter_dimension=0, tiled=True)  170 us
    reduce_scatter x1, waiting for transfers between devices, local_step(): lax.psum_scatter(d_norm_part, 'tensor', scatter_dimension=0, tiled=True)  156 us
    reduce_scatter x1, waiting for transfers between devices, local_step(): lax.psum_scatter(emb_part, 'tensor', scatter_dimension=0, tiled=True)  88 us
    all_gather x1, waiting for transfers between devices, local_step(): grad_all = lax.all_gather(grad_out, 'tensor', tiled=True)  84.6 us
    all_gather x1, waiting for transfers between devices, local_step(): normed_all = lax.all_gather(normed, 'tensor', tiled=True)  77.1 us
    scatter-add x1, other arithmetic, local_step(): jax.ops.segment_sum(dx_all.astype(jnp.float32), seg_ids, num_segments=voc...  76.2 us
    gather x2, local copies, waits for them, and re-layouts, local_step(): jnp.take(emb_shard, jnp.clip(rel_ids, 0, vocab_local - 1), axis=0)  65.6 us
    all_gather x1, waiting for transfers between devices, local_step(): dx_all = lax.all_gather(dx_local, 'tensor', tiled=True)  63.3 us
  transfers between devices with their start and end apart: 6, of which 6 were waited for; matrix products, arithmetic and copies ran while one was open for 5% of the time, Pallas kernels for 0%

commit v1 on v0

v1 whole, which is shorter than its diff:
```python
import jax
import jax.numpy as jnp
from jax import lax
from jax.sharding import PartitionSpec as P

EPS = 1e-6


def rms_norm(x_rows, gain_f):
    inv_rms = lax.rsqrt(jnp.mean(x_rows * x_rows, axis=-1, keepdims=True) + EPS)
    return x_rows * inv_rms * gain_f


def gelu_tanh(values):
    return jax.nn.gelu(values, approximate=True)


def contract_last(left_op, right_op):
    return lax.dot_general(left_op, right_op, (((1,), (1,)), ((), ())), preferred_element_type=jnp.float32)


def contract_first(left_op, right_op):
    return lax.dot_general(left_op, right_op, (((0,), (0,)), ((), ())), preferred_element_type=jnp.float32)


def solution(mesh):
    tok_spec = P(('data', 'tensor'))
    row_spec = P(('data', 'tensor'), None)

    def local_step(token_ids, emb_shard, norm_gain, w_up, w_down, grad_out):
        vocab_local = emb_shard.shape[0]
        offset = lax.axis_index('tensor') * vocab_local
        ids_all = lax.all_gather(token_ids, 'tensor', tiled=True)
        up_all = lax.all_gather(w_up.T, 'tensor', tiled=True)
        down_all = lax.all_gather(w_down, 'tensor', tiled=True)
        rel_ids = ids_all - offset
        vocab_row = lax.broadcasted_iota(jnp.int32, (ids_all.shape[0], vocab_local), 1)
        pick = (vocab_row == rel_ids[:, None]).astype(jnp.bfloat16)
        emb_part = jnp.dot(pick, emb_shard, preferred_element_type=jnp.float32).astype(jnp.bfloat16)
        x_local = lax.psum_scatter(emb_part, 'tensor', scatter_dimension=0, tiled=True)
        x_f = x_local.astype(jnp.float32)
        gain_f = norm_gain.astype(jnp.float32)
        normed_f, norm_back = jax.vjp(lambda x_in: rms_norm(x_in, gain_f), x_f)
        normed = normed_f.astype(jnp.bfloat16)
        pre_act = contract_last(normed, up_all).astype(jnp.bfloat16)
        act_f, gelu_back = jax.vjp(gelu_tanh, pre_act.astype(jnp.float32))
        hidden = act_f.astype(jnp.bfloat16)
        d_hidden = contract_last(grad_out, down_all)
        d_pre = gelu_back(d_hidden)[0].astype(jnp.bfloat16)
        d_norm = jnp.dot(d_pre, up_all, preferred_element_type=jnp.float32)
        dx_local = (grad_out.astype(jnp.float32) + norm_back(d_norm)[0]).astype(jnp.bfloat16)
        dx_all = lax.all_gather(dx_local, 'tensor', tiled=True)
        y_local = jnp.dot(hidden, down_all, preferred_element_type=jnp.float32)
        out_local = (x_f + y_local).astype(jnp.bfloat16)
        d_w_down = lax.psum_scatter(contract_first(hidden, grad_out), 'tensor', scatter_dimension=0, tiled=True)
        d_w_up = lax.psum_scatter(contract_first(d_pre, normed), 'tensor', scatter_dimension=0, tiled=True).T
        vocab_col = lax.broadcasted_iota(jnp.int32, (vocab_local, ids_all.shape[0]), 0)
        place = (vocab_col == rel_ids[None, :]).astype(jnp.bfloat16)
        d_emb = jnp.dot(place, dx_all, preferred_element_type=jnp.float32)
        return out_local, d_emb, d_w_up, d_w_down

    return jax.shard_map(
        local_step,
        mesh=mesh,
        in_specs=(tok_spec, P('tensor', None), P(None), P(None, 'tensor'), P('tensor', None), row_spec),
        out_specs=(row_spec, row_spec, P('data', 'tensor'), row_spec),
        check_vma=False,
    )
```

time: 973 us -> 472 us (0.49)
  waiting for transfers between devices: 641 us -> 270 us
  local copies, waits for them, and re-layouts: 123 us -> 0.07 us
  other arithmetic: 100 us -> 3.04 us
  matrix products: 69.6 us -> 159 us
    reduce_scatter x2, waiting for transfers between devices: 327 us -> 87.4 us  [the longest x1 73.6 us: local_step(): lax.psum_scatter(contract_first(hidden, grad_out), 'tensor', scatter_dime...]
    all_gather x2, waiting for transfers between devices: 162 us -> 40.4 us  [the longest x1 40.3 us: local_step(): up_all = lax.all_gather(w_up.T, 'tensor', tiled=True)]
    dot_general x2 -> x4, matrix products: 22.9 us -> 124 us  [the longest x1 57.8 us: local_step(): jnp.dot(pick, emb_shard, preferred_element_type=jnp.float32)]
    scatter-add x1 -> x0, other arithmetic: 76.2 us -> none  [local_step(): jax.ops.segment_sum(dx_all.astype(jnp.float32), seg_ids, num_segments=voc...]
    gather x2 -> x0, local copies, waits for them, and re-layouts: 65.6 us -> none  [local_step(): jnp.take(emb_shard, jnp.clip(rel_ids, 0, vocab_local - 1), axis=0)]
    convert_element_type x1 -> x0, local copies, waits for them, and re-layouts: 23 us -> none  [local_step(): dx_all.astype(jnp.float32)]
    unnamed x20 -> x10, local copies, waits for them, and re-layouts: 22.3 us -> 0.07 us
    select_n x2 -> x0, other arithmetic: 14.1 us -> none  [the longest x1 13.4 us: local_step(): jnp.where(is_owned[:, None], looked_up, jnp.zeros((), looked_up.dtype))]
  transfers between devices with their start and end apart: 6 -> 6, of which waited for: 6 -> 5; matrix products, arithmetic and copies ran while one was open for 5% -> 31% of each run, Pallas kernels for 0% -> 0%
where the time goes in v1:
time: 472 us; the launch traced here: 470 us
  waiting for transfers between devices  270 us (57%)
  matrix products  159 us (34%)
  blocking collectives  22.9 us (5%)
  between operations  14.2 us (3%)
    reduce_scatter x1, waiting for transfers between devices, local_step(): lax.psum_scatter(emb_part, 'tensor', scatter_dimension=0, tiled=True)  80.4 us
    reduce_scatter x1, waiting for transfers between devices, local_step(): lax.psum_scatter(contract_first(hidden, grad_out), 'tensor', scatter_dime...  73.6 us
    all_gather x1, waiting for transfers between devices, local_step(): dx_all = lax.all_gather(dx_local, 'tensor', tiled=True)  60.4 us
    dot_general x1, matrix products, local_step(): jnp.dot(pick, emb_shard, preferred_element_type=jnp.float32)  57.8 us
    dot_general x1, matrix products, local_step(): d_emb = jnp.dot(place, dx_all, preferred_element_type=jnp.float32)  56 us
    all_gather x1, waiting for transfers between devices, local_step(): up_all = lax.all_gather(w_up.T, 'tensor', tiled=True)  40.3 us
    all_gather x1, blocking collectives, local_step(): ids_all = lax.all_gather(token_ids, 'tensor', tiled=True)  22.9 us
    dot_general x2, matrix products, contract_last(): lax.dot_general(left_op, right_op, (((1,), (1,)), ((), ())), preferred_el...  17.8 us
  transfers between devices with their start and end apart: 6, of which 5 were waited for; matrix products, arithmetic and copies ran while one was open for 31% of the time, Pallas kernels for 0%

profile of v1, /device:TPU:21, one launch (start us, length us, event | category | flops | bytes accessed | tf_op | source)
XLA Modules:
  0.0 470.4 jit_solution(3383198151451616065)
XLA Ops:
  7.2 0.1 all-gather.7.cloned.1.call-start
  7.2 0.7 all-gather.7.cloned.1.call-update
  8.0 0.1 reduce-scatter.4.cloned.1.call-start
  8.0 22.9 %all-gather = s32[16,1,512]{2,1,0:T(1,128)S(1)} all-gather(s32[1,1,512]{2,1,0:T(1,128)} %bitcast.22), channel_id=1, replica_groups=mesh['data'=4,'tensor'=16] {'tensor'}, dimensions={0}, use_global_device_ids=true | all-gather | bytes 34816 | tf_op jit(solution)/shard_map/all_gather | solution.py:33
  30.9 57.8 %fusion.4 = bf16[8192,960]{0,1:T(8,128)(2,1)} fusion(bf16[3072,960]{0,1:T(8,128)(2,1)} %param.7, s32[8192]{0:T(1024)S(1)} %bitcast.20), kind=kOutput, calls=%fused_computation.6 | convolution fusion | flops 48351412224 | bytes 21659648 | tf_op jit(solution)/shard_map/dot_general | solution.py:39
  88.7 0.0 copy-start.2
  88.7 0.0 copy-start.1
  88.7 0.1 reduce-scatter.4.cloned.1.call-update
  88.8 0.1 all-gather.5.cloned.1.call-start
  88.8 0.7 all-gather.5.cloned.1.call-update
  89.5 0.2 all-gather.9.cloned.1.call-start
  89.8 0.0 copy-done.2
  89.8 0.0 all-gather.7.cloned.1.call-done
  89.8 0.1 copy-done.1
  89.9 7.2 %fusion.29 = f32[512,2560]{1,0:T(8,128)} fusion(bf16[512,960]{0,1:T(8,128)(2,1)S(1)} %copy-done.1, bf16[2560,960]{1,0:T(8,128)(2,1)} %all-gather.7.cloned.1.call-done), kind=kOutput, calls=%fused_computation.42 | convolution fusion | flops 2516582400 | bytes 11141120 | tf_op jit(solution)/shard_map/dot_general | solution.py:19
  97.1 80.4 %reduce-scatter.4.cloned.1.call-done = bf16[512,960]{0,1:T(8,128)(2,1)} async-done(((bf16[8192,960]{0,1:T(8,128)(2,1)}), bf16[512,960]{0,1:T(8,128)(2,1)}) %reduce-scatter.4.cloned.1.call-update) | async-done | bytes 983056 | tf_op jit(solution)/shard_map/reduce_scatter | solution.py:40
  177.6 1.5 fusion.17
  179.0 0.0 copy-start
  179.0 40.3 %all-gather.5.cloned.1.call-done = bf16[2560,960]{1,0:T(8,128)(2,1)} async-done(((bf16[160,960]{1,0:T(8,128)(2,1)}), bf16[2560,960]{1,0:T(8,128)(2,1)}) %all-gather.5.cloned.1.call-update) | async-done | bytes 4915216 | tf_op jit(solution)/shard_map/all_gather | solution.py:34
  219.4 0.0 copy-start.3
  219.4 10.6 %fusion.8 = (bf16[512,2560]{1,0:T(8,128)(2,1)S(1)}, bf16[512,2560]{1,0:T(8,128)(2,1)}) fusion(f32[512,2560]{1,0:T(8,128)} %fusion.29, bf16[2560,960]{1,0:T(8,128)(2,1)} %all-gather.5.cloned.1.call-done, bf16[512,960]{0,1:T(8,128)(2,1)} %reduce-scatter.4.cloned.1.call-done, f32[960]{0:T(1024)S(1)} %convert_element_type.37, f32[512]{0:T(512)S(1)} %fusion.25), kind=kOutput, calls=%fused_computation.15 | convolution fusion | flops 2547384320 | bytes 16389888 | tf_op jit(solution)/shard_map/dot_general | solution.py:19
  230.0 0.0 copy-start.4
  230.0 0.0 copy-done
  230.0 0.0 copy-done.3
  230.0 2.9 fusion.21
  232.8 0.0 copy-done.4
  232.9 1.5 fusion.16
  234.4 0.1 all-gather.9.cloned.1.call-update
  234.5 0.1 reduce-scatter.6.cloned.1.call-start
  234.6 7.8 %fusion.22 = f32[2560,960]{1,0:T(8,128)} fusion(bf16[512,2560]{1,0:T(8,128)(2,1)} %copy-done.4, bf16[512,960]{0,1:T(8,128)(2,1)S(1)} %copy-done, f32[960]{0:T(1024)S(1)} %convert_element_type.37, f32[512]{0:T(512)S(1)} %fusion.25), kind=kOutput, calls=%fused_computation.36 | convolution fusion | flops 2518548480 | bytes 13440768 | tf_op jit(solution)/shard_map/dot_general | solution.py:23
  242.3 0.1 reduce-scatter.6.cloned.1.call-update
  242.4 0.3 reduce-scatter.8.cloned.1.call-start
  242.7 9.7 %fusion.26 = f32[2560,960]{1,0:T(8,128)} fusion(bf16[512,960]{0,1:T(8,128)(2,1)S(1)} %copy-done.1, bf16[512,2560]{1,0:T(8,128)(2,1)} %get-tuple-element.5), kind=kOutput, calls=%fused_computation.41 | convolution fusion | flops 2529689600 | bytes 13434880 | tf_op jit(solution)/shard_map/dot_general | solution.py:23
  252.3 0.1 reduce-scatter.8.cloned.1.call-update
  252.4 7.3 %fusion.20 = bf16[512,960]{0,1:T(8,128)(2,1)} fusion(bf16[512,960]{0,1:T(8,128)(2,1)S(1)} %copy-done, bf16[2560,960]{1,0:T(8,128)(2,1)} %all-gather.7.cloned.1.call-done, bf16[512,2560]{1,0:T(8,128)(2,1)} %get-tuple-element.5), kind=kOutput, calls=%fused_computation.34 | convolution fusion | flops 2531164160 | bytes 9502720 | tf_op jit(solution)/shard_map/dot_general | solution.py:53
  259.7 60.4 %all-gather.9.cloned.1.call-done = bf16[8192,960]{0,1:T(8,128)(2,1)} async-done(((bf16[512,960]{0,1:T(8,128)(2,1)}), bf16[8192,960]{0,1:T(8,128)(2,1)}) %all-gather.9.cloned.1.call-update) | async-done | bytes 15728656 | tf_op jit(solution)/shard_map/all_gather | solution.py:52
  320.1 56.0 %fusion.1 = f32[3072,960]{0,1:T(8,128)} fusion(bf16[8192,960]{0,1:T(8,128)(2,1)} %all-gather.9.cloned.1.call-done, s32[8192]{0:T(1024)S(1)} %bitcast.21), kind=kOutput, calls=%fused_computation.3 | convolution fusion | flops 48343547904 | bytes 27557888 | tf_op jit(solution)/shard_map/dot_general | solution.py:59
  376.2 13.8 %reduce-scatter.6.cloned.1.call-done = f32[160,960]{1,0:T(8,128)} async-done(((f32[2560,960]{1,0:T(8,128)}), f32[160,960]{1,0:T(8,128)}) %reduce-scatter.6.cloned.1.call-update) | async-done | bytes 614416 | tf_op jit(solution)/shard_map/reduce_scatter | solution.py:56
  390.0 73.6 %reduce-scatter.8.cloned.1.call-done = f32[160,960]{1,0:T(8,128)} async-done(((f32[2560,960]{1,0:T(8,128)}), f32[160,960]{1,0:T(8,128)}) %reduce-scatter.8.cloned.1.call-update) | async-done | bytes 614416 | tf_op jit(solution)/shard_map/reduce_scatter | solution.py:55
  (4 shorter events, 0.0 us)
Async XLA Ops:
  7.2 82.7 %all-gather.7.cloned.1.call-start = ((), (), s32[]{:S(2)}) async-start(), calls=%async_computation.5 | async-start | bytes 5570560 | tf_op jit(solution)/shard_map/all_gather | solution.py:35
  8.0 169.6 %reduce-scatter.4.cloned.1.call-start = ((), (), s32[]{:S(2)}) async-start(), calls=%async_computation.3 | async-start | bytes 16711680 | tf_op jit(solution)/shard_map/reduce_scatter | solution.py:40
  88.7 1.1 copy-start.2
  88.7 1.2 copy-start.1
  88.8 130.6 %all-gather.5.cloned.1.call-start = ((), (), s32[]{:S(2)}) async-start(), calls=%async_computation.4 | async-start | bytes 5570560 | tf_op jit(solution)/shard_map/all_gather | solution.py:34
  89.5 230.6 %all-gather.9.cloned.1.call-start = ((), (), s32[]{:S(2)}) async-start(), calls=%async_computation.6 | async-start | bytes 16711680 | tf_op jit(solution)/shard_map/all_gather | solution.py:52
  179.0 50.9 %copy-start = (bf16[512,960]{0,1:T(8,128)(2,1)S(1)}, bf16[512,960]{0,1:T(8,128)(2,1)}, u32[]{:S(2)}) copy-start(bf16[512,960]{0,1:T(8,128)(2,1)} %reduce-scatter.4.cloned.1.call-done) | copy-start | bytes 2949124
  219.4 10.6 %copy-start.3 = (bf16[2560,960]{1,0:T(8,128)(2,1)S(1)}, bf16[2560,960]{1,0:T(8,128)(2,1)}, u32[]{:S(2)}) copy-start(bf16[2560,960]{1,0:T(8,128)(2,1)} %all-gather.5.cloned.1.call-done) | copy-start | bytes 14745604
  230.0 2.9 copy-start.4
  234.5 155.5 %reduce-scatter.6.cloned.1.call-start = ((), (), s32[]{:S(2)}) async-start(), calls=%async_computation.7 | async-start | bytes 11141120 | tf_op jit(solution)/shard_map/reduce_scatter | solution.py:56
  242.4 221.2 %reduce-scatter.8.cloned.1.call-start = ((), (), s32[]{:S(2)}) async-start(), calls=%async_computation.8 | async-start | bytes 11141120 | tf_op jit(solution)/shard_map/reduce_scatter | solution.py:55
Sparse Core Ops, SparseCore 0:
  9.6 45.2 all-gather.6
  88.9 88.6 reduce-scatter.3
  179.2 40.1 all-gather.4
  234.6 85.4 all-gather.8
  322.9 67.0 reduce-scatter.5
  392.8 70.7 reduce-scatter.7

commit v2 on v1

v2 whole, which is shorter than its diff:
```python
import functools

import jax
import jax.numpy as jnp
from jax import lax
from jax.experimental import pallas as pl
from jax.experimental.pallas import tpu as pltpu
from jax.sharding import PartitionSpec as P

EPS = 1e-6
CAP = 64
LANES = 128
MESH = pl.DeviceIdType.MESH
VMEM_LIMIT = 67_000_000
F32 = jnp.float32
BF16 = jnp.bfloat16
SQRT_2_PI = 0.7978845608028654
CUBIC = 0.044715


def contract(left_op, right_op, left_dim, right_dim):
    dims = (((left_dim,), (right_dim,)), ((), ()))
    return lax.dot_general(left_op, right_op, dims, preferred_element_type=F32)


def iota(shape, dim):
    return lax.broadcasted_iota(jnp.int32, shape, dim)


def gelu_pair(u):
    t = jnp.tanh(SQRT_2_PI * (u + CUBIC * (u * u * u)))
    cdf = 0.5 * (1.0 + t)
    slope = cdf + u * (0.5 * (1.0 - t * t)) * (SQRT_2_PI * (1.0 + (3.0 * CUBIC) * (u * u)))
    return u * cdf, slope


class Ring:
    def __init__(self, n):
        self.n, self.nz, self.half = n, n // 2, n // 4
        self.me = lax.axis_index('tensor')
        self.c = lax.rem(self.me, 2)
        self.z = self.me // 2

    def chip(self, k):
        return lax.rem(self.z + (k + self.nz) % self.nz, self.nz)

    def dev(self, k):
        return {'tensor': 2 * self.chip(k) + self.c}

    @property
    def sibling(self):
        return {'tensor': self.me + 1 - 2 * self.c}

    def barrier(self):
        sem = pltpu.get_barrier_semaphore()
        for k in range(1, self.nz):
            pl.semaphore_signal(sem, inc=1, device_id=self.dev(k), device_id_type=MESH)
        pl.semaphore_signal(sem, inc=1, device_id=self.sibling, device_id_type=MESH)
        pl.semaphore_wait(sem, self.nz)


def slot_of(nz):
    half = nz // 2
    order = [half] + [s * k for k in range(half - 1, 0, -1) for s in (1, -1)] + [0]
    table = {k: i for i, k in enumerate(order)}
    table[-half] = table[half]
    return table


def gather_messages(half):
    right = [(w, k) for k in range(half) for w in (0, 1) if w == 0 or k < half - 1]
    return right, [(1 - w, k) for w, k in right]


def scatter_messages(half):
    right = [(0, half)]
    for k in range(half - 1, 0, -1):
        right += [(1, k), (0, k)]
    return right, [(1 - w, -k) for w, k in right]


def remote(src, dst, send_sem, recv_sem, device):
    return pltpu.make_async_remote_copy(
        src_ref=src, dst_ref=dst, send_sem=send_sem, recv_sem=recv_sem, device_id=device, device_id_type=MESH
    )


class Fold:
    def __init__(self, dm):
        self.dm = dm
        self.lo = dm // LANES * LANES
        self.dp = self.lo + LANES
        assert 2 * (dm - self.lo) == LANES

    def tail(self, value):
        h = value.shape[0] // 2
        return jnp.concatenate([value[:h, self.lo:self.dm], value[h:, self.lo:self.dm]], axis=1)

    def store(self, ref, value):
        h = value.shape[0] // 2
        ref[:, :self.lo] = value[:, :self.lo]
        ref[:h, self.lo:] = self.tail(value)

    def add(self, ref, value):
        h = value.shape[0] // 2
        ref[:, :self.lo] = ref[:, :self.lo] + value[:, :self.lo]
        ref[:h, self.lo:] = ref[:h, self.lo:] + self.tail(value)

    def unfold(self, ref):
        h = ref.shape[0] // 2
        ref[h:, self.lo:self.dm] = ref[:h, self.dm:self.dp]

    def send(self, src, dst, send_sem, recv_sem, device):
        return FoldCopy(self, src, dst, send_sem, recv_sem, device)


class FoldCopy:
    def __init__(self, fold, src, dst, send_sem, recv_sem, device):
        rows = src.shape[0]
        h = rows // 2
        parts = ((pl.ds(0, h), pl.ds(0, fold.dp)), (pl.ds(h, h), pl.ds(0, fold.lo)))
        self.copies = [
            remote(src.at[r, l], dst.at[r, l], send_sem.at[i], recv_sem.at[i], device)
            for i, (r, l) in enumerate(parts)
        ]

    def start(self):
        for copy in self.copies:
            copy.start()

    def wait_recv(self):
        for copy in self.copies:
            copy.wait_recv()

    def wait_send(self):
        for copy in self.copies:
            copy.wait_send()


def step_kernel(
    n, ids_ref, emb_ref, up_ref, down_ref, grad_ref, gain_ref,
    out_ref, dup_ref, ddown_ref, rows_ref, names_ref, flag_ref,
    w_v, g_v, x_v, xq_v, n_v, h_v, du_v, st_v, rb_v, snd_v, own_v, dnr_v, yr_v, dx_v, es_v, er_v, xs_v, xr_v,
    pick_v, tri_v, ids_v, col_v, req_s, req_r, emb_v, out_v, rows_v,
    ld_sem, emb_sem, ws_sem, wr_sem, ps_sem, pr_sem, qs_sem, qr_sem, xs_sem, xr_sem,
    ss_sem, sr_sem, es_sem, er_sem, out_sem,
):
    ring = Ring(n)
    nz, half, c, z = ring.nz, ring.half, ring.c, ring.z
    slot = slot_of(nz)
    dm, vocab = emb_ref.shape
    fl = up_ref.shape[0]
    tl = ids_ref.shape[1]
    tp = 2 * tl
    slots = nz * CAP
    fold = Fold(dm)
    step = emb_v.shape[2]
    sides = ((0, 1), (1, -1))
    sent = []

    load_grad = pltpu.make_async_copy(grad_ref, g_v.at[c], ld_sem.at[0])
    load_grad.start()
    own_ids = pltpu.make_async_copy(ids_ref, ids_v.at[c], ld_sem.at[1])
    own_ids.start()

    def load_emb(i):
        return pltpu.make_async_copy(emb_ref.at[:, pl.ds(i * step, step)], emb_v.at[i % 2], emb_sem.at[i % 2])

    for i in range(2):
        load_emb(i).start()
    mine = slot[0]
    for w, ref in enumerate((up_ref, down_ref)):
        w_v[w, mine, :, :dm] = ref[...]
        w_v[w, mine, :fl // 2, dm:] = ref[fl // 2:, fold.lo:]
    ring.barrier()

    def start(copy):
        copy.start()
        sent.append(copy)
        return copy

    swap_ids = start(remote(ids_ref, ids_v.at[c], ps_sem.at[0], pr_sem.at[0], ring.sibling))

    moves = [[], []]
    for side, sign in sides:
        for i, (w, k) in enumerate(gather_messages(half)[side]):
            src, dst = w_v.at[w, slot[-k * sign]], w_v.at[w, slot[-(k + 1) * sign]]
            moves[side].append(fold.send(src, dst, ws_sem.at[side, i], wr_sem.at[side, i], ring.dev(sign)))
    for i in range(2):
        for side, _ in sides:
            start(moves[side][i])
    swap_grad = start(remote(grad_ref, g_v.at[c], ps_sem.at[1], pr_sem.at[1], ring.sibling))

    def forward(i):
        for side, sign in sides:
            moves[side][i].wait_recv()
            if i + 2 < len(moves[side]):
                start(moves[side][i + 2])
            w, k = gather_messages(half)[side][i]
            fold.unfold(w_v.at[w, slot[-(k + 1) * sign]])

    own_ids.wait()
    swap_ids.wait_recv()
    ids = jnp.concatenate([ids_v[0], ids_v[1]], axis=1)
    ids_t = jnp.transpose(jnp.broadcast_to(ids, (LANES, tp)))
    seen = jnp.zeros((1, tp), F32)
    for i in range(tp // LANES):
        earlier = iota((LANES, tp), 0) + i * LANES < iota((LANES, tp), 1)
        tri_v[i * LANES:(i + 1) * LANES, :] = jnp.where(earlier, 1.0, 0.0).astype(BF16)
        same = ids_t[i * LANES:(i + 1) * LANES, 0:1] == ids
        hit = jnp.where(earlier & same, 1.0, 0.0)
        seen = jnp.maximum(seen, jnp.max(hit, axis=0, keepdims=True))
    row = iota((n, 1), 0)
    owner = jnp.where(row < nz, 2 * row + c, 2 * (row - nz) + 1 - c)
    base = (owner * vocab).astype(F32)
    member = jnp.where((seen < 0.5) & (ids >= base) & (ids < base + vocab), 1.0, 0.0)
    rank = jnp.dot(member.astype(BF16), tri_v[...], preferred_element_type=F32)
    count = jnp.max(jnp.sum(member, axis=1, keepdims=True), axis=0, keepdims=True)
    over = jnp.where(count > CAP, 1.0, 0.0)
    for k in range(nz):
        hit = (rank[k:k + 1, :] == iota((CAP, 1), 0).astype(F32)) & (member[k:k + 1, :] > 0.5)
        col = jnp.max(jnp.where(hit, ids, -1.0), axis=1, keepdims=True)
        col_v[k * CAP:(k + 1) * CAP, :] = jnp.broadcast_to(col, (CAP, LANES))
    cols_t = jnp.transpose(col_v[...])
    lane = iota((8, LANES), 1)
    per = LANES // CAP
    for k in range(nz):
        at = (k // per) * LANES
        tile = cols_t[0:8, at:at + LANES]
        if k % per:
            tile = pltpu.roll(tile, LANES - (k % per) * CAP, 1)
        req_s[k] = jnp.where(lane < CAP, tile, over)
    asks = []
    for d in range(1, nz):
        asks.append(start(remote(req_s.at[ring.chip(d)], req_r.at[z], qs_sem.at[d], qr_sem.at[d], ring.dev(d))))
    req_r[z] = req_s[z]
    forward(0)
    for t in range(2):
        pick_v[t] = jnp.where(col_v[:, 0:1] == ids_v[t], 1.0, 0.0).astype(BF16)

    for copy in asks:
        copy.wait_recv()
    flag = req_r[0]
    for k in range(1, nz):
        flag = jnp.maximum(flag, req_r[k])
    flag_ref[...] = flag
    tiles = []
    for p in range(nz // per):
        tile = req_r[p * per]
        for j in range(1, per):
            tile = jnp.where(lane < j * CAP, tile, pltpu.roll(req_r[p * per + j], j * CAP, 1))
        tiles.append(tile)
    names = jnp.concatenate(tiles, axis=1) - (ring.me * vocab).astype(F32)
    names_ref[...] = jnp.transpose(jnp.broadcast_to(names[0:1, :], (LANES, slots)))
    for i in range(vocab // step):
        load_emb(i).wait()
        hot = jnp.where(names_ref[:, 0:1] == (iota((1, step), 1) + i * step).astype(F32), 1.0, 0.0).astype(BF16)
        found = contract(hot, emb_v[i % 2], 1, 1)
        if i + 2 < vocab // step:
            load_emb(i + 2).start()
        for k in range(nz):
            part = found[k * CAP:(k + 1) * CAP]
            if i == 0:
                es_v[k, :, :dm] = part
            else:
                es_v[k, :, :dm] = es_v[k, :, :dm] + part
    for k in range(nz):
        fold.store(xs_v.at[k], es_v[k, :, :dm].astype(BF16))
    gives = []
    for d in range(1, nz):
        gives.append(start(fold.send(xs_v.at[ring.chip(d)], xr_v.at[z], xs_sem.at[d], xr_sem.at[d], ring.dev(d))))
    xr_v[z] = xs_v[z]
    forward(1)
    forward(2)
    forward(3)

    for copy in gives:
        copy.wait_recv()
    for k in range(nz):
        fold.unfold(xr_v.at[k])
    got = xr_v[...].reshape(slots, fold.dp)[:, :dm]
    for t in range(2):
        x_v[t] = contract(got, pick_v[t], 0, 0).astype(BF16)
    swap_x = remote(x_v, xq_v, ps_sem.at[2], pr_sem.at[2], ring.sibling)
    swap_x.start()
    load_grad.wait()
    swap_grad.wait_recv()
    swap_x.wait_send()
    swap_x.wait_recv()

    def lane_blocks(body):
        for t in range(2):
            lax.fori_loop(0, tl // LANES, functools.partial(body, t), 0)

    def lanes(b):
        return pl.ds(pl.multiple_of(b * LANES, LANES), LANES)

    def norm(t, b, carry):
        at = lanes(b)
        xb = x_v[t, :, at] + xq_v[t, :, at]
        x_v[t, :, at] = xb
        xf = xb.astype(F32)
        inv = lax.rsqrt(jnp.mean(xf * xf, axis=0, keepdims=True) + EPS)
        n_v[t, :, at] = (xf * inv * gain_ref[...]).astype(BF16)
        return carry

    lane_blocks(norm)

    def hidden(k):
        s = slot[k]

        def half_tokens(t, carry):
            u = jnp.dot(w_v[0, s, :, :dm], n_v[t], preferred_element_type=F32).astype(BF16).astype(F32)
            dh = jnp.dot(w_v[1, s, :, :dm], g_v[t], preferred_element_type=F32)
            act, slope = gelu_pair(u)
            h_v[t, s * fl:(s + 1) * fl, :] = act.astype(BF16)
            du_v[t, s * fl:(s + 1) * fl, :] = (dh * slope).astype(BF16)
            return carry

        lax.fori_loop(0, 2, half_tokens, 0)

    def grad_w(w, k):
        s = slice(slot[k] * fl, (slot[k] + 1) * fl)
        left, right = (h_v, g_v) if w else (du_v, n_v)
        return contract(left[0, s, :], right[0], 1, 1) + contract(left[1, s, :], right[1], 1, 1)

    orders = scatter_messages(half)
    sends = [[], []]
    for side, sign in sides:
        for i in range(len(orders[0])):
            src = st_v.at[side, i] if i < 2 else rb_v.at[side, i - 2]
            dst = rb_v.at[side, i]
            sends[side].append(fold.send(src, dst, ss_sem.at[side, i], sr_sem.at[side, i], ring.dev(sign)))

    def scatter(i):
        for side, _ in sides:
            part = grad_w(*orders[side][i])
            if i < 2:
                fold.store(st_v.at[side, i], part)
            else:
                sends[side][i - 2].wait_recv()
                fold.add(rb_v.at[side, i - 2], part)
            start(sends[side][i])

    hidden(0)
    for k in range(1, half):
        hidden(k)
        hidden(-k)
        for i in (2 * k + 2, 2 * k + 3):
            if i < len(moves[0]):
                forward(i)
    hidden(half)
    scatter(0)
    scatter(1)

    blocks = [(a, min(a + 2 * LANES, dm)) for a in range(0, dm, 2 * LANES)]

    def through(w, right, dst):
        for a, b in blocks:
            left = w_v[w, :, :, a:b].reshape(nz * fl, b - a)
            dst[a:b, :] = contract(left, right, 0, 0)

    through(0, du_v[1 - c], snd_v)
    swap_dn = remote(snd_v, dnr_v, ps_sem.at[3], pr_sem.at[3], ring.sibling)
    swap_dn.start()
    through(0, du_v[c], own_v)
    scatter(2)
    swap_dn.wait_send()
    swap_dn.wait_recv()

    def dx_block(b, carry):
        at = lanes(b)
        xf = x_v[c, :, at].astype(F32)
        inv = lax.rsqrt(jnp.mean(xf * xf, axis=0, keepdims=True) + EPS)
        q = (own_v[:, at] + dnr_v[:, at]) * gain_ref[...]
        dot = jnp.mean(xf * q, axis=0, keepdims=True)
        dxn = inv * q - xf * (inv * inv * inv * dot)
        dx_v[c, :, at] = (g_v[c, :, at].astype(F32) + dxn).astype(BF16)
        return carry

    lax.fori_loop(0, tl // LANES, dx_block, 0)
    swap_dx = start(remote(dx_v.at[c], dx_v.at[c], ps_sem.at[4], pr_sem.at[4], ring.sibling))
    through(1, h_v[1 - c], snd_v)
    swap_y = start(remote(snd_v, yr_v, ps_sem.at[5], pr_sem.at[5], ring.sibling))
    swap_dx.wait_recv()
    for k in range(nz):
        rows = slice(k * CAP, (k + 1) * CAP)
        fold.store(es_v.at[k], contract(pick_v[0, rows, :], dx_v[0], 1, 1) + contract(pick_v[1, rows, :], dx_v[1], 1, 1))
    backs = []
    for d in range(1, nz):
        backs.append(start(fold.send(es_v.at[ring.chip(d)], er_v.at[z], es_sem.at[d], er_sem.at[d], ring.dev(d))))
    er_v[z] = es_v[z]
    scatter(3)
    through(1, h_v[c], own_v)
    swap_y.wait_recv()

    def out_block(b, carry):
        at = lanes(b)
        out_v[:, at] = (x_v[c, :, at].astype(F32) + (own_v[:, at] + yr_v[:, at])).astype(BF16)
        return carry

    lax.fori_loop(0, tl // LANES, out_block, 0)
    keeps = [pltpu.make_async_copy(out_v, out_ref, out_sem.at[0])]
    keeps[0].start()
    last = len(orders[0])
    for i in range(4, last):
        scatter(i)

    for copy in backs:
        copy.wait_recv()
    for k in range(nz):
        fold.unfold(er_v.at[k])
        rows = er_v[k, :, :dm]
        at = slice(k * CAP, (k + 1) * CAP)
        for p in range(3):
            piece = rows.astype(BF16)
            rows_v[p, at, :] = piece
            rows = rows - piece.astype(F32)
    keeps.append(pltpu.make_async_copy(rows_v, rows_ref, out_sem.at[1]))
    keeps[1].start()

    for w in range(2):
        a, b = (last - 1, last - 2) if w == 0 else (last - 2, last - 1)
        part = grad_w(w, 0)
        sends[0][a].wait_recv()
        sends[1][b].wait_recv()
        rb_v[0, a] = rb_v[0, a] + rb_v[1, b]
        fold.unfold(rb_v.at[0, a])
        (dup_ref, ddown_ref)[w][...] = rb_v[0, a, :, :dm] + part
    for copy in sent:
        copy.wait_send()
    for copy in keeps:
        copy.wait()


def step(n, ids, emb_t, up, down, grad_t, gain):
    nz = n // 2
    dm, vocab = emb_t.shape
    tl, fl = ids.shape[1], up.shape[0]
    tp = 2 * tl
    dp = Fold(dm).dp
    slots = nz * CAP
    hops = nz - 1
    vmem, hbm = pl.BlockSpec(memory_space=pltpu.VMEM), pl.BlockSpec(memory_space=pl.ANY)
    dma = pltpu.SemaphoreType.DMA
    tokens = pltpu.VMEM((2, dm, tl), BF16)
    partial = pltpu.VMEM((dm, tl), F32)
    return pl.pallas_call(
        functools.partial(step_kernel, n),
        name='step',
        out_shape=(
            jax.ShapeDtypeStruct((dm, tl), BF16),
            jax.ShapeDtypeStruct((fl, dm), F32),
            jax.ShapeDtypeStruct((fl, dm), F32),
            jax.ShapeDtypeStruct((3, slots, dm), BF16),
            jax.ShapeDtypeStruct((slots, LANES), F32),
            jax.ShapeDtypeStruct((8, LANES), F32),
        ),
        in_specs=[vmem, hbm, vmem, vmem, hbm, vmem],
        out_specs=(hbm, vmem, vmem, hbm, vmem, vmem),
        scratch_shapes=[
            pltpu.VMEM((2, nz, fl, dp), BF16),
            tokens, tokens, tokens, tokens,
            pltpu.VMEM((2, nz * fl, tl), BF16),
            pltpu.VMEM((2, nz * fl, tl), BF16),
            pltpu.VMEM((2, 2, fl, dp), F32),
            pltpu.VMEM((2, hops, fl, dp), F32),
            partial, partial, partial, partial,
            tokens,
            pltpu.VMEM((nz, CAP, dp), F32),
            pltpu.VMEM((nz, CAP, dp), F32),
            pltpu.VMEM((nz, CAP, dp), BF16),
            pltpu.VMEM((nz, CAP, dp), BF16),
            pltpu.VMEM((2, slots, tl), BF16),
            pltpu.VMEM((tp, tp), BF16),
            pltpu.VMEM((2, 1, tl), F32),
            pltpu.VMEM((slots, LANES), F32),
            pltpu.VMEM((nz, 8, LANES), F32),
            pltpu.VMEM((nz, 8, LANES), F32),
            pltpu.VMEM((2, dm, 512), BF16),
            pltpu.VMEM((dm, tl), BF16),
            pltpu.VMEM((3, slots, dm), BF16),
            dma((2,)), dma((2,)), dma((2, hops, 2)), dma((2, hops, 2)), dma((6,)), dma((6,)),
            dma((nz,)), dma((nz,)), dma((nz, 2)), dma((nz, 2)),
            dma((2, hops, 2)), dma((2, hops, 2)), dma((nz, 2)), dma((nz, 2)), dma((2,)),
        ],
        compiler_params=pltpu.CompilerParams(
            collective_id=0, has_side_effects=True, vmem_limit_bytes=VMEM_LIMIT
        ),
    )(ids, emb_t, up, down, grad_t, gain)


def place_kernel(names_ref, rows_ref, out_ref):
    block = out_ref.shape[1]
    here = names_ref[:, 0:1] == (iota((1, block), 1) + pl.program_id(0) * block).astype(F32)
    hot = jnp.where(here, 1.0, 0.0).astype(BF16)
    out_ref[...] = contract(rows_ref[0], hot, 0, 0) + contract(rows_ref[1], hot, 0, 0) + contract(rows_ref[2], hot, 0, 0)


def place(vocab, names, rows):
    _, slots, dm = rows.shape
    block = 512
    return pl.pallas_call(
        place_kernel,
        name='place',
        grid=(vocab // block,),
        out_shape=jax.ShapeDtypeStruct((dm, vocab), F32),
        in_specs=[
            pl.BlockSpec((slots, LANES), lambda i: (0, 0)),
            pl.BlockSpec((3, slots, dm), lambda i: (0, 0, 0)),
        ],
        out_specs=pl.BlockSpec((dm, block), lambda i: (0, i)),
        compiler_params=pltpu.CompilerParams(vmem_limit_bytes=48_000_000),
    )(names, rows)


def swap_kernel(n, src_ref, dst_ref, keep_sem, send_sem, recv_sem):
    me = lax.axis_index('tensor')
    sem = pltpu.get_barrier_semaphore()
    for d in range(1, n):
        pl.semaphore_signal(sem, inc=1, device_id={'tensor': lax.rem(me + d, n)}, device_id_type=MESH)
    pl.semaphore_wait(sem, n - 1)
    keep = pltpu.make_async_copy(src_ref.at[me], dst_ref.at[me], keep_sem)
    keep.start()
    copies = []
    for d in range(1, n):
        to = lax.rem(me + d, n)
        copies.append(remote(src_ref.at[to], dst_ref.at[me], send_sem.at[d], recv_sem.at[d], {'tensor': to}))
        copies[-1].start()
    for copy in copies:
        copy.wait()
    keep.wait()


def swap_blocks(n, blocks, collective_id):
    hbm = pl.BlockSpec(memory_space=pl.ANY)
    return pl.pallas_call(
        functools.partial(swap_kernel, n),
        name='swap_blocks',
        out_shape=jax.ShapeDtypeStruct(blocks.shape, blocks.dtype),
        in_specs=[hbm],
        out_specs=hbm,
        scratch_shapes=[pltpu.SemaphoreType.DMA, pltpu.SemaphoreType.DMA((n,)), pltpu.SemaphoreType.DMA((n,))],
        compiler_params=pltpu.CompilerParams(collective_id=collective_id, has_side_effects=True),
    )(blocks)


def all_blocks(n, block, collective_id):
    return swap_blocks(n, jnp.broadcast_to(block[None], (n,) + block.shape), collective_id)


def rms_norm(x_rows, gain_f):
    inv_rms = lax.rsqrt(jnp.mean(x_rows * x_rows, axis=-1, keepdims=True) + EPS)
    return x_rows * inv_rms * gain_f


def dense_step(n, ids, emb, norm_gain, up, down, grad_out):
    vocab, dm = emb.shape
    fl = up.shape[0]
    base = (lax.axis_index('tensor') * vocab).astype(F32)
    ids_all = all_blocks(n, jnp.broadcast_to(ids, (8, ids.shape[1])), 1)[:, 0]
    hot = (iota((ids_all.size, vocab), 1).astype(F32) == ids_all.reshape(-1, 1) - base).astype(BF16)
    part = jnp.dot(hot, emb, preferred_element_type=F32).astype(BF16)
    x_f = jnp.sum(swap_blocks(n, part.reshape(n, -1, dm), 2).astype(F32), axis=0)
    ws = all_blocks(n, jnp.stack([up, down]), 3)
    up_all, down_all = ws[:, 0].reshape(-1, dm), ws[:, 1].reshape(-1, dm)
    normed_f, norm_back = jax.vjp(lambda x_in: rms_norm(x_in, norm_gain.astype(F32)), x_f)
    normed = normed_f.astype(BF16)
    pre_act = contract(normed, up_all, 1, 1).astype(BF16).astype(F32)
    act_f, slope = gelu_pair(pre_act)
    hidden = act_f.astype(BF16)
    d_pre = (contract(grad_out, down_all, 1, 1) * slope).astype(BF16)
    y = jnp.dot(hidden, down_all, preferred_element_type=F32)
    out = (x_f + y).astype(BF16)
    d_norm = jnp.dot(d_pre, up_all, preferred_element_type=F32)
    dx = (grad_out.astype(F32) + norm_back(d_norm)[0]).astype(BF16)
    d_w = jnp.stack([contract(d_pre, normed, 0, 0), contract(hidden, grad_out, 0, 0)]).reshape(2, n, fl, dm)
    d_w = jnp.sum(swap_blocks(n, jnp.moveaxis(d_w, 1, 0), 4), axis=0)
    dx_all = all_blocks(n, dx, 5).reshape(-1, dm)
    hot_t = (iota((vocab, ids_all.size), 0).astype(F32) == ids_all.reshape(1, -1) - base).astype(BF16)
    d_emb = jnp.dot(hot_t, dx_all, preferred_element_type=F32)
    return out.T, d_emb.T, d_w[0], d_w[1]


def solution(mesh):
    n = mesh.shape['tensor']
    tok_spec = P(('data', 'tensor'))
    row_spec = P(('data', 'tensor'), None)

    def local_step(token_ids, emb_shard, norm_gain, w_up, w_down, grad_out):
        vocab, dm = emb_shard.shape
        ids = token_ids.astype(F32)[None, :]
        gain = jnp.broadcast_to(norm_gain.astype(F32)[:, None], (dm, LANES))
        up = w_up.T
        out, d_up, d_down, rows, names, flags = step(n, ids, emb_shard.T, up, w_down, grad_out.T, gain)
        out, d_emb, d_up, d_down = lax.cond(
            flags[0, LANES - 1] > 0.5,
            lambda: dense_step(n, ids, emb_shard, norm_gain, up, w_down, grad_out),
            lambda: (out, place(vocab, names, rows), d_up, d_down),
        )
        return out.T, d_emb.T, d_up.T, d_down

    return jax.shard_map(
        local_step,
        mesh=mesh,
        in_specs=(tok_spec, P('tensor', None), P(None), P(None, 'tensor'), P('tensor', None), row_spec),
        out_specs=(row_spec, row_spec, P('data', 'tensor'), row_spec),
        check_vma=False,
    )
```

time: 472 us -> 267 us (0.57)
  waiting for transfers between devices: 270 us -> 0 us
  Pallas kernels: 0 us -> 243 us
  matrix products: 159 us -> 0 us
  blocking collectives: 22.9 us -> 0 us
  between operations: 14.2 us -> 1.82 us
  local copies, waits for them, and re-layouts: 0.07 us -> 9.1 us
  loops' own time: 0 us -> 7.91 us
    pallas_call x0 -> x2, Pallas kernels: none -> 243 us  [the longest x1 229 us: step(): pl.pallas_call(functools.partial(step_kernel, n), name='step', out_shape=...]
    reduce_scatter x3 -> x0, waiting for transfers between devices: 168 us -> none  [the longest x1 80.4 us: local_step(): lax.psum_scatter(emb_part, 'tensor', scatter_dimension=0, tiled=True)]
    dot_general x8 -> x0, matrix products: 159 us -> none  [the longest x1 57.8 us: local_step(): jnp.dot(pick, emb_shard, preferred_element_type=jnp.float32)]
    all_gather x3 -> x0, waiting for transfers between devices: 101 us -> none  [the longest x1 60.4 us: local_step(): dx_all = lax.all_gather(dx_local, 'tensor', tiled=True)]
    all_gather x1 -> x0, blocking collectives: 22.9 us -> none  [local_step(): ids_all = lax.all_gather(token_ids, 'tensor', tiled=True)]
    another operation x0 -> x1, loops' own time: none -> 7.91 us  [local_step(): lax.cond(flags[0, LANES - 1] > 0.5, lambda: dense_step(n, ids, emb_shard,...]
    unnamed x10 -> x5, local copies, waits for them, and re-layouts: 0.07 us -> 6.18 us
  transfers between devices with their start and end apart: 6 -> 0, of which waited for: 5 -> 0; matrix products, arithmetic and copies ran while one was open for 31% -> 0% of each run, Pallas kernels for 0% -> 0%
where the time goes in v2:
time: 267 us; the launch traced here: 262 us
  Pallas kernels  243 us (91%)
  local copies, waits for them, and re-layouts  9.1 us (3%)
  loops' own time  7.91 us (3%)
    pallas_call x1, Pallas kernels, step(): pl.pallas_call(functools.partial(step_kernel, n), name='step', out_shape=...  229 us
    pallas_call x1, Pallas kernels, place(): pl.pallas_call(place_kernel, name='place', grid=(vocab // block,), out_sh...  14 us
    another operation x1, loops' own time, local_step(): lax.cond(flags[0, LANES - 1] > 0.5, lambda: dense_step(n, ids, emb_shard,...  7.91 us
    unnamed x5, local copies, waits for them, and re-layouts  6.18 us

profile of v2, /device:TPU:21, one launch (start us, length us, event | category | flops | bytes accessed | tf_op | source)
XLA Modules:
  0.0 262.0 jit_solution(14874698926102930224)
XLA Ops:
  0.6 0.0 copy-start.4
  0.6 0.7 convert_element_type.59
  1.3 1.7 broadcast_in_dim.13.gain_ref
  3.0 228.5 %step.1 = (bf16[960,512]{1,0:T(8,128)(2,1)}, f32[160,960]{1,0:T(8,128)}, f32[160,960]{1,0:T(8,128)}, bf16[3,512,960]{2,1,0:T(8,128)(2,1)}, f32[512,128]{1,0:T(8,128)}, /*index=5*/f32[8,128]{1,0:T(8,128)}) custom-call(f32[1,512]{1,0:T(1,128)S(1)} %bitcast.64, bf16[960,3072]{1,0:T(8,128)(2,1)} %bitcast.46, bf16[160,960]{1,0:T(8,128)(2,1)} %bitcast.56, ...), custom_call_target="tpu_custom_call" | custom-call | tf_op jit(solution)/shard_map/step/pallas_call | solution.py:448
  231.5 1.3 slice.18
  233.4 0.0 copy-done.4
  233.4 21.9 %conditional.1 = (bf16[960,512]{1,0:T(8,128)(2,1)}, f32[960,3072]{1,0:T(8,128)}, f32[160,960]{1,0:T(8,128)}, f32[160,960]{1,0:T(8,128)}) conditional(s32[]{:T(128)} %bitcast.19, (f32[512,128]{1,0:T(8,128)}, bf16[3,512,960]{2,1,0:T(8,128)(2,1)}, bf16[960,512]{1,0:T(8,128)(2,1)}, f32[160,960]{1,0:T(8,128)}, f32[160,960]{1,0:T(8,128)}) %tuple.16, ...), branch_computations={%region_0.0_spmd, %region_1.6_spmd} | conditional | flops 111882289152 | bytes 372352000 | solution.py:596
  233.5 14.0 %place.1 = f32[960,3072]{1,0:T(8,128)} custom-call(f32[512,128]{1,0:T(8,128)} %get-tuple-element.23.names_ref, bf16[3,512,960]{2,1,0:T(8,128)(2,1)} %get-tuple-element.24.rows_ref), custom_call_target="tpu_custom_call" | custom-call | tf_op jit(solution)/shard_map/cond/branch_0_fun/place/pallas_call | solution.py:503
  255.4 2.2 copy.41
  257.6 2.0 copy.42
  259.5 2.0 copy.43
Async XLA Ops:
  0.6 232.8 %copy-start.4 = (bf16[960]{0:T(1024)(128)(2,1)S(1)}, bf16[960]{0:T(1024)(128)(2,1)}, u32[]{:S(2)}) copy-start(bf16[960]{0:T(1024)(128)(2,1)} %param.10) | copy-start | bytes 5764

commit v3 on v2

v3 whole, which is shorter than its diff:
```python
import functools

import jax
import jax.numpy as jnp
from jax import lax
from jax.experimental import pallas as pl
from jax.experimental.pallas import tpu as pltpu
from jax.sharding import PartitionSpec as P

EPS = 1e-6
CAP = 64
MULTI = 16
BHEAD = 32
LANES = 128
MESH = pl.DeviceIdType.MESH
VMEM_LIMIT = 67_000_000
F32 = jnp.float32
BF16 = jnp.bfloat16
SQRT_2_PI = 0.7978845608028654
CUBIC = 0.044715


def contract(left_op, right_op, left_dim, right_dim):
    dims = (((left_dim,), (right_dim,)), ((), ()))
    return lax.dot_general(left_op, right_op, dims, preferred_element_type=F32)


def iota(shape, dim):
    return lax.broadcasted_iota(jnp.int32, shape, dim)


def gelu_pair(u):
    t = jnp.tanh(SQRT_2_PI * (u + CUBIC * (u * u * u)))
    cdf = 0.5 * (1.0 + t)
    slope = cdf + u * (0.5 * (1.0 - t * t)) * (SQRT_2_PI * (1.0 + (3.0 * CUBIC) * (u * u)))
    return u * cdf, slope


class Ring:
    def __init__(self, n):
        self.n, self.nz, self.half = n, n // 2, n // 4
        self.me = lax.axis_index('tensor')
        self.c = lax.rem(self.me, 2)
        self.z = self.me // 2

    def chip(self, k):
        return lax.rem(self.z + (k + self.nz) % self.nz, self.nz)

    def dev(self, k):
        return {'tensor': 2 * self.chip(k) + self.c}

    @property
    def sibling(self):
        return {'tensor': self.me + 1 - 2 * self.c}

    def barrier(self):
        sem = pltpu.get_barrier_semaphore()
        for k in range(1, self.nz):
            pl.semaphore_signal(sem, inc=1, device_id=self.dev(k), device_id_type=MESH)
        pl.semaphore_signal(sem, inc=1, device_id=self.sibling, device_id_type=MESH)
        pl.semaphore_wait(sem, self.nz)


def slot_of(nz):
    half = nz // 2
    order = [half] + [s * k for k in range(half - 1, 0, -1) for s in (1, -1)] + [0]
    table = {k: i for i, k in enumerate(order)}
    table[-half] = table[half]
    return table


def gather_messages(half):
    right = [(w, k) for k in range(half) for w in (0, 1) if w == 0 or k < half - 1]
    return right, [(1 - w, k) for w, k in right]


def scatter_messages(half):
    right = [(0, half)]
    for k in range(half - 1, 0, -1):
        right += [(1, k), (0, k)]
    return right, [(1 - w, -k) for w, k in right]


def remote(src, dst, send_sem, recv_sem, device):
    return pltpu.make_async_remote_copy(
        src_ref=src, dst_ref=dst, send_sem=send_sem, recv_sem=recv_sem, device_id=device, device_id_type=MESH
    )


class Fold:
    def __init__(self, dm):
        self.dm = dm
        self.lo = dm // LANES * LANES
        self.dp = self.lo + LANES
        assert 2 * (dm - self.lo) == LANES

    def tail(self, value, h):
        low = value.shape[0] - h
        return jnp.concatenate([value[:low, self.lo:self.dm], value[h:, self.lo:self.dm]], axis=1)

    def store(self, ref, value, h):
        low = value.shape[0] - h
        ref[:, :self.lo] = value[:, :self.lo]
        ref[:low, self.lo:] = self.tail(value, h)
        if low < h:
            ref[low:h, self.lo:self.dm] = value[low:h, self.lo:self.dm]

    def add(self, ref, value, h):
        low = value.shape[0] - h
        ref[:, :self.lo] = ref[:, :self.lo] + value[:, :self.lo]
        ref[:low, self.lo:] = ref[:low, self.lo:] + self.tail(value, h)

    def unfold(self, ref, h):
        low = ref.shape[0] - h
        ref[h:, self.lo:self.dm] = ref[:low, self.dm:self.dp]

    def send(self, src, dst, h, send_sem, recv_sem, device):
        return FoldCopy(self, src, dst, h, send_sem, recv_sem, device)


class FoldCopy:
    def __init__(self, fold, src, dst, h, send_sem, recv_sem, device):
        parts = ((pl.ds(0, h), pl.ds(0, fold.dp)), (pl.ds(h, src.shape[0] - h), pl.ds(0, fold.lo)))
        self.copies = [
            remote(src.at[r, l], dst.at[r, l], send_sem.at[i], recv_sem.at[i], device)
            for i, (r, l) in enumerate(parts)
        ]

    def start(self):
        for copy in self.copies:
            copy.start()

    def wait_recv(self):
        for copy in self.copies:
            copy.wait_recv()

    def wait_send(self):
        for copy in self.copies:
            copy.wait_send()


def step_kernel(
    n, ids_ref, emb_ref, up_ref, down_ref, grad_ref, gain_ref,
    out_ref, dup_ref, ddown_ref, rows_ref, names_ref, flag_ref,
    w_v, gn_v, x_v, xq_v, hd_v, st_v, rb_v, snd_v, own_v, dnr_v, yr_v, dx_v, es_v, er_v, eb_v, eq_v, xs_v, xr_v,
    pick_v, tri_v, ids_v, col_v, name_v, req_s, req_r, emb_v, found_v, out_v, rows_v, row_v, gain_v,
    ld_sem, emb_sem, ws_sem, wr_sem, ps_sem, pr_sem, qs_sem, qr_sem, xs_sem, xr_sem,
    ss_sem, sr_sem, es_sem, er_sem, out_sem,
):
    ring = Ring(n)
    nz, half, c, z = ring.nz, ring.half, ring.c, ring.z
    slot = slot_of(nz)
    dm, vocab = emb_ref.shape
    fl = up_ref.shape[0]
    tl = ids_ref.shape[1]
    tp = 2 * tl
    slots = nz * CAP
    fold = Fold(dm)
    wh, xh, eh, bh = fl // 2, CAP // 2, MULTI // 2, BHEAD
    step = emb_v.shape[2]
    sides = ((0, 1), (1, -1))
    sent = []

    load_grad = pltpu.make_async_copy(grad_ref, gn_v.at[1, c], ld_sem.at[0])
    load_grad.start()
    own_ids = pltpu.make_async_copy(ids_ref, ids_v.at[c], ld_sem.at[1])
    own_ids.start()

    def load_emb(i):
        b = lax.rem(i, 2)
        at = pl.ds(pl.multiple_of(i * step, step), step)
        return pltpu.make_async_copy(emb_ref.at[:, at], emb_v.at[b], emb_sem.at[b])

    for i in range(2):
        load_emb(i).start()
    mine = slot[0]
    for w, ref in enumerate((up_ref, down_ref)):
        w_v[w, mine, :, :dm] = ref[...]
        w_v[w, mine, :wh, dm:] = ref[wh:, fold.lo:]
    row_v[...] = jnp.zeros_like(row_v)
    row_v[:, :dm] = gain_ref[...].astype(F32)
    gain_v[...] = jnp.transpose(jnp.broadcast_to(row_v[...], (LANES, fold.dp)))
    with jax.named_scope('barrier'):
        ring.barrier()

    def start(copy):
        copy.start()
        sent.append(copy)
        return copy

    swap_ids = start(remote(ids_ref, ids_v.at[c], ps_sem.at[0], pr_sem.at[0], ring.sibling))
    moves = [[], []]
    for side, sign in sides:
        for i, (w, k) in enumerate(gather_messages(half)[side]):
            src, dst = w_v.at[w, slot[-k * sign]], w_v.at[w, slot[-(k + 1) * sign]]
            moves[side].append(fold.send(src, dst, wh, ws_sem.at[side, i], wr_sem.at[side, i], ring.dev(sign)))
    for side, _ in sides:
        start(moves[side][0].copies[0])

    def forward(i):
        with jax.named_scope(f'fwd{i}'):
            for side, sign in sides:
                moves[side][i].wait_recv()
                if i + 2 < len(moves[side]):
                    start(moves[side][i + 2])
                w, k = gather_messages(half)[side][i]
                fold.unfold(w_v.at[w, slot[-(k + 1) * sign]], wh)

    own_ids.wait()
    with jax.named_scope('ids_wait'):
        swap_ids.wait_recv()
    ids = jnp.concatenate([ids_v[0], ids_v[1]], axis=1).astype(F32)
    ids_t = jnp.transpose(jnp.broadcast_to(ids, (LANES, tp)))
    seen = jnp.zeros((1, tp), F32)
    total = jnp.zeros((1, tp), F32)
    for i in range(tp // LANES):
        earlier = iota((LANES, tp), 0) + i * LANES < iota((LANES, tp), 1)
        tri = jnp.where(earlier, 1.0, 0.0)
        tri_v[i * LANES:(i + 1) * LANES, :] = tri.astype(BF16)
        same = jnp.where(ids_t[i * LANES:(i + 1) * LANES, 0:1] == ids, 1.0, 0.0)
        seen = jnp.maximum(seen, jnp.max(same * tri, axis=0, keepdims=True))
        total = total + jnp.sum(same, axis=0, keepdims=True)
    row = iota((n, 1), 0)
    owner = jnp.where(row < nz, 2 * row + c, 2 * (row - nz) + 1 - c)
    base = (owner * vocab).astype(F32)
    member = jnp.where((seen < 0.5) & (ids >= base) & (ids < base + vocab), 1.0, 0.0)
    multi = jnp.where(total > 1.5, 1.0, 0.0)
    several, single = member * multi, member * (1.0 - multi)
    both = jnp.concatenate([several, single], axis=0).astype(BF16)
    rank = jnp.dot(both, tri_v[...], preferred_element_type=F32)
    n_several = jnp.sum(several, axis=1, keepdims=True)
    count = n_several + jnp.sum(single, axis=1, keepdims=True)
    rank = jnp.where(several > 0.5, rank[:n], n_several + rank[n:])
    over = jnp.maximum(jnp.where(count > CAP, 1.0, 0.0), jnp.where(n_several > MULTI, 1.0, 0.0))
    over = jnp.max(over, axis=0, keepdims=True)
    for k in range(nz):
        hit = (rank[k:k + 1, :] == iota((CAP, 1), 0).astype(F32)) & (member[k:k + 1, :] > 0.5)
        col = jnp.max(jnp.where(hit, ids, -1.0), axis=1, keepdims=True)
        col_v[k * CAP:(k + 1) * CAP, :] = jnp.broadcast_to(col, (CAP, LANES))
    cols_t = jnp.transpose(col_v[...])
    lane = iota((8, LANES), 1)
    per = LANES // CAP
    for k in range(nz):
        at = (k // per) * LANES
        tile = cols_t[0:8, at:at + LANES]
        if k % per:
            tile = pltpu.roll(tile, LANES - (k % per) * CAP, 1)
        req_s[k] = jnp.where(lane < CAP, tile, over)
    asks = []
    for d in range(1, nz):
        asks.append(start(remote(req_s.at[ring.chip(d)], req_r.at[z], qs_sem.at[d], qr_sem.at[d], ring.dev(d))))
    for side, _ in sides:
        start(moves[side][0].copies[1])
        start(moves[side][1])
    swap_grad = start(remote(grad_ref, gn_v.at[1, c], ps_sem.at[1], pr_sem.at[1], ring.sibling))
    req_r[z] = req_s[z]
    for t in range(2):
        pick_v[t] = jnp.where(col_v[:, 0:1] == ids[:, t * tl:(t + 1) * tl], 1.0, 0.0).astype(BF16)

    with jax.named_scope('asks_wait'):
        for copy in asks:
            copy.wait_recv()
    flag = req_r[0]
    for k in range(1, nz):
        flag = jnp.maximum(flag, req_r[k])
    flag_ref[0, 0] = jnp.max(jnp.where(lane < CAP, 0.0, flag))
    tiles = []
    for p in range(nz // per):
        tile = req_r[p * per]
        for j in range(1, per):
            tile = jnp.where(lane < j * CAP, tile, pltpu.roll(req_r[p * per + j], j * CAP, 1))
        tiles.append(tile)
    names = jnp.concatenate(tiles, axis=1) - (ring.me * vocab).astype(F32)
    name_v[...] = jnp.transpose(jnp.broadcast_to(names[0:1, :], (LANES, slots)))
    found_v[...] = jnp.zeros_like(found_v)

    def find(i, carry):
        load_emb(i).wait()
        hot = jnp.where(name_v[:, 0:1] == (iota((1, step), 1) + i * step).astype(F32), 1.0, 0.0).astype(BF16)
        found_v[...] = found_v[...] + contract(hot, emb_v[lax.rem(i, 2)], 1, 1)

        @pl.when(i + 2 < vocab // step)
        def _():
            load_emb(i + 2).start()

        return carry

    with jax.named_scope('find'):
        lax.fori_loop(0, vocab // step, find, 0)
    for k in range(nz):
        fold.store(xs_v.at[k], found_v[k * CAP:(k + 1) * CAP, :].astype(BF16), xh)
    gives = []
    for d in range(1, nz):
        gives.append(start(fold.send(xs_v.at[ring.chip(d)], xr_v.at[z], xh, xs_sem.at[d], xr_sem.at[d], ring.dev(d))))
    xr_v[z] = xs_v[z]
    forward(0)
    forward(1)

    with jax.named_scope('gives_wait'):
        for copy in gives:
            copy.wait_recv()
    for k in range(nz):
        fold.unfold(xr_v.at[k], xh)
    got = xr_v[...].reshape(slots, fold.dp)[:, :dm]
    for t in range(2):
        x_v[t] = contract(got, pick_v[t], 0, 0).astype(BF16)
    swap_x = remote(x_v, xq_v, ps_sem.at[2], pr_sem.at[2], ring.sibling)
    swap_x.start()
    load_grad.wait()
    swap_grad.wait_recv()
    with jax.named_scope('swapx_wait'):
        swap_x.wait_send()
        swap_x.wait_recv()

    def lanes(b):
        return pl.ds(pl.multiple_of(b * LANES, LANES), LANES)

    def norm(i, carry):
        t, at = i // (tl // LANES), lanes(lax.rem(i, tl // LANES))
        xb = x_v[t, :, at] + xq_v[t, :, at]
        x_v[t, :, at] = xb
        xf = xb.astype(F32)
        inv = lax.rsqrt(jnp.mean(xf * xf, axis=0, keepdims=True) + EPS)
        gn_v[0, t, :, at] = (xf * inv * gain_v[:dm, :]).astype(BF16)
        return carry

    lax.fori_loop(0, tp // LANES, norm, 0)

    def hidden(lo, hi):
        def body(i, carry):
            s, t = lo + i // 2, lax.rem(i, 2)
            u = jnp.dot(w_v[0, s, :, :dm], gn_v[0, t], preferred_element_type=F32).astype(BF16).astype(F32)
            dh = jnp.dot(w_v[1, s, :, :dm], gn_v[1, t], preferred_element_type=F32)
            act, slope = gelu_pair(u)
            at = pl.ds(pl.multiple_of(s * fl, fl), fl)
            hd_v[1, t, at, :] = act.astype(BF16)
            hd_v[0, t, at, :] = (dh * slope).astype(BF16)
            return carry

        with jax.named_scope(f'hid{lo}'):
            lax.fori_loop(0, 2 * (hi - lo), body, 0)

    def grad_w(w, s):
        at = pl.ds(pl.multiple_of(s * fl, fl), fl)
        return contract(hd_v[w, 0, at, :], gn_v[w, 0], 1, 1) + contract(hd_v[w, 1, at, :], gn_v[w, 1], 1, 1)

    orders = scatter_messages(half)
    sends = [[], []]
    for side, sign in sides:
        for i in range(len(orders[0])):
            src = st_v.at[side, i] if i < 2 else rb_v.at[side, i - 2]
            dst = rb_v.at[side, i]
            sends[side].append(fold.send(src, dst, wh, ss_sem.at[side, i], sr_sem.at[side, i], ring.dev(sign)))

    def scatter(i):
        with jax.named_scope(f'scat{i}'):
            (w0, k0), (_, k1) = orders[0][i], orders[1][i]
            if i >= 2:
                for side, _ in sides:
                    sends[side][i - 2].wait_recv()

            def body(side, carry):
                w = w0 + side * (1 - 2 * w0)
                part = grad_w(w, slot[k0] + side * (slot[k1] - slot[k0]))
                if i < 2:
                    fold.store(st_v.at[side, i], part, wh)
                else:
                    fold.add(rb_v.at[side, i - 2], part, wh)
                return carry

            lax.fori_loop(0, 2, body, 0)
            for side, _ in sides:
                start(sends[side][i])

    last = len(moves[0]) - 1
    hidden(nz - 1, nz)
    hidden(nz - 3, nz - 1)
    for k in range(2, half):
        forward(2 * k - 2)
        forward(2 * k - 1)
        hidden(nz - 1 - 2 * k, nz + 1 - 2 * k)
    forward(last)
    hidden(0, 1)
    scatter(0)
    scatter(1)

    wide = 2 * LANES

    def through(w, t, dst):
        def body(b, carry):
            at = pl.ds(pl.multiple_of(b * wide, wide), wide)
            left = w_v[w, :, :, at].reshape(nz * fl, wide)
            dst[at, :] = contract(left, hd_v[w_of_hd[w], t], 0, 0)
            return carry

        lax.fori_loop(0, fold.dp // wide, body, 0)

    w_of_hd = (0, 1)
    with jax.named_scope('thru'):
        through(0, 1 - c, snd_v)
    body_rows = pl.ds(0, dm)
    swap_dn = remote(snd_v.at[body_rows], dnr_v, ps_sem.at[3], pr_sem.at[3], ring.sibling)
    swap_dn.start()
    through(0, c, own_v)
    with jax.named_scope('swapdn_wait'):
        swap_dn.wait_send()
        swap_dn.wait_recv()

    def dx_block(b, carry):
        at = lanes(b)
        xf = x_v[c, :, at].astype(F32)
        inv = lax.rsqrt(jnp.mean(xf * xf, axis=0, keepdims=True) + EPS)
        q = (own_v[:dm, at] + dnr_v[:, at]) * gain_v[:dm, :]
        dot = jnp.mean(xf * q, axis=0, keepdims=True)
        dxn = inv * q - xf * (inv * inv * inv * dot)
        dx_v[c, :, at] = (gn_v[1, c, :, at].astype(F32) + dxn).astype(BF16)
        return carry

    lax.fori_loop(0, tl // LANES, dx_block, 0)
    swap_dx = start(remote(dx_v.at[c], dx_v.at[c], ps_sem.at[4], pr_sem.at[4], ring.sibling))
    through(1, 1 - c, snd_v)
    swap_y = start(remote(snd_v.at[body_rows], yr_v, ps_sem.at[5], pr_sem.at[5], ring.sibling))
    with jax.named_scope('swapdx_wait'):
        swap_dx.wait_recv()

    def pack(k, carry):
        at = pl.ds(pl.multiple_of(k * CAP, CAP), CAP)
        rows = contract(pick_v[0, at, :], dx_v[0], 1, 1) + contract(pick_v[1, at, :], dx_v[1], 1, 1)
        fold.store(es_v.at[k], rows[:MULTI], eh)
        fold.store(eb_v.at[k], rows[MULTI:].astype(BF16), bh)
        return carry

    lax.fori_loop(0, nz, pack, 0)
    backs = []
    for d in range(1, nz):
        kk, to = ring.chip(d), ring.dev(d)
        backs.append(start(fold.send(es_v.at[kk], er_v.at[z], eh, es_sem.at[0, d], er_sem.at[0, d], to)))
        backs.append(start(fold.send(eb_v.at[kk], eq_v.at[z], bh, es_sem.at[1, d], er_sem.at[1, d], to)))
    er_v[z] = es_v[z]
    eq_v[z] = eb_v[z]
    scatter(2)
    through(1, c, own_v)
    scatter(3)
    with jax.named_scope('swapy_wait'):
        swap_y.wait_recv()

    def out_block(b, carry):
        at = lanes(b)
        out_v[:, at] = (x_v[c, :, at].astype(F32) + (own_v[:dm, at] + yr_v[:, at])).astype(BF16)
        return carry

    lax.fori_loop(0, tl // LANES, out_block, 0)
    keeps = [pltpu.make_async_copy(out_v, out_ref, out_sem.at[0])]
    keeps[0].start()
    last = len(orders[0])
    for i in range(4, last):
        scatter(i)

    with jax.named_scope('backs_wait'):
        for copy in backs:
            copy.wait_recv()
    lots, rest = nz * MULTI, CAP - MULTI

    def spread(k, carry):
        fold.unfold(er_v.at[k], eh)
        fold.unfold(eq_v.at[k], bh)
        rows = er_v[k, :, :dm]
        head = name_v[pl.ds(pl.multiple_of(k * CAP, CAP), MULTI), :]
        for p in range(3):
            at = pl.ds(pl.multiple_of(p * lots + k * MULTI, MULTI), MULTI)
            piece = rows.astype(BF16)
            rows_v[at, :] = piece
            names_ref[at, :] = head
            rows = rows - piece.astype(F32)
        at = pl.ds(pl.multiple_of(3 * lots + k * rest, 16), rest)
        rows_v[at, :] = eq_v[k, :, :dm]
        names_ref[at, :] = name_v[pl.ds(pl.multiple_of(k * CAP + MULTI, 16), rest), :]
        return carry

    lax.fori_loop(0, nz, spread, 0)
    keeps.append(pltpu.make_async_copy(rows_v, rows_ref, out_sem.at[1]))
    keeps[1].start()

    for w in range(2):
        a, b = (last - 1, last - 2) if w == 0 else (last - 2, last - 1)
        part = grad_w(w, mine)
        with jax.named_scope(f'fin{w}'):
            sends[0][a].wait_recv()
            sends[1][b].wait_recv()
        rb_v[0, a] = rb_v[0, a] + rb_v[1, b]
        fold.unfold(rb_v.at[0, a], wh)
        (dup_ref, ddown_ref)[w][...] = rb_v[0, a, :, :dm] + part
    for copy in sent:
        copy.wait_send()
    for copy in keeps:
        copy.wait()


def step(n, ids, emb_t, up, down, grad_t, gain):
    nz = n // 2
    dm, vocab = emb_t.shape
    tl, fl = ids.shape[1], up.shape[0]
    tp = 2 * tl
    dp = Fold(dm).dp
    slots = nz * CAP
    parts = slots + 2 * nz * MULTI
    hops = nz - 1
    vmem, hbm = pl.BlockSpec(memory_space=pltpu.VMEM), pl.BlockSpec(memory_space=pl.ANY)
    dma = pltpu.SemaphoreType.DMA
    tokens = pltpu.VMEM((2, dm, tl), BF16)
    return pl.pallas_call(
        functools.partial(step_kernel, n),
        name='step',
        out_shape=(
            jax.ShapeDtypeStruct((dm, tl), BF16),
            jax.ShapeDtypeStruct((fl, dm), F32),
            jax.ShapeDtypeStruct((fl, dm), F32),
            jax.ShapeDtypeStruct((parts, dm), BF16),
            jax.ShapeDtypeStruct((parts, LANES), F32),
            jax.ShapeDtypeStruct((1, 1), F32),
        ),
        in_specs=[vmem, hbm, vmem, vmem, hbm, vmem],
        out_specs=(hbm, vmem, vmem, hbm, vmem, pl.BlockSpec(memory_space=pltpu.SMEM)),
        scratch_shapes=[
            pltpu.VMEM((2, nz, fl, dp), BF16),
            pltpu.VMEM((2, 2, dm, tl), BF16),
            tokens, tokens,
            pltpu.VMEM((2, 2, nz * fl, tl), BF16),
            pltpu.VMEM((2, 2, fl, dp), F32),
            pltpu.VMEM((2, hops, fl, dp), F32),
            pltpu.VMEM((dp, tl), F32),
            pltpu.VMEM((dp, tl), F32),
            pltpu.VMEM((dm, tl), F32),
            pltpu.VMEM((dm, tl), F32),
            tokens,
            pltpu.VMEM((nz, MULTI, dp), F32),
            pltpu.VMEM((nz, MULTI, dp), F32),
            pltpu.VMEM((nz, CAP - MULTI, dp), BF16),
            pltpu.VMEM((nz, CAP - MULTI, dp), BF16),
            pltpu.VMEM((nz, CAP, dp), BF16),
            pltpu.VMEM((nz, CAP, dp), BF16),
            pltpu.VMEM((2, slots, tl), BF16),
            pltpu.VMEM((tp, tp), BF16),
            pltpu.VMEM((2, 1, tl), jnp.int32),
            pltpu.VMEM((slots, LANES), F32),
            pltpu.VMEM((slots, LANES), F32),
            pltpu.VMEM((nz, 8, LANES), F32),
            pltpu.VMEM((nz, 8, LANES), F32),
            pltpu.VMEM((2, dm, 512), BF16),
            pltpu.VMEM((slots, dm), F32),
            pltpu.VMEM((dm, tl), BF16),
            pltpu.VMEM((parts, dm), BF16),
            pltpu.VMEM((1, dp), F32),
            pltpu.VMEM((dp, LANES), F32),
            dma((2,)), dma((2,)), dma((2, hops, 2)), dma((2, hops, 2)), dma((6,)), dma((6,)),
            dma((nz,)), dma((nz,)), dma((nz, 2)), dma((nz, 2)),
            dma((2, hops, 2)), dma((2, hops, 2)), dma((2, nz, 2)), dma((2, nz, 2)), dma((2,)),
        ],
        compiler_params=pltpu.CompilerParams(
            collective_id=0, has_side_effects=True, vmem_limit_bytes=VMEM_LIMIT
        ),
    )(ids, emb_t, up, down, grad_t, gain)


def place_kernel(names_ref, rows_ref, out_ref, up_ref, down_ref, emb_out, out_out, up_out, down_out):
    block = emb_out.shape[1]
    here = names_ref[:, 0:1] == (iota((1, block), 1) + pl.program_id(0) * block).astype(F32)
    hot = jnp.where(here, 1.0, 0.0).astype(BF16)
    emb_out[...] = contract(rows_ref[...], hot, 0, 0)
    out_out[...] = out_ref[...]
    up_out[...] = up_ref[...]
    down_out[...] = down_ref[...]


def place(vocab, names, rows, out, d_up, d_down):
    parts, dm = rows.shape
    grid = 4
    passing = [pl.BlockSpec((a.shape[0] // grid, a.shape[1]), lambda i: (i, 0)) for a in (out, d_up, d_down)]
    return pl.pallas_call(
        place_kernel,
        name='place',
        grid=(grid,),
        out_shape=(jax.ShapeDtypeStruct((dm, vocab), F32),)
        + tuple(jax.ShapeDtypeStruct(a.shape, a.dtype) for a in (out, d_up, d_down)),
        in_specs=[pl.BlockSpec((parts, LANES), lambda i: (0, 0)), pl.BlockSpec((parts, dm), lambda i: (0, 0))] + passing,
        out_specs=(pl.BlockSpec((dm, vocab // grid), lambda i: (0, i)),) + tuple(passing),
        compiler_params=pltpu.CompilerParams(vmem_limit_bytes=48_000_000),
    )(names, rows, out, d_up, d_down)


def swap_kernel(n, src_ref, dst_ref, keep_sem, send_sem, recv_sem):
    me = lax.axis_index('tensor')
    sem = pltpu.get_barrier_semaphore()
    for d in range(1, n):
        pl.semaphore_signal(sem, inc=1, device_id={'tensor': lax.rem(me + d, n)}, device_id_type=MESH)
    pl.semaphore_wait(sem, n - 1)
    keep = pltpu.make_async_copy(src_ref.at[me], dst_ref.at[me], keep_sem)
    keep.start()
    copies = []
    for d in range(1, n):
        to = lax.rem(me + d, n)
        copies.append(remote(src_ref.at[to], dst_ref.at[me], send_sem.at[d], recv_sem.at[d], {'tensor': to}))
        copies[-1].start()
    for copy in copies:
        copy.wait()
    keep.wait()


def swap_blocks(n, blocks, collective_id):
    hbm = pl.BlockSpec(memory_space=pl.ANY)
    return pl.pallas_call(
        functools.partial(swap_kernel, n),
        name='swap_blocks',
        out_shape=jax.ShapeDtypeStruct(blocks.shape, blocks.dtype),
        in_specs=[hbm],
        out_specs=hbm,
        scratch_shapes=[pltpu.SemaphoreType.DMA, pltpu.SemaphoreType.DMA((n,)), pltpu.SemaphoreType.DMA((n,))],
        compiler_params=pltpu.CompilerParams(collective_id=collective_id, has_side_effects=True),
    )(blocks)


def all_blocks(n, block, collective_id):
    return swap_blocks(n, jnp.broadcast_to(block[None], (n,) + block.shape), collective_id)


def rms_norm(x_rows, gain_f):
    inv_rms = lax.rsqrt(jnp.mean(x_rows * x_rows, axis=-1, keepdims=True) + EPS)
    return x_rows * inv_rms * gain_f


def dense_step(n, ids, emb, norm_gain, up, down, grad_out):
    vocab, dm = emb.shape
    fl = up.shape[0]
    base = (lax.axis_index('tensor') * vocab).astype(F32)
    ids_all = all_blocks(n, jnp.broadcast_to(ids.astype(F32), (8, ids.shape[1])), 1)[:, 0]
    hot = (iota((ids_all.size, vocab), 1).astype(F32) == ids_all.reshape(-1, 1) - base).astype(BF16)
    part = jnp.dot(hot, emb, preferred_element_type=F32).astype(BF16)
    x_f = jnp.sum(swap_blocks(n, part.reshape(n, -1, dm), 2).astype(F32), axis=0)
    ws = all_blocks(n, jnp.stack([up, down]), 3)
    up_all, down_all = ws[:, 0].reshape(-1, dm), ws[:, 1].reshape(-1, dm)
    normed_f, norm_back = jax.vjp(lambda x_in: rms_norm(x_in, norm_gain.astype(F32)), x_f)
    normed = normed_f.astype(BF16)
    pre_act = contract(normed, up_all, 1, 1).astype(BF16).astype(F32)
    act_f, slope = gelu_pair(pre_act)
    hidden = act_f.astype(BF16)
    d_pre = (contract(grad_out, down_all, 1, 1) * slope).astype(BF16)
    y = jnp.dot(hidden, down_all, preferred_element_type=F32)
    out = (x_f + y).astype(BF16)
    d_norm = jnp.dot(d_pre, up_all, preferred_element_type=F32)
    dx = (grad_out.astype(F32) + norm_back(d_norm)[0]).astype(BF16)
    d_w = jnp.stack([contract(d_pre, normed, 0, 0), contract(hidden, grad_out, 0, 0)]).reshape(2, n, fl, dm)
    d_w = jnp.sum(swap_blocks(n, jnp.moveaxis(d_w, 1, 0), 4), axis=0)
    dx_all = all_blocks(n, dx, 5).reshape(-1, dm)
    hot_t = (iota((vocab, ids_all.size), 0).astype(F32) == ids_all.reshape(1, -1) - base).astype(BF16)
    d_emb = jnp.dot(hot_t, dx_all, preferred_element_type=F32)
    return d_emb.T, out.T, d_w[0], d_w[1]


def solution(mesh):
    n = mesh.shape['tensor']
    tok_spec = P(('data', 'tensor'))
    row_spec = P(('data', 'tensor'), None)

    def local_step(token_ids, emb_shard, norm_gain, w_up, w_down, grad_out):
        vocab, dm = emb_shard.shape
        ids, gain, up = token_ids[None, :], norm_gain[None, :], w_up.T
        out, d_up, d_down, rows, names, flag = step(n, ids, emb_shard.T, up, w_down, grad_out.T, gain)
        placed = place(vocab, names, rows, out, d_up, d_down)

        def again(state):
            return (jnp.zeros((), F32),) + dense_step(n, ids, emb_shard, norm_gain, up, w_down, grad_out)

        state = lax.while_loop(lambda state: state[0] > 0.5, again, (flag[0, 0],) + tuple(placed))
        _, d_emb, out, d_up, d_down = state
        return out.T, d_emb.T, d_up.T, d_down

    return jax.shard_map(
        local_step,
        mesh=mesh,
        in_specs=(tok_spec, P('tensor', None), P(None), P(None, 'tensor'), P('tensor', None), row_spec),
        out_specs=(row_spec, row_spec, P('data', 'tensor'), row_spec),
        check_vma=False,
    )
```

time: 267 us -> 227 us (0.85); the launches traced: 262 us -> 226 us
  Pallas kernels: 243 us -> 217 us
  loops' own time: 7.91 us -> 0.99 us
    pallas_call x1, Pallas kernels: 229 us -> 209 us  [step(): pl.pallas_call(functools.partial(step_kernel, n), name='step', out_shape=...]
    another operation x1, loops' own time: 7.91 us -> 0.99 us  [local_step(): lax.while_loop(lambda state: state[0] > 0.5, again, (flag[0, 0],) + tuple...]
    pallas_call x1, Pallas kernels: 14 us -> 8.15 us  [place(): pl.pallas_call(place_kernel, name='place', grid=(grid,), out_shape=(jax.S...]
    unnamed x5 -> x14, local copies, waits for them, and re-layouts: 6.18 us -> 5.78 us
where the time goes in v3:
time: 227 us; the launch traced here: 226 us
  Pallas kernels  217 us (96%)
  local copies, waits for them, and re-layouts  7.06 us (3%)
    pallas_call x1, Pallas kernels, step(): pl.pallas_call(functools.partial(step_kernel, n), name='step', out_shape=...  209 us
    pallas_call x1, Pallas kernels, place(): pl.pallas_call(place_kernel, name='place', grid=(grid,), out_shape=(jax.S...  8.15 us
    unnamed x14, local copies, waits for them, and re-layouts  5.78 us

profile of v3, /device:TPU:21, one launch (start us, length us, event | category | flops | bytes accessed | tf_op | source)
XLA Modules:
  0.0 226.4 jit_solution(6169446941186147492)
XLA Ops:
  0.6 1.3 broadcast_in_dim.13.gain_ref
  1.9 0.0 copy-start.9
  1.9 0.0 copy-start.11
  1.9 209.3 %step.1 = (bf16[960,512]{1,0:T(8,128)(2,1)}, f32[160,960]{1,0:T(8,128)}, f32[160,960]{1,0:T(8,128)}, bf16[768,960]{1,0:T(8,128)(2,1)}, f32[768,128]{1,0:T(8,128)}, /*index=5*/f32[1,1]{1,0:T(1,128)}) custom-call(s32[1,512]{1,0:T(1,128)} %bitcast.63, bf16[960,3072]{1,0:T(8,128)(2,1)} %bitcast.59, bf16[160,960]{1,0:T(8,128)(2,1)} %bitcast.55, ...), custom_call_target="tpu_custom_call" | custom-call | tf_op jit(solution)/shard_map/step/pallas_call | solution.py:511
  211.3 0.0 copy-start
  211.3 1.4 copy-done
  212.7 0.0 copy-start.1
  212.7 1.2 copy-done.1
  213.9 0.0 copy-start.2
  213.9 1.1 copy-done.2
  215.0 0.0 copy-start.3
  215.0 1.1 copy-done.3
  216.1 0.0 copy-start.4
  216.1 1.0 copy-done.4
  217.1 8.2 %place.1 = (f32[960,3072]{1,0:T(8,128)}, bf16[960,512]{1,0:T(8,128)(2,1)}, f32[160,960]{1,0:T(8,128)}, f32[160,960]{1,0:T(8,128)}) custom-call(f32[768,128]{1,0:T(8,128)S(1)} %copy-done.4, bf16[768,960]{1,0:T(8,128)(2,1)S(1)} %copy-done, bf16[960,512]{1,0:T(8,128)(2,1)S(1)} %copy-done.1, f32[160,960]{1,0:T(8,128)S(1)} %copy-done.2, f32[160,960]{1,0:T(8,128)S(1)} %copy-done.3), custom_call_target="tpu_custom_call" | custom-call | tf_op jit(solution)/shard_map/place/pallas_call | solution.py:579
  225.2 0.0 copy-done.9
  225.2 0.0 copy-done.11
  225.2 1.0 while.15
Async XLA Ops:
  1.9 223.3 %copy-start.9 = (bf16[960]{0:T(1024)(128)(2,1)S(1)}, bf16[960]{0:T(1024)(128)(2,1)}, u32[]{:S(2)}) copy-start(bf16[960]{0:T(1024)(128)(2,1)} %param.10) | copy-start | bytes 5764
  1.9 223.3 %copy-start.11 = (s32[512]{0:T(512)S(1)}, s32[512]{0:T(512)}, u32[]{:S(2)}) copy-start(s32[512]{0:T(512)} %param.8) | copy-start | bytes 6148
  211.3 1.4 copy-start
  212.7 1.2 copy-start.1
  213.9 1.1 copy-start.2
  215.0 1.1 copy-start.3
  216.1 1.0 copy-start.4

commit v4 on v3

--- a/solution.py
+++ b/solution.py
@@ -37,9 +37,10 @@
 
 
 class Ring:
-    def __init__(self, n):
-        self.n, self.nz, self.half = n, n // 2, n // 4
+    def __init__(self, n, groups):
+        self.n, self.nz, self.half, self.groups = n, n // 2, n // 4, groups
         self.me = lax.axis_index('tensor')
+        self.g = lax.axis_index('data')
         self.c = lax.rem(self.me, 2)
         self.z = self.me // 2
 
@@ -48,6 +49,9 @@
 
     def dev(self, k):
         return {'tensor': 2 * self.chip(k) + self.c}
+
+    def twin(self, e):
+        return {'data': lax.rem(self.g + e, self.groups), 'tensor': self.me}
 
     @property
     def sibling(self):
@@ -58,7 +62,9 @@
         for k in range(1, self.nz):
             pl.semaphore_signal(sem, inc=1, device_id=self.dev(k), device_id_type=MESH)
         pl.semaphore_signal(sem, inc=1, device_id=self.sibling, device_id_type=MESH)
-        pl.semaphore_wait(sem, self.nz)
+        for e in range(1, self.groups):
+            pl.semaphore_signal(sem, inc=1, device_id=self.twin(e), device_id_type=MESH)
+        pl.semaphore_wait(sem, self.nz + self.groups - 1)
 
 
 def slot_of(nz):
@@ -72,6 +78,15 @@
 def gather_messages(half):
     right = [(w, k) for k in range(half) for w in (0, 1) if w == 0 or k < half - 1]
     return right, [(1 - w, k) for w, k in right]
+
+
+BLOCK = 16
+
+
+def shared_blocks(groups):
+    each = max(1, 12 // groups)
+    assert groups * each % 2 == 0
+    return each, BLOCK * (-(-groups * each // 2))
 
 
 def scatter_messages(half):
@@ -140,16 +155,17 @@
 
 
 def step_kernel(
-    n, ids_ref, emb_ref, up_ref, down_ref, grad_ref, gain_ref,
+    n, groups, ids_ref, emb_ref, up_ref, down_ref, grad_ref, gain_ref,
     out_ref, dup_ref, ddown_ref, rows_ref, names_ref, flag_ref,
     w_v, gn_v, x_v, xq_v, hd_v, st_v, rb_v, snd_v, own_v, dnr_v, yr_v, dx_v, es_v, er_v, eb_v, eq_v, xs_v, xr_v,
     pick_v, tri_v, ids_v, col_v, name_v, req_s, req_r, emb_v, found_v, out_v, rows_v, row_v, gain_v,
-    ld_sem, emb_sem, ws_sem, wr_sem, ps_sem, pr_sem, qs_sem, qr_sem, xs_sem, xr_sem,
+    ld_sem, emb_sem, ws_sem, wr_sem, bs_sem, br_sem, ts_sem, tr_sem, ps_sem, pr_sem, qs_sem, qr_sem, xs_sem, xr_sem,
     ss_sem, sr_sem, es_sem, er_sem, out_sem,
 ):
-    ring = Ring(n)
+    ring = Ring(n, groups)
     nz, half, c, z = ring.nz, ring.half, ring.c, ring.z
     slot = slot_of(nz)
+    each, shared = shared_blocks(groups)
     dm, vocab = emb_ref.shape
     fl = up_ref.shape[0]
     tl = ids_ref.shape[1]
@@ -157,6 +173,8 @@
     slots = nz * CAP
     fold = Fold(dm)
     wh, xh, eh, bh = fl // 2, CAP // 2, MULTI // 2, BHEAD
+    gh = (fl - shared) // 2
+    ring_rows = pl.ds(shared, fl - shared)
     step = emb_v.shape[2]
     sides = ((0, 1), (1, -1))
     sent = []
@@ -176,9 +194,9 @@
     mine = slot[0]
     for w, ref in enumerate((up_ref, down_ref)):
         w_v[w, mine, :, :dm] = ref[...]
-        w_v[w, mine, :wh, dm:] = ref[wh:, fold.lo:]
+        w_v[w, mine, shared:shared + gh, dm:] = ref[shared + gh:, fold.lo:]
     row_v[...] = jnp.zeros_like(row_v)
-    row_v[:, :dm] = gain_ref[...].astype(F32)
+    row_v[:, :dm] = gain_ref[...].astype(F32).reshape(1, dm)
     gain_v[...] = jnp.transpose(jnp.broadcast_to(row_v[...], (LANES, fold.dp)))
     with jax.named_scope('barrier'):
         ring.barrier()
@@ -188,12 +206,60 @@
         sent.append(copy)
         return copy
 
+    blocks = []
+    for j in range(each):
+        b = ring.g * each + j
+        blocks.append((lax.rem(b, 2), pl.ds(pl.multiple_of(BLOCK * (b // 2), BLOCK), BLOCK)))
+
+    def hops(k):
+        return [
+            remote(
+                w_v.at[blocks[j][0], slot[-k * sign], blocks[j][1]],
+                w_v.at[blocks[j][0], slot[-(k + 1) * sign], blocks[j][1]],
+                bs_sem.at[side, j, k], br_sem.at[side, j, k], ring.dev(sign),
+            )
+            for j in range(each) for side, sign in sides if k < half - 1 or side == j % 2
+        ]
+
+    stages = ((nz - 3, nz), (nz - 5, nz - 3), (0, nz - 5))
+
+    def twins(stage):
+        lo, hi = stages[stage]
+        return [
+            remote(
+                w_v.at[w, pl.ds(lo, hi - lo), at], w_v.at[w, pl.ds(lo, hi - lo), at],
+                ts_sem.at[stage, j, e], tr_sem.at[stage, j, e], ring.twin(e),
+            )
+            for j, (w, at) in enumerate(blocks) for e in range(1, groups)
+        ]
+
+    block_moves = [hops(k) for k in range(half)]
+    twin_moves = [twins(stage) for stage in range(len(stages))]
+
+    def relay(k, stage):
+        with jax.named_scope(f'relay{k}'):
+            for copy in block_moves[k]:
+                copy.wait_recv()
+            if k + 1 < half:
+                for copy in block_moves[k + 1]:
+                    start(copy)
+            if stage is not None:
+                for copy in twin_moves[stage]:
+                    start(copy)
+
+    def from_twins(stage):
+        with jax.named_scope(f'twins{stage}'):
+            for copy in twin_moves[stage]:
+                copy.wait_recv()
+
+    for copy in block_moves[0]:
+        start(copy)
     swap_ids = start(remote(ids_ref, ids_v.at[c], ps_sem.at[0], pr_sem.at[0], ring.sibling))
     moves = [[], []]
     for side, sign in sides:
         for i, (w, k) in enumerate(gather_messages(half)[side]):
-            src, dst = w_v.at[w, slot[-k * sign]], w_v.at[w, slot[-(k + 1) * sign]]
-            moves[side].append(fold.send(src, dst, wh, ws_sem.at[side, i], wr_sem.at[side, i], ring.dev(sign)))
+            src, dst = w_v.at[w, slot[-k * sign], ring_rows], w_v.at[w, slot[-(k + 1) * sign], ring_rows]
+            moves[side].append(fold.send(src, dst, gh, ws_sem.at[side, i], wr_sem.at[side, i], ring.dev(sign)))
     for side, _ in sides:
         start(moves[side][0].copies[0])
 
@@ -204,7 +270,7 @@
                 if i + 2 < len(moves[side]):
                     start(moves[side][i + 2])
                 w, k = gather_messages(half)[side][i]
-                fold.unfold(w_v.at[w, slot[-(k + 1) * sign]], wh)
+                fold.unfold(w_v.at[w, slot[-(k + 1) * sign], ring_rows], gh)
 
     own_ids.wait()
     with jax.named_scope('ids_wait'):
@@ -249,6 +315,7 @@
     asks = []
     for d in range(1, nz):
         asks.append(start(remote(req_s.at[ring.chip(d)], req_r.at[z], qs_sem.at[d], qr_sem.at[d], ring.dev(d))))
+    relay(0, 0)
     for side, _ in sides:
         start(moves[side][0].copies[1])
         start(moves[side][1])
@@ -260,6 +327,7 @@
     with jax.named_scope('asks_wait'):
         for copy in asks:
             copy.wait_recv()
+    relay(1, 1)
     flag = req_r[0]
     for k in range(1, nz):
         flag = jnp.maximum(flag, req_r[k])
@@ -289,34 +357,37 @@
         lax.fori_loop(0, vocab // step, find, 0)
     for k in range(nz):
         fold.store(xs_v.at[k], found_v[k * CAP:(k + 1) * CAP, :].astype(BF16), xh)
+    relay(2, None)
     gives = []
     for d in range(1, nz):
         gives.append(start(fold.send(xs_v.at[ring.chip(d)], xr_v.at[z], xh, xs_sem.at[d], xr_sem.at[d], ring.dev(d))))
     xr_v[z] = xs_v[z]
     forward(0)
     forward(1)
+    relay(3, 2)
+    forward(2)
 
     with jax.named_scope('gives_wait'):
         for copy in gives:
             copy.wait_recv()
+    forward(3)
     for k in range(nz):
         fold.unfold(xr_v.at[k], xh)
     got = xr_v[...].reshape(slots, fold.dp)[:, :dm]
+    swaps = []
     for t in range(2):
         x_v[t] = contract(got, pick_v[t], 0, 0).astype(BF16)
-    swap_x = remote(x_v, xq_v, ps_sem.at[2], pr_sem.at[2], ring.sibling)
-    swap_x.start()
+        swaps.append(remote(x_v.at[t], xq_v.at[t], ps_sem.at[2 + t], pr_sem.at[2 + t], ring.sibling))
+        swaps[t].start()
+    forward(4)
     load_grad.wait()
     swap_grad.wait_recv()
-    with jax.named_scope('swapx_wait'):
-        swap_x.wait_send()
-        swap_x.wait_recv()
 
     def lanes(b):
         return pl.ds(pl.multiple_of(b * LANES, LANES), LANES)
 
-    def norm(i, carry):
-        t, at = i // (tl // LANES), lanes(lax.rem(i, tl // LANES))
+    def norm(t, b, carry):
+        at = lanes(b)
         xb = x_v[t, :, at] + xq_v[t, :, at]
         x_v[t, :, at] = xb
         xf = xb.astype(F32)
@@ -324,7 +395,11 @@
         gn_v[0, t, :, at] = (xf * inv * gain_v[:dm, :]).astype(BF16)
         return carry
 
-    lax.fori_loop(0, tp // LANES, norm, 0)
+    for t in range(2):
+        with jax.named_scope('swapx_wait'):
+            swaps[t].wait_send()
+            swaps[t].wait_recv()
+        lax.fori_loop(0, tl // LANES, functools.partial(norm, t), 0)
 
     def hidden(lo, hi):
         def body(i, carry):
@@ -372,17 +447,15 @@
             for side, _ in sides:
                 start(sends[side][i])
 
-    last = len(moves[0]) - 1
-    hidden(nz - 1, nz)
-    hidden(nz - 3, nz - 1)
-    for k in range(2, half):
-        forward(2 * k - 2)
-        forward(2 * k - 1)
-        hidden(nz - 1 - 2 * k, nz + 1 - 2 * k)
-    forward(last)
+    forward(5)
+    forward(6)
+    for stage in range(len(stages)):
+        from_twins(stage)
     hidden(0, 1)
     scatter(0)
+    hidden(1, nz - 5)
     scatter(1)
+    hidden(nz - 5, nz)
 
     wide = 2 * LANES
 
@@ -399,7 +472,7 @@
     with jax.named_scope('thru'):
         through(0, 1 - c, snd_v)
     body_rows = pl.ds(0, dm)
-    swap_dn = remote(snd_v.at[body_rows], dnr_v, ps_sem.at[3], pr_sem.at[3], ring.sibling)
+    swap_dn = remote(snd_v.at[body_rows], dnr_v, ps_sem.at[4], pr_sem.at[4], ring.sibling)
     swap_dn.start()
     through(0, c, own_v)
     with jax.named_scope('swapdn_wait'):
@@ -417,9 +490,9 @@
         return carry
 
     lax.fori_loop(0, tl // LANES, dx_block, 0)
-    swap_dx = start(remote(dx_v.at[c], dx_v.at[c], ps_sem.at[4], pr_sem.at[4], ring.sibling))
+    swap_dx = start(remote(dx_v.at[c], dx_v.at[c], ps_sem.at[5], pr_sem.at[5], ring.sibling))
     through(1, 1 - c, snd_v)
-    swap_y = start(remote(snd_v.at[body_rows], yr_v, ps_sem.at[5], pr_sem.at[5], ring.sibling))
+    swap_y = start(remote(snd_v.at[body_rows], yr_v, ps_sem.at[6], pr_sem.at[6], ring.sibling))
     with jax.named_scope('swapdx_wait'):
         swap_dx.wait_recv()
 
@@ -496,7 +569,7 @@
         copy.wait()
 
 
-def step(n, ids, emb_t, up, down, grad_t, gain):
+def step(n, groups, ids, emb_t, up, down, grad_t, gain):
     nz = n // 2
     dm, vocab = emb_t.shape
     tl, fl = ids.shape[1], up.shape[0]
@@ -505,11 +578,12 @@
     slots = nz * CAP
     parts = slots + 2 * nz * MULTI
     hops = nz - 1
+    each, _ = shared_blocks(groups)
     vmem, hbm = pl.BlockSpec(memory_space=pltpu.VMEM), pl.BlockSpec(memory_space=pl.ANY)
     dma = pltpu.SemaphoreType.DMA
     tokens = pltpu.VMEM((2, dm, tl), BF16)
     return pl.pallas_call(
-        functools.partial(step_kernel, n),
+        functools.partial(step_kernel, n, groups),
         name='step',
         out_shape=(
             jax.ShapeDtypeStruct((dm, tl), BF16),
@@ -552,7 +626,9 @@
             pltpu.VMEM((parts, dm), BF16),
             pltpu.VMEM((1, dp), F32),
             pltpu.VMEM((dp, LANES), F32),
-            dma((2,)), dma((2,)), dma((2, hops, 2)), dma((2, hops, 2)), dma((6,)), dma((6,)),
+            dma((2,)), dma((2,)), dma((2, hops, 2)), dma((2, hops, 2)),
+            dma((2, each, nz // 2)), dma((2, each, nz // 2)), dma((3, each, groups)), dma((3, each, groups)),
+            dma((7,)), dma((7,)),
             dma((nz,)), dma((nz,)), dma((nz, 2)), dma((nz, 2)),
             dma((2, hops, 2)), dma((2, hops, 2)), dma((2, nz, 2)), dma((2, nz, 2)), dma((2,)),
         ],
@@ -584,7 +660,7 @@
         + tuple(jax.ShapeDtypeStruct(a.shape, a.dtype) for a in (out, d_up, d_down)),
         in_specs=[pl.BlockSpec((parts, LANES), lambda i: (0, 0)), pl.BlockSpec((parts, dm), lambda i: (0, 0))] + passing,
         out_specs=(pl.BlockSpec((dm, vocab // grid), lambda i: (0, i)),) + tuple(passing),
-        compiler_params=pltpu.CompilerParams(vmem_limit_bytes=48_000_000),
+        compiler_params=pltpu.CompilerParams(vmem_limit_bytes=VMEM_LIMIT),
     )(names, rows, out, d_up, d_down)
 
 
@@ -657,14 +733,14 @@
 
 
 def solution(mesh):
-    n = mesh.shape['tensor']
+    n, groups = mesh.shape['tensor'], mesh.shape['data']
     tok_spec = P(('data', 'tensor'))
     row_spec = P(('data', 'tensor'), None)
 
     def local_step(token_ids, emb_shard, norm_gain, w_up, w_down, grad_out):
         vocab, dm = emb_shard.shape
-        ids, gain, up = token_ids[None, :], norm_gain[None, :], w_up.T
-        out, d_up, d_down, rows, names, flag = step(n, ids, emb_shard.T, up, w_down, grad_out.T, gain)
+        ids, gain, up = token_ids[None, :], norm_gain, w_up.T
+        out, d_up, d_down, rows, names, flag = step(n, groups, ids, emb_shard.T, up, w_down, grad_out.T, gain)
         placed = place(vocab, names, rows, out, d_up, d_down)
 
         def again(state):

time: 227 us -> 204 us (0.90)
  Pallas kernels: 217 us -> 202 us
  local copies, waits for them, and re-layouts: 7.06 us -> 0.01 us
    pallas_call x1, Pallas kernels: 209 us -> 192 us  [step(): pl.pallas_call(functools.partial(step_kernel, n, groups), name='step', ou...]
    unnamed x14 -> x4, local copies, waits for them, and re-layouts: 5.78 us -> 0.01 us
where the time goes in v4:
time: 204 us
  Pallas kernels  202 us (99%)
    pallas_call x1, Pallas kernels, step(): pl.pallas_call(functools.partial(step_kernel, n, groups), name='step', ou...  192 us
    pallas_call x1, Pallas kernels, place(): pl.pallas_call(place_kernel, name='place', grid=(grid,), out_shape=(jax.S...  10.2 us

profile of v4, /device:TPU:21, one launch (start us, length us, event | category | flops | bytes accessed | tf_op | source)
XLA Modules:
  0.0 203.9 jit_solution(4610802690620896378)
XLA Ops:
  0.6 0.0 copy-start.4
  0.6 0.0 copy-start.6
  0.7 191.9 %step.1 = (bf16[960,512]{1,0:T(8,128)(2,1)}, f32[160,960]{1,0:T(8,128)}, f32[160,960]{1,0:T(8,128)}, bf16[768,960]{1,0:T(8,128)(2,1)}, f32[768,128]{1,0:T(8,128)}, /*index=5*/f32[1,1]{1,0:T(1,128)}) custom-call(s32[1,512]{1,0:T(1,128)} %bitcast.63, bf16[960,3072]{1,0:T(8,128)(2,1)} %bitcast.59, bf16[160,960]{1,0:T(8,128)(2,1)} %bitcast.55, ...), custom_call_target="tpu_custom_call" | custom-call | tf_op jit(solution)/shard_map/step/pallas_call | solution.py:585
  192.6 10.2 %place.1 = (f32[960,3072]{1,0:T(8,128)}, bf16[960,512]{1,0:T(8,128)(2,1)}, f32[160,960]{1,0:T(8,128)}, f32[160,960]{1,0:T(8,128)}) custom-call(f32[768,128]{1,0:T(8,128)} %get-tuple-element.70.names_ref, bf16[768,960]{1,0:T(8,128)(2,1)} %get-tuple-element.71.rows_ref, bf16[960,512]{1,0:T(8,128)(2,1)} %get-tuple-element.72.out_ref, ...), custom_call_target="tpu_custom_call" | custom-call | tf_op jit(solution)/shard_map/place/pallas_call | solution.py:655
  202.7 0.0 copy-done.4
  202.7 0.0 copy-done.6
  202.7 0.9 while.15
Async XLA Ops:
  0.6 202.1 %copy-start.4 = (bf16[960]{0:T(1024)(128)(2,1)S(1)}, bf16[960]{0:T(1024)(128)(2,1)}, u32[]{:S(2)}) copy-start(bf16[960]{0:T(1024)(128)(2,1)} %gain_ref.1) | copy-start | bytes 5764
  0.6 202.1 %copy-start.6 = (s32[512]{0:T(512)S(1)}, s32[512]{0:T(512)}, u32[]{:S(2)}) copy-start(s32[512]{0:T(512)} %param.8) | copy-start | bytes 6148

commit v5 on v4

v5 whole, which is shorter than its diff:
```python
import functools

import jax
import jax.numpy as jnp
from jax import lax
from jax.experimental import pallas as pl
from jax.experimental.pallas import tpu as pltpu
from jax.sharding import PartitionSpec as P

EPS = 1e-6
CAP = 64
MULTI = 16
PAIR = 2
BHEAD = 32
PLACE_GRID = 6
PLACE_ROWS = 256
LANES = 128
MESH = pl.DeviceIdType.MESH
VMEM_LIMIT = 67_000_000
F32 = jnp.float32
BF16 = jnp.bfloat16
SQRT_2_PI = 0.7978845608028654
CUBIC = 0.044715


def contract(left_op, right_op, left_dim, right_dim):
    dims = (((left_dim,), (right_dim,)), ((), ()))
    return lax.dot_general(left_op, right_op, dims, preferred_element_type=F32)


def first_first(left_op, right_op):
    return contract(left_op, right_op, 0, 0)


def last_last(left_op, right_op):
    return contract(left_op, right_op, 1, 1)


def iota(shape, dim):
    return lax.broadcasted_iota(jnp.int32, shape, dim)


def down(rows, start=0):
    return iota((rows, 1), 0) + start


def across(lanes, start=0):
    return iota((1, lanes), 1) + start


def flags(mask):
    return jnp.where(mask, 1.0, 0.0)


def one_hot(mask):
    return flags(mask).astype(BF16)


def over_rows(reduce, value):
    return reduce(value, axis=0, keepdims=True)


def over_lanes(reduce, value):
    return reduce(value, axis=1, keepdims=True)


def earlier_than(rows, lanes, start):
    return down(rows, start) < across(lanes)


def gelu_pair(u):
    t = jnp.tanh(SQRT_2_PI * (u + CUBIC * (u * u * u)))
    cdf = 0.5 * (1.0 + t)
    slope = cdf + u * (0.5 * (1.0 - t * t)) * (SQRT_2_PI * (1.0 + (3.0 * CUBIC) * (u * u)))
    return u * cdf, slope


def rows_at(i):
    return slice(i * LANES, (i + 1) * LANES)


class Ring:
    def __init__(self, n, groups):
        self.n, self.nz, self.half, self.groups = n, n // 2, n // 4, groups
        self.me = lax.axis_index('tensor')
        self.g = lax.axis_index('data')
        self.c = lax.rem(self.me, 2)
        self.z = self.me // 2

    def chip(self, k):
        return lax.rem(self.z + (k + self.nz) % self.nz, self.nz)

    def dev(self, k):
        return {'tensor': 2 * self.chip(k) + self.c}

    def twin(self, e):
        return {'data': lax.rem(self.g + e, self.groups), 'tensor': self.me}

    @property
    def sibling(self):
        return {'tensor': self.me + 1 - 2 * self.c}

    def greet(self):
        sem = pltpu.get_barrier_semaphore()
        for k in range(1, self.nz):
            pl.semaphore_signal(sem, device_id=self.dev(k), device_id_type=MESH)
        pl.semaphore_signal(sem, device_id=self.sibling, device_id_type=MESH)
        for e in range(1, self.groups):
            pl.semaphore_signal(sem, device_id=self.twin(e), device_id_type=MESH)

    def meet(self):
        pl.semaphore_wait(pltpu.get_barrier_semaphore(), self.nz + self.groups - 1)


def slot_of(nz):
    half = nz // 2
    order = [half] + [s * k for k in range(half - 1, 0, -1) for s in (1, -1)] + [0]
    table = {k: i for i, k in enumerate(order)}
    table[-half] = table[half]
    return table


def gather_messages(half):
    right = [(w, k) for k in range(half) for w in (0, 1) if w == 0 or k < half - 1]
    return right, [(1 - w, k) for w, k in right]


BLOCK = 16


def shared_blocks(fl, groups):
    shared = fl - 2 * BLOCK
    count = 2 if groups * BLOCK <= shared else 1
    height = 2 * shared // (groups * count)
    assert height % BLOCK == 0 and height * groups * count == 2 * shared
    return count, height, shared


def far_first(nz):
    return [(nz // 2 + (-1) ** r * ((r + 1) // 2)) % nz for r in range(nz)]


def scatter_messages(half):
    right = [(0, half)]
    for k in range(half - 1, 0, -1):
        right += [(1, k), (0, k)]
    return right, [(1 - w, -k) for w, k in right]


def remote(src, dst, send_sem, recv_sem, device):
    return pltpu.make_async_remote_copy(
        src_ref=src, dst_ref=dst, send_sem=send_sem, recv_sem=recv_sem, device_id=device, device_id_type=MESH
    )


class Fold:
    def __init__(self, dm):
        self.dm = dm
        self.lo = dm // LANES * LANES
        self.dp = self.lo + LANES
        assert 2 * (dm - self.lo) == LANES

    def tail(self, value, h):
        low = value.shape[0] - h
        return jnp.concatenate([value[:low, self.lo:self.dm], value[h:, self.lo:self.dm]], axis=1)

    def store(self, ref, value, h):
        low = value.shape[0] - h
        ref[:, :self.lo] = value[:, :self.lo]
        ref[:low, self.lo:] = self.tail(value, h)
        if low < h:
            ref[low:h, self.lo:self.dm] = value[low:h, self.lo:self.dm]

    def add(self, ref, value, h):
        low = value.shape[0] - h
        ref[:, :self.lo] = ref[:, :self.lo] + value[:, :self.lo]
        ref[:low, self.lo:] = ref[:low, self.lo:] + self.tail(value, h)

    def unfold(self, ref, h):
        low = ref.shape[0] - h
        ref[h:, self.lo:self.dm] = ref[:low, self.dm:self.dp]

    def send(self, src, dst, h, send_sem, recv_sem, device):
        return FoldCopy(self, src, dst, h, send_sem, recv_sem, device, self.spare[jnp.dtype(src.dtype)])


class FoldCopy:
    def __init__(self, fold, src, dst, h, send_sem, recv_sem, device, spare):
        low = src.shape[0] - h
        parts = ((pl.ds(0, h), pl.ds(0, fold.dp)), (pl.ds(h, low), pl.ds(0, fold.lo)))
        self.copies = [remote(src.at[r, l], dst.at[r, l], send_sem, recv_sem, device) for r, l in parts]
        size = h * fold.dp + low * fold.lo
        tile = 16 if jnp.dtype(spare.dtype) == jnp.dtype(BF16) else 8
        width = next(w for w in range(LANES, spare.shape[1] + 1, LANES)
                     if size % (w * tile) == 0 and size // w <= spare.shape[0])
        whole = spare.at[pl.ds(0, size // width), pl.ds(0, width)]
        self.whole = remote(whole, whole, send_sem, recv_sem, device)

    def start(self):
        for copy in self.copies:
            copy.start()

    def wait_recv(self):
        self.whole.wait_recv()

    def wait_send(self):
        self.whole.wait_send()


def step_kernel(
    n, groups, ids_ref, emb_ref, up_ref, down_ref, grad_ref, gain_ref,
    out_ref, dup_ref, ddown_ref, rows_ref, names_ref, bounds_ref, flag_ref,
    w_v, gn_v, x_v, hd_v, st_v, rb_v, snd_v, own_v, dnr_v, yr_v, dx_v, es_v, er_v, eb_v, eq_v, xs_v, xr_v,
    pick_v, tri_v, ids_v, col_v, name_v, nrow_v, req_s, req_r, emb_v, found_v, out_v, rows_v, row_v, gain_v,
    own_w, line_v, flag_v, names_v, bounds_v, dw_v, xo_v, xf_sem, xg_sem,
    ld_sem, emb_sem, ws_sem, wr_sem, bs_sem, br_sem, ts_sem, tr_sem, ps_sem, pr_sem, qs_sem, qr_sem, xr_sem,
    ss_sem, sr_sem, er_sem, out_sem,
):
    ring = Ring(n, groups)
    nz, half, c, z = ring.nz, ring.half, ring.c, ring.z
    slot = slot_of(nz)
    dm, vocab = emb_ref.shape
    fl = up_ref.shape[0]
    each, height, shared = shared_blocks(fl, groups)
    order = far_first(nz)
    back = [order.index((nz - d) % nz) for d in order]
    tl = ids_ref.shape[1]
    tp = 2 * tl
    slots = nz * CAP
    fold = Fold(dm)
    fold.spare = {jnp.dtype(BF16): gn_v.at[0, 0], jnp.dtype(F32): own_v}
    wh, xh, eh, bh = fl // 2, CAP // 2, MULTI // 2, BHEAD
    gh = (fl - shared) // 2
    ring_rows = pl.ds(shared, fl - shared)
    step = emb_v.shape[2]
    sides = ((0, 1), (1, -1))
    sent = []

    ring.greet()
    own_ids = pltpu.make_async_copy(ids_ref, ids_v.at[c], ld_sem.at[1])
    load_w = [pltpu.make_async_copy(ref, own_w.at[w], ld_sem.at[2 + w]) for w, ref in enumerate((up_ref, down_ref))]
    load_gain = pltpu.make_async_copy(gain_ref, line_v, ld_sem.at[4])
    load_grad = pltpu.make_async_copy(grad_ref, gn_v.at[1, c], ld_sem.at[0])
    for copy in [own_ids, load_gain] + load_w + [load_grad]:
        copy.start()

    def load_emb(i):
        at = pl.ds(pl.multiple_of(i * step, step), step)
        return pltpu.make_async_copy(emb_ref.at[:, at], emb_v.at[i], emb_sem.at[i])

    for i in range(vocab // step):
        load_emb(i).start()
    for i in range(tp // LANES):
        tri_v[rows_at(i), :] = one_hot(earlier_than(LANES, tp, i * LANES))
    mine = slot[0]
    for w in range(PAIR):
        load_w[w].wait()
        w_v[w, mine, :, :dm] = own_w[w]
        w_v[w, mine, shared:shared + gh, dm:] = own_w[w, shared + gh:, fold.lo:]
    row_v[...] = jnp.zeros_like(row_v)
    load_gain.wait()
    row_v[:, :dm] = line_v[...].astype(F32).reshape(1, dm)
    gain_v[...] = jnp.transpose(jnp.broadcast_to(row_v[...], (LANES, fold.dp)))
    own_ids.wait()
    with jax.named_scope('barrier'):
        ring.meet()

    def start(copy, after=None):
        if after is not None:
            after.wait_send()
            sent[:] = [other for other in sent if other is not after]
        copy.start()
        sent.append(copy)
        return copy

    blocks = []
    for j in range(each):
        b = ring.g * each + j
        blocks.append((lax.rem(b, PAIR), pl.ds(pl.multiple_of(height * (b // 2), BLOCK), height)))

    def hops(k):
        return [
            remote(
                w_v.at[blocks[j][0], slot[-k * sign], blocks[j][1]],
                w_v.at[blocks[j][0], slot[-(k + 1) * sign], blocks[j][1]],
                bs_sem.at[side, j, k % 2], br_sem.at[side, j, k], ring.dev(sign),
            )
            for j in range(each) for side, sign in sides if k < half - 1 or side == j % 2
        ]

    def hop_before(k):
        keep = [k < half - 1 or side == j % 2 for j in range(each) for side, _ in sides]
        return [copy for copy, use in zip(block_moves[k - 2], keep) if use]

    stages = ((nz - 3, nz - 1), (nz - 5, nz - 3), (0, nz - 5))

    def twins(stage):
        lo, hi = stages[stage]
        return [
            remote(
                w_v.at[w, pl.ds(lo, hi - lo), at], w_v.at[w, pl.ds(lo, hi - lo), at],
                ts_sem.at[stage % 2, j, e - 1], tr_sem.at[stage, j, e - 1], ring.twin(e),
            )
            for j, (w, at) in enumerate(blocks) for e in range(1, groups)
        ]

    block_moves = [hops(k) for k in range(half)]
    twin_moves = [twins(stage) for stage in range(len(stages))]

    def relay(k, stage):
        with jax.named_scope(f'relay{k}'):
            for copy in block_moves[k]:
                copy.wait_recv()
            if k + 1 < half:
                earlier = hop_before(k + 1) if k >= 1 else [None] * len(block_moves[1])
                for copy, after in zip(block_moves[k + 1], earlier):
                    start(copy, after)
            if stage is not None:
                earlier = twin_moves[stage - 2] if stage >= 2 else [None] * len(twin_moves[stage])
                for copy, after in zip(twin_moves[stage], earlier):
                    start(copy, after)

    def from_twins(stage):
        with jax.named_scope(f'twins{stage}'):
            for copy in twin_moves[stage]:
                copy.wait_recv()

    for copy in block_moves[0]:
        start(copy)
    swap_ids = start(remote(ids_v.at[c], ids_v.at[c], ps_sem.at[0], pr_sem.at[0], ring.sibling))
    moves = [[], []]
    for side, sign in sides:
        for i, (w, k) in enumerate(gather_messages(half)[side]):
            src, dst = w_v.at[w, slot[-k * sign], ring_rows], w_v.at[w, slot[-(k + 1) * sign], ring_rows]
            moves[side].append(fold.send(src, dst, gh, ws_sem.at[side, i % 2], wr_sem.at[side, i], ring.dev(sign)))
    def forward(i):
        with jax.named_scope(f'fwd{i}'):
            for side, sign in sides:
                moves[side][i].wait_recv()
                if i + 2 < len(moves[side]):
                    start(moves[side][i + 2], moves[side][i])
                w, k = gather_messages(half)[side][i]
                fold.unfold(w_v.at[w, slot[-(k + 1) * sign], ring_rows], gh)

    with jax.named_scope('ids_wait'):
        swap_ids.wait_recv()
    ids = jnp.concatenate([ids_v[0], ids_v[1]], axis=1).astype(F32)
    ids_t = jnp.transpose(jnp.broadcast_to(ids, (LANES, tp)))
    seen = jnp.zeros((1, tp), F32)
    total = jnp.zeros((1, tp), F32)
    for i in range(tp // LANES):
        tri = flags(earlier_than(LANES, tp, i * LANES))
        same = flags(ids_t[rows_at(i), :1] == ids)
        seen = jnp.maximum(seen, over_rows(jnp.max, same * tri))
        total = total + over_rows(jnp.sum, same)
    row = down(n)
    place = lax.rem(row, nz)
    chip = lax.rem(z + half + (1 - 2 * lax.rem(place, 2)) * ((place + 1) // 2), nz)
    owner = 2 * chip + jnp.where(row < nz, c, 1 - c)
    base = (owner * vocab).astype(F32)
    member = flags((seen < 0.5) & (ids >= base) & (ids < base + vocab))
    multi = flags(total > 1.5)
    several, single = member * multi, member * (1.0 - multi)
    both = jnp.concatenate([several, single], axis=0).astype(BF16)
    rank = jnp.dot(both, tri_v[...], preferred_element_type=F32)
    n_several = over_lanes(jnp.sum, several)
    count = n_several + over_lanes(jnp.sum, single)
    rank = jnp.where(several > 0.5, rank[:n], n_several + rank[n:])
    over = over_rows(jnp.max, flags((count > CAP) | (n_several > MULTI)))
    for k in range(n):
        hit = (rank[k:k + 1, :] == down(CAP).astype(F32)) & (member[k:k + 1, :] > 0.5)
        col = over_lanes(jnp.max, jnp.where(hit, ids, -1.0))
        col_v[k * CAP:(k + 1) * CAP, :] = jnp.broadcast_to(col, (CAP, LANES))
    cols_t = jnp.transpose(col_v[:slots, :])
    lane = iota((8, LANES), 1)
    per = LANES // CAP
    for k in range(nz):
        at = (k // per) * LANES
        tile = cols_t[0:8, at:at + LANES]
        if k % per:
            tile = pltpu.roll(tile, LANES - (k % per) * CAP, 1)
        req_s[k] = jnp.where(lane < CAP, tile, over)
    asks = []
    for p, d in enumerate(order[:-1]):
        asks.append(start(remote(req_s.at[p], req_r.at[back[p]], qs_sem.at[p], qr_sem.at[p], ring.dev(d))))
    relay(0, 0)
    for i in range(PAIR):
        for side, _ in sides:
            start(moves[side][i])
    swap_grad = start(remote(grad_ref, gn_v.at[1, c], ps_sem.at[1], pr_sem.at[1], ring.sibling))
    req_r[nz - 1] = req_s[nz - 1]
    for q in range(PAIR):
        for t in range(PAIR):
            pick_v[q, t] = one_hot(col_v[q * slots:(q + 1) * slots, :1] == ids[:, t * tl:(t + 1) * tl])

    with jax.named_scope('asks_wait'):
        for copy in asks:
            copy.wait_recv()
    flag = req_r[0]
    for k in range(1, nz):
        flag = jnp.maximum(flag, req_r[k])
    flag_v[...] = over_rows(jnp.max, over_lanes(jnp.max, jnp.where(lane < CAP, 0.0, flag)))
    keeps = [pltpu.make_async_copy(flag_v, flag_ref, out_sem.at[2])]
    keeps[0].start()
    tiles = []
    for p in range(nz // per):
        tile = req_r[p * per]
        for j in range(1, per):
            tile = jnp.where(lane < j * CAP, tile, pltpu.roll(req_r[p * per + j], j * CAP, 1))
        tiles.append(tile)
    names = jnp.concatenate(tiles, axis=1) - (ring.me * vocab).astype(F32)
    nrow_v[...] = names
    name_v[...] = jnp.transpose(jnp.broadcast_to(names[0:1, :], (LANES, slots)))
    gives = []

    def find(part):
        cols = slice(part * slots // 2, (part + 1) * slots // 2)
        found_v[...] = jnp.zeros_like(found_v)

        def body(i, carry):
            if part == 0:
                load_emb(i).wait()
            hot = one_hot(down(step, i * step).astype(F32) == nrow_v[:1, cols])
            found_v[:dm, :] = found_v[:dm, :] + jnp.dot(emb_v[i], hot, preferred_element_type=F32)
            return carry

        with jax.named_scope(f'find{part}'):
            lax.fori_loop(0, vocab // step, body, 0)
        found = jnp.transpose(found_v[...])[:, :dm].astype(BF16)
        for q in range(nz // 2):
            fold.store(xs_v.at[part * nz // 2 + q], found[q * CAP:(q + 1) * CAP, :], xh)

    def hand(p):
        return fold.send(xr_v.at[p], xo_v.at[p], xh, xf_sem.at[p], xg_sem.at[p], ring.sibling)

    def give(part):
        for p in range(part * nz // 2, (part + 1) * nz // 2):
            if order[p]:
                to = ring.dev(order[p])
                give_row = fold.send(xs_v.at[p], xr_v.at[back[p]], xh, qs_sem.at[p], xr_sem.at[p], to)
                gives.append(start(give_row, asks[p]))

    relay(1, 1)
    find(0)
    relay(2, None)
    forward(0)
    give(0)
    find(1)
    forward(1)
    give(1)
    xr_v[nz - 1] = xs_v[nz - 1]
    handed = {nz - 1: start(hand(nz - 1))}
    relay(3, 2)
    forward(2)

    with jax.named_scope('gives_wait'):
        for p in range(nz - 1):
            gives[p].wait_recv()
            handed[back[p]] = start(hand(back[p]))
    forward(3)

    def unpack(rows_of, q):
        for p in range(nz):
            fold.unfold(rows_of.at[p], xh)
        rows = rows_of[...].reshape(slots, fold.dp)[:, :dm]
        return [first_first(rows, pick_v[q, t]).astype(BF16) for t in range(PAIR)]

    for t, part in enumerate(unpack(xr_v, 0)):
        x_v[t] = part
    forward(4)
    load_grad.wait()
    swap_grad.wait_recv()
    with jax.named_scope('sibling_wait'):
        for copy in handed.values():
            copy.wait_recv()
    for t, part in enumerate(unpack(xo_v, 1)):
        x_v[t] = x_v[t] + part

    def lanes(b):
        return pl.ds(pl.multiple_of(b * LANES, LANES), LANES)

    def norm(i, carry):
        t, at = i // (tl // LANES), lanes(lax.rem(i, tl // LANES))
        xf = x_v[t, :, at].astype(F32)
        inv = lax.rsqrt(over_rows(jnp.mean, xf * xf) + EPS)
        gn_v[0, t, :, at] = (xf * inv * gain_v[:dm, :]).astype(BF16)
        return carry

    lax.fori_loop(0, tp // LANES, norm, 0)

    def hidden(lo, hi):
        def body(i, carry):
            s, t = lo + i // 2, lax.rem(i, PAIR)
            u = jnp.dot(w_v[0, s, :, :dm], gn_v[0, t], preferred_element_type=F32).astype(BF16).astype(F32)
            dh = jnp.dot(w_v[1, s, :, :dm], gn_v[1, t], preferred_element_type=F32)
            act, slope = gelu_pair(u)
            at = pl.ds(pl.multiple_of(s * fl, fl), fl)
            hd_v[1, t, at, :] = act.astype(BF16)
            hd_v[0, t, at, :] = (dh * slope).astype(BF16)
            return carry

        with jax.named_scope(f'hid{lo}'):
            lax.fori_loop(0, 2 * (hi - lo), body, 0)

    def grad_w(w, s):
        at = pl.ds(pl.multiple_of(s * fl, fl), fl)
        return last_last(hd_v[w, 0, at, :], gn_v[w, 0]) + last_last(hd_v[w, 1, at, :], gn_v[w, 1])

    orders = scatter_messages(half)
    sends = [[], []]
    for side, sign in sides:
        for i in range(len(orders[0])):
            src = st_v.at[side, i] if i < 2 else rb_v.at[side, i - 2]
            dst = rb_v.at[side, i]
            sends[side].append(fold.send(src, dst, wh, ss_sem.at[side, i % 2], sr_sem.at[side, i], ring.dev(sign)))

    def scatter(i):
        with jax.named_scope(f'scat{i}'):
            (w0, k0), (_, k1) = orders[0][i], orders[1][i]
            if i >= 2:
                for side, _ in sides:
                    sends[side][i - 2].wait_recv()

            def body(side, carry):
                w = w0 + side * (1 - 2 * w0)
                part = grad_w(w, slot[k0] + side * (slot[k1] - slot[k0]))
                if i < 2:
                    fold.store(st_v.at[side, i], part, wh)
                else:
                    fold.add(rb_v.at[side, i - 2], part, wh)
                return carry

            if i:
                lax.fori_loop(0, 2, body, 0)
            for side, _ in sides:
                if i == 0:
                    body(side, 0)
                start(sends[side][i], sends[side][i - 2] if i >= 2 else None)

    forward(5)
    forward(6)
    for stage in range(len(stages)):
        from_twins(stage)
    hidden(0, 1)
    scatter(0)
    hidden(1, nz - 5)
    scatter(1)
    hidden(nz - 5, nz)

    wide = 2 * LANES

    def through(w, t, dst):
        def body(b, carry):
            at = pl.ds(pl.multiple_of(b * wide, wide), wide)
            left = w_v[w, :, :, at].reshape(nz * fl, wide)
            dst[at, :] = first_first(left, hd_v[w_of_hd[w], t])
            return carry

        lax.fori_loop(0, fold.dp // wide, body, 0)

    w_of_hd = (0, 1)
    with jax.named_scope('thru'):
        through(0, 1 - c, snd_v)
    body_rows = pl.ds(0, dm)
    swap_dn = remote(snd_v.at[body_rows], dnr_v, ps_sem.at[2], pr_sem.at[2], ring.sibling)
    swap_dn.start()
    through(0, c, own_v)
    with jax.named_scope('swapdn_wait'):
        swap_dn.wait_send()
        swap_dn.wait_recv()

    def dx_block(b, carry):
        at = lanes(b)
        xf = x_v[c, :, at].astype(F32)
        inv = lax.rsqrt(over_rows(jnp.mean, xf * xf) + EPS)
        q = (own_v[:dm, at] + dnr_v[:, at]) * gain_v[:dm, :]
        dot = over_rows(jnp.mean, xf * q)
        dxn = inv * q - xf * (inv * inv * inv * dot)
        dx_v[c, :, at] = (gn_v[1, c, :, at].astype(F32) + dxn).astype(BF16)
        return carry

    lax.fori_loop(0, tl // LANES, dx_block, 0)
    swap_dx = start(remote(dx_v.at[c], dx_v.at[c], ps_sem.at[3], pr_sem.at[3], ring.sibling))
    through(1, 1 - c, snd_v)
    swap_y = start(remote(snd_v.at[body_rows], yr_v, ps_sem.at[4], pr_sem.at[4], ring.sibling))
    with jax.named_scope('swapdx_wait'):
        swap_dx.wait_recv()

    def pack(k, carry):
        at = pl.ds(pl.multiple_of(k * CAP, CAP), CAP)
        rows = last_last(pick_v[0, 0, at, :], dx_v[0]) + last_last(pick_v[0, 1, at, :], dx_v[1])
        fold.store(es_v.at[k], rows[:MULTI], eh)
        fold.store(eb_v.at[k], rows[MULTI:].astype(BF16), bh)
        return carry

    lax.fori_loop(0, nz, pack, 0)
    backs = []
    for p, d in enumerate(order[:-1]):
        to, q = ring.dev(d), back[p]
        backs.append(start(fold.send(es_v.at[p], er_v.at[q], eh, qs_sem.at[p], er_sem.at[0, p], to), gives[p]))
        backs.append(start(fold.send(eb_v.at[p], eq_v.at[q], bh, xf_sem.at[p], er_sem.at[1, p], to), handed[p]))
    er_v[nz - 1] = es_v[nz - 1]
    eq_v[nz - 1] = eb_v[nz - 1]
    scatter(2)
    through(1, c, own_v)
    scatter(3)
    with jax.named_scope('swapy_wait'):
        swap_y.wait_recv()

    def out_block(b, carry):
        at = lanes(b)
        out_v[:, at] = (x_v[c, :, at].astype(F32) + (own_v[:dm, at] + yr_v[:, at])).astype(BF16)
        return carry

    lax.fori_loop(0, tl // LANES, out_block, 0)
    keeps.append(pltpu.make_async_copy(out_v, out_ref, out_sem.at[0]))
    keeps[-1].start()
    last = len(orders[0])
    for i in range(4, last):
        scatter(i)

    with jax.named_scope('backs_wait'):
        for copy in backs:
            copy.wait_recv()
    lots, rest = nz * MULTI, CAP - MULTI

    def spread(k, carry):
        fold.unfold(er_v.at[k], eh)
        fold.unfold(eq_v.at[k], bh)
        rows = er_v[k, :, :dm]
        head = name_v[pl.ds(pl.multiple_of(k * CAP, CAP), MULTI), :]
        for p in range(3):
            at = pl.ds(pl.multiple_of(p * lots + k * MULTI, MULTI), MULTI)
            piece = rows.astype(BF16)
            rows_v[at, :] = piece
            names_v[at, :] = head
            rows = rows - piece.astype(F32)
        at = pl.ds(pl.multiple_of(3 * lots + k * rest, 16), rest)
        rows_v[at, :] = eq_v[k, :, :dm]
        names_v[at, :] = name_v[pl.ds(pl.multiple_of(k * CAP + MULTI, 16), rest), :]
        return carry

    lax.fori_loop(0, nz, spread, 0)

    parts = rows_v.shape[0]
    key = jnp.where(names_v[...] < 0.0, 2.0 * vocab, names_v[...])
    names_v[...] = key
    key = jnp.transpose(key)[0:1, :]
    rank_row = jnp.zeros((1, parts), F32)
    for i in range(parts // LANES):
        col = names_v[rows_at(i), :1]
        ahead = (col < key) | ((col == key) & earlier_than(LANES, parts, i * LANES))
        rank_row = rank_row + over_rows(jnp.sum, flags(ahead))
    for i in range(parts // LANES):
        hit = down(LANES, i * LANES).astype(F32) == rank_row
        tri_v[rows_at(i), :dm] = jnp.dot(one_hot(hit), rows_v[...], preferred_element_type=F32).astype(BF16)
        name = over_lanes(jnp.sum, jnp.where(hit, key, 0.0))
        names_v[rows_at(i), :] = jnp.broadcast_to(name, (LANES, LANES))
    which = across(LANES)
    bounds = jnp.zeros((1, LANES), F32)
    for b in range(PLACE_GRID + 1):
        before = over_lanes(jnp.sum, flags(key < b * (vocab // PLACE_GRID)))
        bounds = jnp.where(which == b, before, bounds)
    bounds_v[...] = bounds.astype(jnp.int32)
    for j, (src, dst) in enumerate(((tri_v.at[pl.ds(0, parts), pl.ds(0, fold.dp)], rows_ref), (names_v, names_ref), (bounds_v, bounds_ref))):
        keeps.append(pltpu.make_async_copy(src, dst, out_sem.at[3 + j]))
        keeps[-1].start()

    for w in range(PAIR):
        a, b = (last - 1, last - 2) if w == 0 else (last - 2, last - 1)
        part = grad_w(w, mine)
        with jax.named_scope(f'fin{w}'):
            sends[0][a].wait_recv()
            sends[1][b].wait_recv()
        rb_v[0, a] = rb_v[0, a] + rb_v[1, b]
        fold.unfold(rb_v.at[0, a], wh)
        dw_v[w] = rb_v[0, a, :, :dm] + part
        keeps.append(pltpu.make_async_copy(dw_v.at[w], (dup_ref, ddown_ref)[w], out_sem.at[6 + w]))
        keeps[-1].start()
    with jax.named_scope('exit_sends'):
        for copy in sent:
            copy.wait_send()
    with jax.named_scope('exit_keeps'):
        for copy in keeps:
            copy.wait()


def step(n, groups, ids, emb_t, up, down, grad_t, gain):
    nz = n // 2
    dm, vocab = emb_t.shape
    tl, fl = ids.shape[1], up.shape[0]
    tp = 2 * tl
    dp = Fold(dm).dp
    slots = nz * CAP
    parts = slots + 2 * nz * MULTI
    assert max(parts, dp) <= tp
    hops = nz - 1
    each, _, _ = shared_blocks(fl, groups)
    vmem, hbm = pl.BlockSpec(memory_space=pltpu.VMEM), pl.BlockSpec(memory_space=pl.ANY)
    dma = pltpu.SemaphoreType.DMA
    tokens = pltpu.VMEM((PAIR, dm, tl), BF16)
    return pl.pallas_call(
        functools.partial(step_kernel, n, groups),
        name='step',
        out_shape=(
            jax.ShapeDtypeStruct((dm, tl), BF16),
            jax.ShapeDtypeStruct((fl, dm), F32),
            jax.ShapeDtypeStruct((fl, dm), F32),
            jax.ShapeDtypeStruct((parts, dp), BF16),
            jax.ShapeDtypeStruct((parts, LANES), F32),
            jax.ShapeDtypeStruct((1, LANES), jnp.int32),
            jax.ShapeDtypeStruct((1, 1), F32),
        ),
        in_specs=[hbm] * 6,
        out_specs=(hbm,) * 7,
        scratch_shapes=[
            pltpu.VMEM((PAIR, nz, fl, dp), BF16),
            pltpu.VMEM((PAIR, PAIR, dm, tl), BF16),
            tokens,
            pltpu.VMEM((PAIR, PAIR, nz * fl, tl), BF16),
            pltpu.VMEM((PAIR, PAIR, fl, dp), F32),
            pltpu.VMEM((PAIR, hops, fl, dp), F32),
            pltpu.VMEM((dp, tl), F32),
            pltpu.VMEM((dp, tl), F32),
            pltpu.VMEM((dm, tl), F32),
            pltpu.VMEM((dm, tl), F32),
            tokens,
            pltpu.VMEM((nz, MULTI, dp), F32),
            pltpu.VMEM((nz, MULTI, dp), F32),
            pltpu.VMEM((nz, CAP - MULTI, dp), BF16),
            pltpu.VMEM((nz, CAP - MULTI, dp), BF16),
            pltpu.VMEM((nz, CAP, dp), BF16),
            pltpu.VMEM((nz, CAP, dp), BF16),
            pltpu.VMEM((PAIR, PAIR, slots, tl), BF16),
            pltpu.VMEM((tp, tp), BF16),
            pltpu.VMEM((PAIR, 1, tl), jnp.int32),
            pltpu.VMEM((2 * slots, LANES), F32),
            pltpu.VMEM((slots, LANES), F32),
            pltpu.VMEM((8, slots), F32),
            pltpu.VMEM((nz, 8, LANES), F32),
            pltpu.VMEM((nz, 8, LANES), F32),
            pltpu.VMEM((vocab // 512, dm, 512), BF16),
            pltpu.VMEM((dp, slots // 2), F32),
            pltpu.VMEM((dm, tl), BF16),
            pltpu.VMEM((parts, dm), BF16),
            pltpu.VMEM((1, dp), F32),
            pltpu.VMEM((dp, LANES), F32),
            pltpu.VMEM((PAIR, fl, dm), BF16),
            pltpu.VMEM((dm,), BF16),
            pltpu.VMEM((1, 1), F32),
            pltpu.VMEM((parts, LANES), F32),
            pltpu.VMEM((1, LANES), jnp.int32),
            pltpu.VMEM((PAIR, fl, dm), F32),
            pltpu.VMEM((nz, CAP, dp), BF16),
            dma((nz,)), dma((nz,)),
            dma((5,)), dma((vocab // 512,)), dma((PAIR, PAIR)), dma((PAIR, hops)),
            dma((PAIR, each, 2)), dma((PAIR, each, nz // 2)), dma((PAIR, each, groups - 1)), dma((3, each, groups - 1)),
            dma((5,)), dma((5,)), dma((hops,)), dma((hops,)), dma((hops,)),
            dma((PAIR, PAIR)), dma((PAIR, hops)), dma((PAIR, hops)), dma((9,)),
        ],
        compiler_params=pltpu.CompilerParams(
            collective_id=0, has_side_effects=True, vmem_limit_bytes=VMEM_LIMIT
        ),
    )(ids, emb_t, up, down, grad_t, gain)


def place_kernel(
    bounds_ref, names_hbm, rows_hbm, out_ref, up_ref, down_ref, emb_out, out_out, up_out, down_out,
    names_v, rows_v, emb_v, out_v, up_v, down_v, in_sem, emb_sem, out_sem,
):
    def load(i, src, dst):
        copy = pltpu.make_async_copy(src, dst, in_sem.at[i])
        copy.start()
        return copy

    needed = [load(0, names_hbm, names_v), load(1, rows_hbm, rows_v)]
    passing = ((out_ref, out_v, out_out), (up_ref, up_v, up_out), (down_ref, down_v, down_out))
    loads = [load(2 + j, src, via) for j, (src, via, _) in enumerate(passing)]
    dm, vocab = emb_v.shape
    block = vocab // PLACE_GRID
    last = rows_v.shape[0] // PLACE_ROWS - 1
    for copy in needed:
        copy.wait()

    def store(i):
        at = pl.ds(pl.multiple_of(i * block, LANES), block)
        return pltpu.make_async_copy(emb_v.at[:, at], emb_out.at[:, at], emb_sem.at[i])

    def fill(i, carry):
        to = pl.ds(pl.multiple_of(i * block, LANES), block)
        lo = jnp.minimum(bounds_ref[0, i] // PLACE_ROWS, last)
        hi = (bounds_ref[0, i + 1] + PLACE_ROWS - 1) // PLACE_ROWS

        def part(q):
            at = pl.ds(pl.multiple_of(q * PLACE_ROWS, PLACE_ROWS), PLACE_ROWS)
            return first_first(rows_v[at, :dm], one_hot(names_v[at, :1] == across(block, i * block).astype(F32)))

        emb_v[:, to] = part(lo)

        def more(q, inner):
            emb_v[:, to] = emb_v[:, to] + part(q)
            return inner

        lax.fori_loop(lo + 1, hi, more, 0)
        store(i).start()
        return carry

    lax.fori_loop(0, PLACE_GRID, fill, 0)
    keeps = []
    for j, (_, via, dst) in enumerate(passing):
        loads[j].wait()
        keeps.append(pltpu.make_async_copy(via, dst, out_sem.at[j]))
        keeps[-1].start()
    for i in range(PLACE_GRID):
        store(i).wait()
    for copy in keeps:
        copy.wait()


def place(vocab, bounds, names, rows, out, d_up, d_down):
    hbm = pl.BlockSpec(memory_space=pl.ANY)
    emb = jax.ShapeDtypeStruct((out.shape[0], vocab), F32)
    results = (emb,) + tuple(jax.ShapeDtypeStruct(a.shape, a.dtype) for a in (out, d_up, d_down))
    dma = pltpu.SemaphoreType.DMA
    return pl.pallas_call(
        place_kernel,
        name='place',
        out_shape=results,
        in_specs=[pl.BlockSpec(memory_space=pltpu.SMEM)] + [hbm] * 5,
        out_specs=(hbm,) * 4,
        scratch_shapes=[pltpu.VMEM(a.shape, a.dtype) for a in (names, rows) + results]
        + [dma((5,)), dma((PLACE_GRID,)), dma((3,))],
        compiler_params=pltpu.CompilerParams(vmem_limit_bytes=VMEM_LIMIT),
    )(bounds, names, rows, out, d_up, d_down)


def swap_kernel(n, src_ref, dst_ref, keep_sem, send_sem, recv_sem):
    me = lax.axis_index('tensor')
    sem = pltpu.get_barrier_semaphore()
    for d in range(1, n):
        pl.semaphore_signal(sem, device_id={'tensor': lax.rem(me + d, n)}, device_id_type=MESH)
    pl.semaphore_wait(sem, n - 1)
    keep = pltpu.make_async_copy(src_ref.at[me], dst_ref.at[me], keep_sem)
    keep.start()
    copies = []
    for d in range(1, n):
        to = lax.rem(me + d, n)
        copies.append(remote(src_ref.at[to], dst_ref.at[me], send_sem.at[d], recv_sem.at[d], {'tensor': to}))
        copies[-1].start()
    for copy in copies:
        copy.wait()
    keep.wait()


def swap_blocks(n, blocks, collective_id):
    hbm = pl.BlockSpec(memory_space=pl.ANY)
    return pl.pallas_call(
        functools.partial(swap_kernel, n),
        name='swap_blocks',
        out_shape=jax.ShapeDtypeStruct(blocks.shape, blocks.dtype),
        in_specs=[hbm],
        out_specs=hbm,
        scratch_shapes=[pltpu.SemaphoreType.DMA, pltpu.SemaphoreType.DMA((n,)), pltpu.SemaphoreType.DMA((n,))],
        compiler_params=pltpu.CompilerParams(collective_id=collective_id, has_side_effects=True),
    )(blocks)


def all_blocks(n, block, collective_id):
    return swap_blocks(n, jnp.broadcast_to(block[None], (n,) + block.shape), collective_id)


def rms_norm(x_rows, gain_f):
    inv_rms = lax.rsqrt(jnp.mean(x_rows * x_rows, axis=-1, keepdims=True) + EPS)
    return x_rows * inv_rms * gain_f


def dense_step(n, ids, emb, norm_gain, up, down, grad_out):
    vocab, dm = emb.shape
    fl = up.shape[0]
    base = (lax.axis_index('tensor') * vocab).astype(F32)
    ids_all = all_blocks(n, jnp.broadcast_to(ids.astype(F32), (8, ids.shape[1])), 1)[:, 0]
    hot = (iota((ids_all.size, vocab), 1).astype(F32) == ids_all.reshape(-1, 1) - base).astype(BF16)
    part = jnp.dot(hot, emb, preferred_element_type=F32).astype(BF16)
    x_f = jnp.sum(swap_blocks(n, part.reshape(n, -1, dm), 2).astype(F32), axis=0)
    ws = all_blocks(n, jnp.stack([up, down]), 3)
    up_all, down_all = ws[:, 0].reshape(-1, dm), ws[:, 1].reshape(-1, dm)
    normed_f, norm_back = jax.vjp(lambda x_in: rms_norm(x_in, norm_gain.astype(F32)), x_f)
    normed = normed_f.astype(BF16)
    pre_act = last_last(normed, up_all).astype(BF16).astype(F32)
    act_f, slope = gelu_pair(pre_act)
    hidden = act_f.astype(BF16)
    d_pre = (last_last(grad_out, down_all) * slope).astype(BF16)
    y = jnp.dot(hidden, down_all, preferred_element_type=F32)
    out = (x_f + y).astype(BF16)
    d_norm = jnp.dot(d_pre, up_all, preferred_element_type=F32)
    dx = (grad_out.astype(F32) + norm_back(d_norm)[0]).astype(BF16)
    d_w = jnp.stack([first_first(d_pre, normed), first_first(hidden, grad_out)]).reshape(PAIR, n, fl, dm)
    d_w = jnp.sum(swap_blocks(n, jnp.moveaxis(d_w, 1, 0), 4), axis=0)
    dx_all = all_blocks(n, dx, 5).reshape(-1, dm)
    hot_t = (iota((vocab, ids_all.size), 0).astype(F32) == ids_all.reshape(1, -1) - base).astype(BF16)
    d_emb = jnp.dot(hot_t, dx_all, preferred_element_type=F32)
    return d_emb.T, out.T, d_w[0], d_w[1]


def solution(mesh):
    n, groups = mesh.shape['tensor'], mesh.shape['data']
    tok_spec = P(('data', 'tensor'))
    row_spec = P(('data', 'tensor'), None)

    def local_step(token_ids, emb_shard, norm_gain, w_up, w_down, grad_out):
        vocab, dm = emb_shard.shape
        ids, gain, up = token_ids[None, :], norm_gain, w_up.T
        out, d_up, d_down, rows, names, bounds, flag = step(n, groups, ids, emb_shard.T, up, w_down, grad_out.T, gain)
        placed = place(vocab, bounds, names, rows, out, d_up, d_down)

        def again(state):
            return (jnp.zeros((), F32),) + dense_step(n, ids, emb_shard, norm_gain, up, w_down, grad_out)

        state = lax.while_loop(lambda state: state[0] > 0.5, again, (flag[0, 0],) + tuple(placed))
        _, d_emb, out, d_up, d_down = state
        return out.T, d_emb.T, d_up.T, d_down

    return jax.shard_map(
        local_step,
        mesh=mesh,
        in_specs=(tok_spec, P('tensor', None), P(None), P(None, 'tensor'), P('tensor', None), row_spec),
        out_specs=(row_spec, row_spec, P('data', 'tensor'), row_spec),
        check_vma=False,
    )
```

time: 204 us -> 193 us (0.946)
  Pallas kernels: 202 us -> 191 us
    pallas_call x1, Pallas kernels: 192 us -> 183 us  [step(): pl.pallas_call(functools.partial(step_kernel, n, groups), name='step', ou...]
where the time goes in v5:
time: 193 us
  Pallas kernels  191 us (99%)
    pallas_call x1, Pallas kernels, step(): pl.pallas_call(functools.partial(step_kernel, n, groups), name='step', ou...  183 us
    pallas_call x1, Pallas kernels, place(): pl.pallas_call(place_kernel, name='place', out_shape=results, in_specs=[p...  8.27 us

profile of v5, /device:TPU:21, one launch (start us, length us, event | category | flops | bytes accessed | tf_op | source)
XLA Modules:
  0.0 192.8 jit_solution(12066534927688761701)
XLA Ops:
  0.6 0.0 copy-start.4
  0.6 0.0 copy-start.6
  0.7 182.7 %step.1 = (bf16[960,512]{1,0:T(8,128)(2,1)}, f32[160,960]{1,0:T(8,128)}, f32[160,960]{1,0:T(8,128)}, bf16[768,1024]{1,0:T(8,128)(2,1)}, f32[768,128]{1,0:T(8,128)}, /*index=5*/s32[1,128]{1,0:T(1,128)}, f32[1,1]{1,0:T(1,128)}) custom-call(s32[1,512]{1,0:T(1,128)} %bitcast.63, bf16[960,3072]{1,0:T(8,128)(2,1)} %bitcast.59, bf16[160,960]{1,0:T(8,128)(2,1)} %bitcast.55, ...), custom_call_target="tpu_custom_call" | custom-call | tf_op jit(solution)/shard_map/step/pallas_call | solution.py:702
  183.3 8.3 %place.1 = (f32[960,3072]{1,0:T(8,128)}, bf16[960,512]{1,0:T(8,128)(2,1)}, f32[160,960]{1,0:T(8,128)}, f32[160,960]{1,0:T(8,128)}) custom-call(s32[1,128]{1,0:T(1,128)} %get-tuple-element.71.bounds_ref, f32[768,128]{1,0:T(8,128)} %get-tuple-element.72.names_hbm, bf16[768,1024]{1,0:T(8,128)(2,1)} %get-tuple-element.73.rows_hbm, ...), custom_call_target="tpu_custom_call" | custom-call | tf_op jit(solution)/shard_map/place/pallas_call | solution.py:825
  191.6 0.0 copy-done.4
  191.6 0.0 copy-done.6
  191.6 0.9 while.15
Async XLA Ops:
  0.6 191.0 %copy-start.4 = (bf16[960]{0:T(1024)(128)(2,1)S(1)}, bf16[960]{0:T(1024)(128)(2,1)}, u32[]{:S(2)}) copy-start(bf16[960]{0:T(1024)(128)(2,1)} %gain_ref.1) | copy-start | bytes 5764
  0.6 191.0 %copy-start.6 = (s32[512]{0:T(512)S(1)}, s32[512]{0:T(512)}, u32[]{:S(2)}) copy-start(s32[512]{0:T(512)} %param.8) | copy-start | bytes 6148

commit v6 on v5

--- a/solution.py
+++ b/solution.py
@@ -1,4 +1,5 @@
 import functools
+import math
 
 import jax
 import jax.numpy as jnp
@@ -137,7 +138,9 @@
 
 
 def far_first(nz):
-    return [(nz // 2 + (-1) ** r * ((r + 1) // 2)) % nz for r in range(nz)]
+    half = nz // 2
+    far = [half] + [half + s * k for k in range(1, half) for s in (-1, 1)]
+    return far[:half - 1] + [0] + far[half - 1:]
 
 
 def scatter_messages(half):
@@ -180,21 +183,26 @@
         low = ref.shape[0] - h
         ref[h:, self.lo:self.dm] = ref[:low, self.dm:self.dp]
 
+    def parts(self, src, dst, h, device):
+        low = src.shape[0] - h
+        areas = ((pl.ds(0, h), pl.ds(0, self.dp)), (pl.ds(h, low), pl.ds(0, self.lo)))
+        return [(src.at[area], dst.at[area], device) for area in areas]
+
     def send(self, src, dst, h, send_sem, recv_sem, device):
-        return FoldCopy(self, src, dst, h, send_sem, recv_sem, device, self.spare[jnp.dtype(src.dtype)])
-
-
-class FoldCopy:
-    def __init__(self, fold, src, dst, h, send_sem, recv_sem, device, spare):
-        low = src.shape[0] - h
-        parts = ((pl.ds(0, h), pl.ds(0, fold.dp)), (pl.ds(h, low), pl.ds(0, fold.lo)))
-        self.copies = [remote(src.at[r, l], dst.at[r, l], send_sem, recv_sem, device) for r, l in parts]
-        size = h * fold.dp + low * fold.lo
-        tile = 16 if jnp.dtype(spare.dtype) == jnp.dtype(BF16) else 8
-        width = next(w for w in range(LANES, spare.shape[1] + 1, LANES)
-                     if size % (w * tile) == 0 and size // w <= spare.shape[0])
-        whole = spare.at[pl.ds(0, size // width), pl.ds(0, width)]
-        self.whole = remote(whole, whole, send_sem, recv_sem, device)
+        return Batch(self.parts(src, dst, h, device), self.spare, send_sem, recv_sem)
+
+
+class Batch:
+    def __init__(self, parts, spare, send_sem, recv_sem):
+        self.copies = [remote(src, dst, send_sem, recv_sem, device) for src, dst, device in parts]
+        dtype = jnp.dtype(parts[0][0].dtype)
+        size = sum(math.prod(src.shape) for src, _, _ in parts)
+        ref = spare[dtype]
+        tile = 8 * 4 // dtype.itemsize
+        width = next(w for w in range(LANES, ref.shape[1] + 1, LANES)
+                     if size % (w * tile) == 0 and size // w <= ref.shape[0])
+        whole = ref.at[pl.ds(0, size // width), pl.ds(0, width)]
+        self.whole = remote(whole, whole, send_sem, recv_sem, parts[0][2])
 
     def start(self):
         for copy in self.copies:
@@ -213,8 +221,8 @@
     w_v, gn_v, x_v, hd_v, st_v, rb_v, snd_v, own_v, dnr_v, yr_v, dx_v, es_v, er_v, eb_v, eq_v, xs_v, xr_v,
     pick_v, tri_v, ids_v, col_v, name_v, nrow_v, req_s, req_r, emb_v, found_v, out_v, rows_v, row_v, gain_v,
     own_w, line_v, flag_v, names_v, bounds_v, dw_v, xo_v, xf_sem, xg_sem,
-    ld_sem, emb_sem, ws_sem, wr_sem, bs_sem, br_sem, ts_sem, tr_sem, ps_sem, pr_sem, qs_sem, qr_sem, xr_sem,
-    ss_sem, sr_sem, er_sem, out_sem,
+    ld_sem, emb_sem, ws_sem, wr_sem, bs_sem, br_sem, ts_sem, tr_sem, ps_sem, pr_sem, qs_sem, gs_sem, xr_sem,
+    ss_sem, sr_sem, es_sem, er_sem, out_sem,
 ):
     ring = Ring(n, groups)
     nz, half, c, z = ring.nz, ring.half, ring.c, ring.z
@@ -224,11 +232,14 @@
     each, height, shared = shared_blocks(fl, groups)
     order = far_first(nz)
     back = [order.index((nz - d) % nz) for d in order]
+    own = order.index(0)
+    others = [(p, d) for p, d in enumerate(order) if d]
+    part_of = nz // 2
     tl = ids_ref.shape[1]
     tp = 2 * tl
     slots = nz * CAP
     fold = Fold(dm)
-    fold.spare = {jnp.dtype(BF16): gn_v.at[0, 0], jnp.dtype(F32): own_v}
+    fold.spare = {jnp.dtype(BF16): tri_v, jnp.dtype(F32): own_v}
     wh, xh, eh, bh = fl // 2, CAP // 2, MULTI // 2, BHEAD
     gh = (fl - shared) // 2
     ring_rows = pl.ds(shared, fl - shared)
@@ -250,17 +261,11 @@
 
     for i in range(vocab // step):
         load_emb(i).start()
-    for i in range(tp // LANES):
-        tri_v[rows_at(i), :] = one_hot(earlier_than(LANES, tp, i * LANES))
     mine = slot[0]
     for w in range(PAIR):
         load_w[w].wait()
         w_v[w, mine, :, :dm] = own_w[w]
         w_v[w, mine, shared:shared + gh, dm:] = own_w[w, shared + gh:, fold.lo:]
-    row_v[...] = jnp.zeros_like(row_v)
-    load_gain.wait()
-    row_v[:, :dm] = line_v[...].astype(F32).reshape(1, dm)
-    gain_v[...] = jnp.transpose(jnp.broadcast_to(row_v[...], (LANES, fold.dp)))
     own_ids.wait()
     with jax.named_scope('barrier'):
         ring.meet()
@@ -279,60 +284,43 @@
         blocks.append((lax.rem(b, PAIR), pl.ds(pl.multiple_of(height * (b // 2), BLOCK), height)))
 
     def hops(k):
-        return [
-            remote(
-                w_v.at[blocks[j][0], slot[-k * sign], blocks[j][1]],
-                w_v.at[blocks[j][0], slot[-(k + 1) * sign], blocks[j][1]],
-                bs_sem.at[side, j, k % 2], br_sem.at[side, j, k], ring.dev(sign),
-            )
-            for j in range(each) for side, sign in sides if k < half - 1 or side == j % 2
+        parts = [
+            (w_v.at[w, slot[-k * sign], at], w_v.at[w, slot[-(k + 1) * sign], at], ring.dev(sign))
+            for j, (w, at) in enumerate(blocks) for side, sign in sides if k < half - 1 or side == j % 2
         ]
-
-    def hop_before(k):
-        keep = [k < half - 1 or side == j % 2 for j in range(each) for side, _ in sides]
-        return [copy for copy, use in zip(block_moves[k - 2], keep) if use]
+        return Batch(parts, fold.spare, bs_sem.at[k % 2], br_sem.at[k])
 
     stages = ((nz - 3, nz - 1), (nz - 5, nz - 3), (0, nz - 5))
 
     def twins(stage):
         lo, hi = stages[stage]
-        return [
-            remote(
-                w_v.at[w, pl.ds(lo, hi - lo), at], w_v.at[w, pl.ds(lo, hi - lo), at],
-                ts_sem.at[stage % 2, j, e - 1], tr_sem.at[stage, j, e - 1], ring.twin(e),
-            )
-            for j, (w, at) in enumerate(blocks) for e in range(1, groups)
-        ]
+        refs = [w_v.at[w, pl.ds(lo, hi - lo), at] for w, at in blocks]
+        parts = [(ref, ref, ring.twin(e)) for ref in refs for e in range(1, groups)]
+        return Batch(parts, fold.spare, ts_sem.at[stage % 2], tr_sem.at[stage])
 
     block_moves = [hops(k) for k in range(half)]
     twin_moves = [twins(stage) for stage in range(len(stages))]
 
     def relay(k, stage):
         with jax.named_scope(f'relay{k}'):
-            for copy in block_moves[k]:
-                copy.wait_recv()
+            block_moves[k].wait_recv()
             if k + 1 < half:
-                earlier = hop_before(k + 1) if k >= 1 else [None] * len(block_moves[1])
-                for copy, after in zip(block_moves[k + 1], earlier):
-                    start(copy, after)
+                start(block_moves[k + 1], block_moves[k - 1] if k >= 1 else None)
             if stage is not None:
-                earlier = twin_moves[stage - 2] if stage >= 2 else [None] * len(twin_moves[stage])
-                for copy, after in zip(twin_moves[stage], earlier):
-                    start(copy, after)
+                start(twin_moves[stage], twin_moves[stage - 2] if stage >= 2 else None)
 
     def from_twins(stage):
         with jax.named_scope(f'twins{stage}'):
-            for copy in twin_moves[stage]:
-                copy.wait_recv()
-
-    for copy in block_moves[0]:
-        start(copy)
+            twin_moves[stage].wait_recv()
+
+    start(block_moves[0])
     swap_ids = start(remote(ids_v.at[c], ids_v.at[c], ps_sem.at[0], pr_sem.at[0], ring.sibling))
     moves = [[], []]
     for side, sign in sides:
         for i, (w, k) in enumerate(gather_messages(half)[side]):
             src, dst = w_v.at[w, slot[-k * sign], ring_rows], w_v.at[w, slot[-(k + 1) * sign], ring_rows]
             moves[side].append(fold.send(src, dst, gh, ws_sem.at[side, i % 2], wr_sem.at[side, i], ring.dev(sign)))
+
     def forward(i):
         with jax.named_scope(f'fwd{i}'):
             for side, sign in sides:
@@ -355,16 +343,22 @@
         total = total + over_rows(jnp.sum, same)
     row = down(n)
     place = lax.rem(row, nz)
-    chip = lax.rem(z + half + (1 - 2 * lax.rem(place, 2)) * ((place + 1) // 2), nz)
+    chip = lax.rem(z + sum(jnp.where(place == p, d, 0) for p, d in others), nz)
     owner = 2 * chip + jnp.where(row < nz, c, 1 - c)
     base = (owner * vocab).astype(F32)
     member = flags((seen < 0.5) & (ids >= base) & (ids < base + vocab))
     multi = flags(total > 1.5)
     several, single = member * multi, member * (1.0 - multi)
-    both = jnp.concatenate([several, single], axis=0).astype(BF16)
-    rank = jnp.dot(both, tri_v[...], preferred_element_type=F32)
-    n_several = over_lanes(jnp.sum, several)
-    count = n_several + over_lanes(jnp.sum, single)
+    both = jnp.concatenate([several, single], axis=0)
+    tri = one_hot(earlier_than(LANES, LANES, 0))
+    before = jnp.zeros((2 * n, 1), F32)
+    ranks = []
+    for i in range(tp // LANES):
+        some = both[:, rows_at(i)]
+        ranks.append(before + jnp.dot(some.astype(BF16), tri, preferred_element_type=F32))
+        before = before + over_lanes(jnp.sum, some)
+    rank = jnp.concatenate(ranks, axis=1)
+    n_several, count = before[:n], before[:n] + before[n:]
     rank = jnp.where(several > 0.5, rank[:n], n_several + rank[n:])
     over = over_rows(jnp.max, flags((count > CAP) | (n_several > MULTI)))
     for k in range(n):
@@ -380,22 +374,20 @@
         if k % per:
             tile = pltpu.roll(tile, LANES - (k % per) * CAP, 1)
         req_s[k] = jnp.where(lane < CAP, tile, over)
-    asks = []
-    for p, d in enumerate(order[:-1]):
-        asks.append(start(remote(req_s.at[p], req_r.at[back[p]], qs_sem.at[p], qr_sem.at[p], ring.dev(d))))
+    parts = [(req_s.at[p], req_r.at[back[p]], ring.dev(d)) for p, d in others]
+    asks = start(Batch(parts, fold.spare, qs_sem.at[0], qs_sem.at[1]))
     relay(0, 0)
     for i in range(PAIR):
         for side, _ in sides:
             start(moves[side][i])
     swap_grad = start(remote(grad_ref, gn_v.at[1, c], ps_sem.at[1], pr_sem.at[1], ring.sibling))
-    req_r[nz - 1] = req_s[nz - 1]
+    req_r[own] = req_s[own]
     for q in range(PAIR):
         for t in range(PAIR):
             pick_v[q, t] = one_hot(col_v[q * slots:(q + 1) * slots, :1] == ids[:, t * tl:(t + 1) * tl])
 
     with jax.named_scope('asks_wait'):
-        for copy in asks:
-            copy.wait_recv()
+        asks.wait_recv()
     flag = req_r[0]
     for k in range(1, nz):
         flag = jnp.maximum(flag, req_r[k])
@@ -411,7 +403,8 @@
     names = jnp.concatenate(tiles, axis=1) - (ring.me * vocab).astype(F32)
     nrow_v[...] = names
     name_v[...] = jnp.transpose(jnp.broadcast_to(names[0:1, :], (LANES, slots)))
-    gives = []
+    gives = {}
+    handed = []
 
     def find(part):
         cols = slice(part * slots // 2, (part + 1) * slots // 2)
@@ -430,15 +423,22 @@
         for q in range(nz // 2):
             fold.store(xs_v.at[part * nz // 2 + q], found[q * CAP:(q + 1) * CAP, :], xh)
 
-    def hand(p):
-        return fold.send(xr_v.at[p], xo_v.at[p], xh, xf_sem.at[p], xg_sem.at[p], ring.sibling)
-
     def give(part):
-        for p in range(part * nz // 2, (part + 1) * nz // 2):
+        at = range(part * part_of, (part + 1) * part_of)
+        parts = [area for p in at for area in fold.parts(xr_v.at[p], xo_v.at[p], xh, ring.sibling)]
+        handed.append(Batch(parts, fold.spare, xf_sem.at[part], xg_sem.at[part]))
+        sent.append(handed[part])
+        for p in at:
             if order[p]:
                 to = ring.dev(order[p])
-                give_row = fold.send(xs_v.at[p], xr_v.at[back[p]], xh, qs_sem.at[p], xr_sem.at[p], to)
-                gives.append(start(give_row, asks[p]))
+                gives[p] = start(fold.send(xs_v.at[p], xr_v.at[back[p]], xh, gs_sem.at[p], xr_sem.at[p], to))
+            else:
+                xr_v[p] = xs_v[p]
+                hand(p)
+
+    def hand(p):
+        for copy in handed[p // part_of].copies[2 * (p % part_of):2 * (p % part_of) + 2]:
+            copy.start()
 
     relay(1, 1)
     find(0)
@@ -448,33 +448,45 @@
     find(1)
     forward(1)
     give(1)
-    xr_v[nz - 1] = xs_v[nz - 1]
-    handed = {nz - 1: start(hand(nz - 1))}
+    row_v[...] = jnp.zeros_like(row_v)
+    load_gain.wait()
+    row_v[:, :dm] = line_v[...].astype(F32).reshape(1, dm)
+    gain_v[...] = jnp.transpose(jnp.broadcast_to(row_v[...], (LANES, fold.dp)))
     relay(3, 2)
     forward(2)
 
-    with jax.named_scope('gives_wait'):
-        for p in range(nz - 1):
-            gives[p].wait_recv()
-            handed[back[p]] = start(hand(back[p]))
+    def arrived(part):
+        with jax.named_scope(f'gives_wait{part}'):
+            for p in range(part * part_of, (part + 1) * part_of):
+                if order[p]:
+                    gives[p].wait_recv()
+                    hand(back[p])
+
+    def unpack(rows_of, q, part):
+        at = slice(part * part_of, (part + 1) * part_of)
+        for p in range(part * part_of, (part + 1) * part_of):
+            fold.unfold(rows_of.at[p], xh)
+        rows = rows_of[at].reshape(part_of * CAP, fold.dp)[:, :dm]
+        picks = slice(part * part_of * CAP, (part + 1) * part_of * CAP)
+        for t in range(PAIR):
+            value = first_first(rows, pick_v[q, t, picks]).astype(BF16)
+            x_v[t] = x_v[t] + value if q or part else value
+
+    def from_sibling(part):
+        with jax.named_scope(f'sibling_wait{part}'):
+            handed[part].wait_recv()
+        unpack(xo_v, 1, part)
+
+    arrived(0)
+    unpack(xr_v, 0, 0)
+    from_sibling(0)
+    arrived(1)
     forward(3)
-
-    def unpack(rows_of, q):
-        for p in range(nz):
-            fold.unfold(rows_of.at[p], xh)
-        rows = rows_of[...].reshape(slots, fold.dp)[:, :dm]
-        return [first_first(rows, pick_v[q, t]).astype(BF16) for t in range(PAIR)]
-
-    for t, part in enumerate(unpack(xr_v, 0)):
-        x_v[t] = part
+    unpack(xr_v, 0, 1)
     forward(4)
     load_grad.wait()
     swap_grad.wait_recv()
-    with jax.named_scope('sibling_wait'):
-        for copy in handed.values():
-            copy.wait_recv()
-    for t, part in enumerate(unpack(xo_v, 1)):
-        x_v[t] = x_v[t] + part
+    from_sibling(1)
 
     def lanes(b):
         return pl.ds(pl.multiple_of(b * LANES, LANES), LANES)
@@ -565,6 +577,7 @@
     swap_dn = remote(snd_v.at[body_rows], dnr_v, ps_sem.at[2], pr_sem.at[2], ring.sibling)
     swap_dn.start()
     through(0, c, own_v)
+    scatter(2)
     with jax.named_scope('swapdn_wait'):
         swap_dn.wait_send()
         swap_dn.wait_recv()
@@ -595,13 +608,11 @@
 
     lax.fori_loop(0, nz, pack, 0)
     backs = []
-    for p, d in enumerate(order[:-1]):
-        to, q = ring.dev(d), back[p]
-        backs.append(start(fold.send(es_v.at[p], er_v.at[q], eh, qs_sem.at[p], er_sem.at[0, p], to), gives[p]))
-        backs.append(start(fold.send(eb_v.at[p], eq_v.at[q], bh, xf_sem.at[p], er_sem.at[1, p], to), handed[p]))
-    er_v[nz - 1] = es_v[nz - 1]
-    eq_v[nz - 1] = eb_v[nz - 1]
-    scatter(2)
+    for kind, (src, dst, h) in enumerate(((es_v, er_v, eh), (eb_v, eq_v, bh))):
+        parts = [area for p, d in others for area in fold.parts(src.at[p], dst.at[back[p]], h, ring.dev(d))]
+        backs.append(start(Batch(parts, fold.spare, es_sem.at[kind], er_sem.at[kind])))
+    er_v[own] = es_v[own]
+    eq_v[own] = eb_v[own]
     through(1, c, own_v)
     scatter(3)
     with jax.named_scope('swapy_wait'):
@@ -695,8 +706,7 @@
     parts = slots + 2 * nz * MULTI
     assert max(parts, dp) <= tp
     hops = nz - 1
-    each, _, _ = shared_blocks(fl, groups)
-    vmem, hbm = pl.BlockSpec(memory_space=pltpu.VMEM), pl.BlockSpec(memory_space=pl.ANY)
+    hbm = pl.BlockSpec(memory_space=pl.ANY)
     dma = pltpu.SemaphoreType.DMA
     tokens = pltpu.VMEM((PAIR, dm, tl), BF16)
     return pl.pallas_call(
@@ -752,11 +762,11 @@
             pltpu.VMEM((1, LANES), jnp.int32),
             pltpu.VMEM((PAIR, fl, dm), F32),
             pltpu.VMEM((nz, CAP, dp), BF16),
-            dma((nz,)), dma((nz,)),
+            dma((PAIR,)), dma((PAIR,)),
             dma((5,)), dma((vocab // 512,)), dma((PAIR, PAIR)), dma((PAIR, hops)),
-            dma((PAIR, each, 2)), dma((PAIR, each, nz // 2)), dma((PAIR, each, groups - 1)), dma((3, each, groups - 1)),
-            dma((5,)), dma((5,)), dma((hops,)), dma((hops,)), dma((hops,)),
-            dma((PAIR, PAIR)), dma((PAIR, hops)), dma((PAIR, hops)), dma((9,)),
+            dma((PAIR,)), dma((nz // 2,)), dma((PAIR,)), dma((3,)),
+            dma((5,)), dma((5,)), dma((PAIR,)), dma((nz,)), dma((nz,)),
+            dma((PAIR, PAIR)), dma((PAIR, hops)), dma((PAIR,)), dma((PAIR,)), dma((9,)),
         ],
         compiler_params=pltpu.CompilerParams(
             collective_id=0, has_side_effects=True, vmem_limit_bytes=VMEM_LIMIT
@@ -773,12 +783,15 @@
         copy.start()
         return copy
 
-    needed = [load(0, names_hbm, names_v), load(1, rows_hbm, rows_v)]
+    parts = names_hbm.shape[0]
+    real = pl.ds(0, parts)
+    needed = [load(0, names_hbm, names_v.at[real]), load(1, rows_hbm, rows_v.at[real])]
     passing = ((out_ref, out_v, out_out), (up_ref, up_v, up_out), (down_ref, down_v, down_out))
     loads = [load(2 + j, src, via) for j, (src, via, _) in enumerate(passing)]
     dm, vocab = emb_v.shape
     block = vocab // PLACE_GRID
-    last = rows_v.shape[0] // PLACE_ROWS - 1
+    names_v[parts:] = jnp.full((PLACE_ROWS, LANES), -1.0)
+    rows_v[parts:] = jnp.zeros((PLACE_ROWS, rows_v.shape[1]), BF16)
     for copy in needed:
         copy.wait()
 
@@ -788,20 +801,19 @@
 
     def fill(i, carry):
         to = pl.ds(pl.multiple_of(i * block, LANES), block)
-        lo = jnp.minimum(bounds_ref[0, i] // PLACE_ROWS, last)
-        hi = (bounds_ref[0, i + 1] + PLACE_ROWS - 1) // PLACE_ROWS
+        lo = bounds_ref[0, i] // BLOCK * BLOCK
 
         def part(q):
-            at = pl.ds(pl.multiple_of(q * PLACE_ROWS, PLACE_ROWS), PLACE_ROWS)
+            at = pl.ds(pl.multiple_of(lo + q * PLACE_ROWS, BLOCK), PLACE_ROWS)
             return first_first(rows_v[at, :dm], one_hot(names_v[at, :1] == across(block, i * block).astype(F32)))
 
-        emb_v[:, to] = part(lo)
+        emb_v[:, to] = part(0)
 
         def more(q, inner):
             emb_v[:, to] = emb_v[:, to] + part(q)
             return inner
 
-        lax.fori_loop(lo + 1, hi, more, 0)
+        lax.fori_loop(1, (bounds_ref[0, i + 1] - lo + PLACE_ROWS - 1) // PLACE_ROWS, more, 0)
         store(i).start()
         return carry
 
@@ -828,7 +840,8 @@
         out_shape=results,
         in_specs=[pl.BlockSpec(memory_space=pltpu.SMEM)] + [hbm] * 5,
         out_specs=(hbm,) * 4,
-        scratch_shapes=[pltpu.VMEM(a.shape, a.dtype) for a in (names, rows) + results]
+        scratch_shapes=[pltpu.VMEM((a.shape[0] + PLACE_ROWS, a.shape[1]), a.dtype) for a in (names, rows)]
+        + [pltpu.VMEM(a.shape, a.dtype) for a in results]
         + [dma((5,)), dma((PLACE_GRID,)), dma((3,))],
         compiler_params=pltpu.CompilerParams(vmem_limit_bytes=VMEM_LIMIT),
     )(bounds, names, rows, out, d_up, d_down)

time: 193 us -> 190 us (0.984); the launches traced: 193 us -> 187 us
  Pallas kernels: 191 us -> 185 us
    pallas_call x1, Pallas kernels: 183 us -> 177 us  [step(): pl.pallas_call(functools.partial(step_kernel, n, groups), name='step', ou...]
where the time goes in v6:
time: 190 us; the launch traced here: 187 us
  Pallas kernels  185 us (97%)
    pallas_call x1, Pallas kernels, step(): pl.pallas_call(functools.partial(step_kernel, n, groups), name='step', ou...  177 us
    pallas_call x1, Pallas kernels, place(): pl.pallas_call(place_kernel, name='place', out_shape=results, in_specs=[p...  7.86 us

profile of v6, /device:TPU:21, one launch (start us, length us, event | category | flops | bytes accessed | tf_op | source)
XLA Modules:
  0.0 186.6 jit_solution(15786969487642992521)
XLA Ops:
  0.6 0.0 copy-start.4
  0.6 0.0 copy-start.6
  0.7 176.9 %step.1 = (bf16[960,512]{1,0:T(8,128)(2,1)}, f32[160,960]{1,0:T(8,128)}, f32[160,960]{1,0:T(8,128)}, bf16[768,1024]{1,0:T(8,128)(2,1)}, f32[768,128]{1,0:T(8,128)}, /*index=5*/s32[1,128]{1,0:T(1,128)}, f32[1,1]{1,0:T(1,128)}) custom-call(s32[1,512]{1,0:T(1,128)} %bitcast.63, bf16[960,3072]{1,0:T(8,128)(2,1)} %bitcast.59, bf16[160,960]{1,0:T(8,128)(2,1)} %bitcast.55, ...), custom_call_target="tpu_custom_call" | custom-call | tf_op jit(solution)/shard_map/step/pallas_call | solution.py:712
  177.6 7.9 %place.1 = (f32[960,3072]{1,0:T(8,128)}, bf16[960,512]{1,0:T(8,128)(2,1)}, f32[160,960]{1,0:T(8,128)}, f32[160,960]{1,0:T(8,128)}) custom-call(s32[1,128]{1,0:T(1,128)} %get-tuple-element.71.bounds_ref, f32[768,128]{1,0:T(8,128)} %get-tuple-element.72.names_hbm, bf16[768,1024]{1,0:T(8,128)(2,1)} %get-tuple-element.73.rows_hbm, ...), custom_call_target="tpu_custom_call" | custom-call | tf_op jit(solution)/shard_map/place/pallas_call | solution.py:837
  185.4 0.0 copy-done.4
  185.4 0.0 copy-done.6
  185.5 0.9 while.15
Async XLA Ops:
  0.6 184.8 %copy-start.4 = (bf16[960]{0:T(1024)(128)(2,1)S(1)}, bf16[960]{0:T(1024)(128)(2,1)}, u32[]{:S(2)}) copy-start(bf16[960]{0:T(1024)(128)(2,1)} %gain_ref.1) | copy-start | bytes 5764
  0.6 184.8 %copy-start.6 = (s32[512]{0:T(512)S(1)}, s32[512]{0:T(512)}, u32[]{:S(2)}) copy-start(s32[512]{0:T(512)} %param.8) | copy-start | bytes 6148

commit v7 on v6

--- a/solution.py
+++ b/solution.py
@@ -678,14 +678,15 @@
         keeps[-1].start()
 
     for w in range(PAIR):
+        dw_v[w] = grad_w(w, mine)
+    for w in range(PAIR):
         a, b = (last - 1, last - 2) if w == 0 else (last - 2, last - 1)
-        part = grad_w(w, mine)
         with jax.named_scope(f'fin{w}'):
             sends[0][a].wait_recv()
             sends[1][b].wait_recv()
         rb_v[0, a] = rb_v[0, a] + rb_v[1, b]
         fold.unfold(rb_v.at[0, a], wh)
-        dw_v[w] = rb_v[0, a, :, :dm] + part
+        dw_v[w] = rb_v[0, a, :, :dm] + dw_v[w]
         keeps.append(pltpu.make_async_copy(dw_v.at[w], (dup_ref, ddown_ref)[w], out_sem.at[6 + w]))
         keeps[-1].start()
     with jax.named_scope('exit_sends'):

time: 190 us -> 189 us (level)
  no operation moved by 1% of the time
where the time goes in v7:
time: 189 us; the launch traced here: 186 us
  Pallas kernels  184 us (97%)
    pallas_call x1, Pallas kernels, step(): pl.pallas_call(functools.partial(step_kernel, n, groups), name='step', ou...  177 us
    pallas_call x1, Pallas kernels, place(): pl.pallas_call(place_kernel, name='place', out_shape=results, in_specs=[p...  7.86 us

profile of v7, /device:TPU:21, one launch (start us, length us, event | category | flops | bytes accessed | tf_op | source)
XLA Modules:
  0.0 186.3 jit_solution(9564232672096621665)
XLA Ops:
  0.6 0.0 copy-start.4
  0.6 0.0 copy-start.6
  0.7 176.6 %step.1 = (bf16[960,512]{1,0:T(8,128)(2,1)}, f32[160,960]{1,0:T(8,128)}, f32[160,960]{1,0:T(8,128)}, bf16[768,1024]{1,0:T(8,128)(2,1)}, f32[768,128]{1,0:T(8,128)}, /*index=5*/s32[1,128]{1,0:T(1,128)}, f32[1,1]{1,0:T(1,128)}) custom-call(s32[1,512]{1,0:T(1,128)} %bitcast.63, bf16[960,3072]{1,0:T(8,128)(2,1)} %bitcast.59, bf16[160,960]{1,0:T(8,128)(2,1)} %bitcast.55, ...), custom_call_target="tpu_custom_call" | custom-call | tf_op jit(solution)/shard_map/step/pallas_call | solution.py:713
  177.3 7.9 %place.1 = (f32[960,3072]{1,0:T(8,128)}, bf16[960,512]{1,0:T(8,128)(2,1)}, f32[160,960]{1,0:T(8,128)}, f32[160,960]{1,0:T(8,128)}) custom-call(s32[1,128]{1,0:T(1,128)} %get-tuple-element.71.bounds_ref, f32[768,128]{1,0:T(8,128)} %get-tuple-element.72.names_hbm, bf16[768,1024]{1,0:T(8,128)(2,1)} %get-tuple-element.73.rows_hbm, ...), custom_call_target="tpu_custom_call" | custom-call | tf_op jit(solution)/shard_map/place/pallas_call | solution.py:838
  185.2 0.0 copy-done.4
  185.2 0.0 copy-done.6
  185.2 0.9 while.15
Async XLA Ops:
  0.6 184.5 %copy-start.4 = (bf16[960]{0:T(1024)(128)(2,1)S(1)}, bf16[960]{0:T(1024)(128)(2,1)}, u32[]{:S(2)}) copy-start(bf16[960]{0:T(1024)(128)(2,1)} %gain_ref.1) | copy-start | bytes 5764
  0.6 184.5 %copy-start.6 = (s32[512]{0:T(512)S(1)}, s32[512]{0:T(512)}, u32[]{:S(2)}) copy-start(s32[512]{0:T(512)} %param.8) | copy-start | bytes 6148
